TPU v7x, 32 devices: a whole 2x2x4 slice. The times are simulated.
32 devices in a mesh: groups: 2 (over y), expert: 8 (over z, core), tensor: 2 (over x).
Axes of the slice: x: 2, y: 2, z: 4, core: 2. Of those that a mesh axis runs over, the one named last changes fastest.
Arguments:
- hidden_in: bfloat16 [128, 2880], P(('groups', 'expert')), parts along dimension 0, may hold values from -6 to 6
- queries: bfloat16 [128, 32, 64], P(('groups', 'expert'), 'tensor'), parts along dimension 0, may hold values from -8 to 8
- new_keys: bfloat16 [128, 8, 64], P(('groups', 'expert'), 'tensor'), parts along dimension 0, may hold values from -4 to 4
- new_values: bfloat16 [128, 8, 64], P(('groups', 'expert'), 'tensor'), parts along dimension 0, may hold values from -4 to 4
- cache_keys: bfloat16 [128, 8, 64, 256], P(('groups', 'expert'), 'tensor'), parts along dimension 0, may hold values from -8 to 8
- cache_values: bfloat16 [128, 8, 64, 256], P(('groups', 'expert'), 'tensor'), parts along dimension 0, may hold values from -4 to 4
- cache_lengths: int32 [128], P(('groups', 'expert')), parts along dimension 0, may hold values from 2 to 256, as said below
- out_weight: bfloat16 [2048, 2880], P('tensor'), may hold values from -0.125 to 0.125
- norm_gain: float32 [2880], replicated, may hold values from 0.1 to 1.9
- expert_ids: int32 [128, 4], P(('groups', 'expert')), parts along dimension 0, may hold values from 0 to 7, all different within a row; in each aligned block of 8 rows (0 to 7, 8 to 15, ...) at most 4 rows name the same one
- route_probs: float32 [128, 4], P(('groups', 'expert')), parts along dimension 0, may hold values from 0.05 to 1
- route_order: int32 [128, 4], P(('groups', 'expert')), parts along dimension 0, may hold values from 0 to 3, each once within a row
- gate_weight: bfloat16 [8, 2880, 1440], P('expert', None, 'tensor'), may hold values from -0.109375 to 0.109375
- up_weight: bfloat16 [8, 2880, 1440], P('expert', None, 'tensor'), may hold values from -0.109375 to 0.109375
- down_weight: bfloat16 [8, 1440, 2880], P('expert', 'tensor'), may hold values from -0.15625 to 0.15625
Outputs:
- layer_out: bfloat16 [128, 2880], P(('groups', 'expert'), 'tensor'), parts along dimension 0
There are 2 independent parts, one for each index of `groups`. A program takes and returns all parts, laid end to end along the dimension named above; an argument that names none is the same for every part. Nothing has to cross between parts.
Inputs may be any that keep to these rules, and one draw needn't show every extreme that they name: `cache_lengths`: some sequence fills all 256 slots. `expert_ids`: each row names 4 different experts; among the 8 rows of one device no expert is named by more than 4 rows, a bound that some block reaches. `route_order`: each row is a permutation of 0 to 3.
All inputs are finite; a program needn't handle non-finite values.
Results may differ from a plain program's by a relative error of at most 0.007.
Values may be sent and summed in bfloat16 or wider, within the bound.
No kernel may reach another device: no remote copies, remote signals or barrier semaphores. Data moves between devices by JAX's collectives and lax.ppermute only.
A program may use at most 64 MiB of HBM per device.

v0:
```python
import jax
import jax.numpy as jnp
from jax import lax
from jax.sharding import PartitionSpec as P

EPSILON = 1e-05
GLU_SLOPE = 1.702


def attend(queries, new_keys, new_values, cache_keys, cache_values, cache_lengths):
    sequence_count, head_count, head_dim = queries.shape
    kv_heads = new_keys.shape[1]
    group_size = head_count // kv_heads
    scaling = 1.0 / head_dim**0.5
    query_rows = queries.reshape(sequence_count, kv_heads, group_size, head_dim)
    scores = (
        jnp.einsum("sgqd,sgdc->sgqc", query_rows, cache_keys, preferred_element_type=jnp.float32)
        * scaling
    )
    own_score = (
        jnp.einsum("sgqd,sgd->sgq", query_rows, new_keys, preferred_element_type=jnp.float32)
        * scaling
    )
    positions = jnp.arange(cache_keys.shape[3], dtype=jnp.int32)
    visible = positions[None, :] < cache_lengths[:, None]
    scores = jnp.where(visible[:, None, None, :], scores, -1e30)
    highest = jnp.maximum(jnp.max(scores, axis=3), own_score)
    cache_exp = jnp.exp(scores - highest[..., None])
    own_exp = jnp.exp(own_score - highest)
    totals = jnp.sum(cache_exp, axis=3) + own_exp
    cache_prob = (cache_exp / totals[..., None]).astype(jnp.bfloat16)
    own_prob = (own_exp / totals).astype(jnp.bfloat16)
    attended = jnp.einsum(
        "sgqc,sgdc->sgqd", cache_prob, cache_values, preferred_element_type=jnp.float32
    )
    attended = (
        attended
        + own_prob.astype(jnp.float32)[..., None] * new_values.astype(jnp.float32)[:, :, None, :]
    )
    return attended.astype(jnp.bfloat16).reshape(sequence_count, head_count * head_dim)


def apply_norm(residual, norm_gain):
    mean_square = jnp.mean(residual * residual, axis=1, keepdims=True)
    return (residual * lax.rsqrt(mean_square + EPSILON) * norm_gain).astype(jnp.bfloat16)


def route_tables(expert_ids, route_probs, route_order, experts, capacity):
    tokens, top_count = expert_ids.shape
    flat_ids = expert_ids.reshape(tokens * top_count)
    expert_mark = (flat_ids[:, None] == jnp.arange(experts, dtype=jnp.int32)[None, :]).astype(
        jnp.int32
    )
    earlier = jnp.cumsum(expert_mark, axis=0) - expert_mark
    position = jnp.sum(earlier * expert_mark, axis=1)
    slot_code = flat_ids * capacity + position
    slot_table = slot_code[:, None] == jnp.arange(experts * capacity, dtype=jnp.int32)[None, :]
    slot_table = slot_table.astype(jnp.float32).reshape(tokens, top_count, experts * capacity)
    picked = jnp.zeros((tokens, top_count), jnp.float32)
    for column in range(top_count):
        picked = picked + jnp.where(route_order == column, route_probs[:, column : column + 1], 0.0)
    weights = picked / jnp.sum(route_probs, axis=1, keepdims=True)
    select_experts = jnp.sum(slot_table, axis=1)
    weighted_output = jnp.sum(slot_table * weights[:, :, None], axis=1)
    return (select_experts, weighted_output)


def per_device(
    hidden_in,
    queries,
    new_keys,
    new_values,
    cache_keys,
    cache_values,
    cache_lengths,
    out_weight,
    norm_gain,
    expert_ids,
    route_probs,
    route_order,
    gate_weight,
    up_weight,
    down_weight,
):
    sequence_count, model_width = hidden_in.shape
    expert_ranks = lax.axis_size("expert")
    tensor_ranks = lax.axis_size("tensor")
    local_experts = gate_weight.shape[0]
    experts = local_experts * expert_ranks
    top_count = expert_ids.shape[1]
    capacity = min(sequence_count, max(2, (sequence_count * top_count + experts - 1) // experts))
    slab_width = model_width // tensor_ranks
    offset = lax.axis_index("tensor") * slab_width
    attended = attend(queries, new_keys, new_values, cache_keys, cache_values, cache_lengths)
    partial_sums = jnp.dot(attended, out_weight, preferred_element_type=jnp.float32)
    attention = lax.psum(partial_sums, "tensor")
    residual = hidden_in.astype(jnp.float32) + attention
    normed = apply_norm(residual, norm_gain)
    select_experts, weighted_output = route_tables(
        expert_ids, route_probs, route_order, experts, capacity
    )
    outgoing = jnp.dot(
        select_experts.T.astype(jnp.bfloat16), normed, preferred_element_type=jnp.float32
    ).astype(jnp.bfloat16)
    outgoing = outgoing.reshape(expert_ranks, local_experts * capacity, model_width)
    arrived = lax.all_to_all(outgoing, "expert", split_axis=0, concat_axis=0, tiled=True)
    arrived = arrived.reshape(expert_ranks, local_experts, capacity, model_width)
    gate_sums = jnp.einsum(
        "secd,edf->secf", arrived, gate_weight, preferred_element_type=jnp.float32
    )
    upward = jnp.einsum("secd,edf->secf", arrived, up_weight, preferred_element_type=jnp.float32)
    active = (gate_sums * jax.nn.sigmoid(GLU_SLOPE * gate_sums) * (upward + 1.0)).astype(
        jnp.bfloat16
    )
    expert_part = jnp.einsum(
        "secf,efd->secd", active, down_weight, preferred_element_type=jnp.float32
    )
    expert_part = expert_part.reshape(expert_ranks, local_experts * capacity, model_width)
    kept = lax.dynamic_slice_in_dim(residual, offset, slab_width, 1)
    returned = lax.all_to_all(expert_part, "expert", split_axis=0, concat_axis=0, tiled=True)
    returned = returned.reshape(experts * capacity, model_width)
    blended = jnp.dot(weighted_output, returned, precision=lax.Precision.HIGHEST)
    expert_mixture = lax.psum_scatter(
        blended.astype(jnp.bfloat16), "tensor", scatter_dimension=1, tiled=True
    ).astype(jnp.float32)
    return (kept + expert_mixture).astype(jnp.bfloat16)


def solution(mesh):
    in_specs = (
        P(("groups", "expert"), None),
        P(("groups", "expert"), "tensor", None),
        P(("groups", "expert"), "tensor", None),
        P(("groups", "expert"), "tensor", None),
        P(("groups", "expert"), "tensor", None, None),
        P(("groups", "expert"), "tensor", None, None),
        P(("groups", "expert")),
        P("tensor", None),
        P(),
        P(("groups", "expert"), None),
        P(("groups", "expert"), None),
        P(("groups", "expert"), None),
        P("expert", None, "tensor"),
        P("expert", None, "tensor"),
        P("expert", "tensor", None),
    )
    out_specs = P(("groups", "expert"), "tensor")
    return jax.shard_map(
        per_device, mesh=mesh, in_specs=in_specs, out_specs=out_specs, check_vma=False
    )
```

profile of v0, /device:TPU:0, one launch (start us, length us, event | category | flops | bytes accessed | tf_op | source)
XLA Modules:
  0.0 103.0 jit_solution(494024333283374364)
XLA Ops:
  6.5 0.0 copy-start
  6.5 0.0 all-reduce.2.cloned.1.call-start
  6.5 0.8 iota_compare_fusion.2
  7.4 0.9 fusion.35
  8.3 0.0 copy-done
  8.3 1.1 %fusion.40 = (f32[8,4,4]{2,1,0:T(4,128)S(1)}, f32[8,4,4,256]{3,2,1,0:T(4,128)S(1)}) fusion(bf16[8,4,4,64]{3,2,1,0:T(4,128)(2,1)} %bitcast.74, bf16[8,4,64,256]{3,2,1,0:T(8,128)(2,1)S(1)} %copy-done, pred[8,256]{1,0:T(8,128)(4,1)S(1)} %iota_compare_fusion.2), kind=kOutput, calls=%fused_computation.54 | convolution fusion | flops 4292480 | bytes 1198592 | tf_op jit(solution)/shard_map/sgqd,sgdc->sgqc/dot_general | solution.py:17
  9.4 0.0 copy-start.3
  9.4 0.0 copy-start.4
  9.4 0.2 fusion.28
  9.6 0.0 copy-start.5
  9.6 0.0 copy-start.1
  9.7 0.7 convert_element_type.51
  10.4 0.0 copy-start.2
  10.4 1.7 %fusion.22 = bf16[8,4,4,64]{3,2,1,0:T(4,128)(2,1)S(1)} fusion(bf16[8,4,64,256]{3,2,1,0:T(8,128)(2,1)} %param.20, f32[8,4,4,256]{3,2,1,0:T(4,128)S(1)} %get-tuple-element.16, f32[8,4,4]{2,1,0:T(4,128)S(1)} %get-tuple-element.10, f32[8,4,4]{2,1,0:T(4,128)S(1)} %multiply_maximum_fusion, f32[8,4,64]{2,1,0:T(4,128)S(1)} %convert_element_type.51, ...), kind=kOutput, calls=%fused_computation.16 | convolution fusion | flops 4317184 | bytes 1205760 | tf_op jit(solution)/shard_map/sgqc,sgdc->sgqd/dot_general | solution.py:33
  12.1 0.1 reshape.87
  12.2 5.0 %fusion.41 = f32[8,2880]{1,0:T(8,128)} fusion(bf16[8,1024]{1,0:T(8,128)(2,1)S(1)} %reshape.87, bf16[1024,2880]{0,1:T(8,128)(2,1)} %param.22), kind=kOutput, calls=%fused_computation.55 | convolution fusion | flops 47185920 | bytes 6006784 | tf_op jit(solution)/shard_map/dot_general | solution.py:95
  17.2 0.0 all-reduce.2.cloned.1.call-update
  17.2 0.0 reduce-scatter.4.cloned.1.call-start
  17.2 0.0 copy-done.3
  17.3 0.0 copy-done.4
  17.3 0.1 copy.31
  17.4 0.1 eq.53
  17.4 0.1 fusion.34
  17.5 0.1 reduce_window_sum.11
  17.6 0.2 select_reduce_fusion.1
  17.8 0.1 reduce_sum.58
  17.8 0.1 copy.33
  17.9 0.0 copy-done.5
  18.0 0.1 convert_reduce_fusion
  18.0 23.1 %all-reduce.2.cloned.1.call-done = f32[8,2880]{1,0:T(8,128)} async-done(((f32[8,2880]{1,0:T(8,128)}), f32[8,2880]{1,0:T(8,128)}) %all-reduce.2.cloned.1.call-update) | async-done | bytes 92176 | tf_op jit(solution)/shard_map/psum | solution.py:96
  41.2 0.0 copy-done.1
  41.2 1.0 %multiply_reduce_fusion = (f32[8]{0:T(128)S(1)}, f32[8,2880]{1,0:T(8,128)S(1)}) fusion(f32[8,2880]{1,0:T(8,128)} %all-reduce.2.cloned.1.call-done, bf16[8,2880]{1,0:T(8,128)(2,1)S(1)} %copy-done.1), kind=kLoop, calls=%fused_computation.24 | loop fusion | flops 92152 | bytes 230432 | tf_op jit(solution)/shard_map/reduce_sum | solution.py:44
  42.2 0.0 copy-done.2
  42.2 0.3 convolution_convert_fusion
  42.5 0.1 reshape.88
  42.6 12.5 %all_to_all.10 = bf16[8,4,2880]{2,1,0:T(4,128)(2,1)S(1)} all-to-all(bf16[8,4,2880]{2,1,0:T(4,128)(2,1)S(1)} %reshape.88), channel_id=1, replica_groups=mesh['groups'=2,'expert'=8,'tensor'=2] {'expert'}, dimensions={0} | all-to-all | bytes 368640 | tf_op jit(solution)/shard_map/all_to_all | solution.py:106
  55.1 0.0 slice-start
  55.1 3.6 %fusion.7 = f32[8,1,4,720]{3,0,2,1:T(8,128)S(1)} fusion(bf16[1,2880,720]{1,2,0:T(8,128)(2,1)} %param.27, bf16[8,4,2880]{2,1,0:T(4,128)(2,1)S(1)} %all_to_all.10), kind=kOutput, calls=%fused_computation.10 | convolution fusion | flops 132710400 | bytes 4423680 | tf_op jit(solution)/shard_map/secd,edf->secf/dot_general | solution.py:108
  58.8 0.0 slice-start.1
  58.8 3.5 %fusion.23 = bf16[8,4,720]{2,0,1:T(8,128)(2,1)S(1)} fusion(bf16[1,2880,720]{1,2,0:T(8,128)(2,1)} %param.28, bf16[8,4,2880]{2,1,0:T(4,128)(2,1)S(1)} %all_to_all.10, f32[8,1,4,720]{3,0,2,1:T(8,128)S(1)} %fusion.7), kind=kOutput, calls=%fused_computation.17 | convolution fusion | flops 132894720 | bytes 4469760 | tf_op jit(solution)/shard_map/secd,edf->secf/dot_general | solution.py:111
  62.3 0.0 slice-done
  62.3 0.0 slice-done.1
  62.3 0.8 fusion
  63.1 14.5 %all_to_all.11 = f32[8,4,2880]{2,1,0:T(4,128)S(1)} all-to-all(f32[8,4,2880]{2,1,0:T(4,128)S(1)} %fusion), channel_id=1, replica_groups=mesh['groups'=2,'expert'=8,'tensor'=2] {'expert'}, dimensions={0} | all-to-all | bytes 737280 | tf_op jit(solution)/shard_map/all_to_all | solution.py:120
  77.7 0.1 reshape.93
  77.8 0.3 convolution_convert_fusion.1
  78.1 1.2 %copy.41 = bf16[8,2880]{0,1:T(8,128)(2,1)} copy(bf16[8,2880]{1,0:T(8,128)(2,1)S(1)} %convolution_convert_fusion.1) | data formatting | bytes 92160
  79.2 0.0 reduce-scatter.4.cloned.1.call-update
  79.3 15.1 %reduce-scatter.4.cloned.1.call-done = bf16[1440,8]{1,0:T(8,128)(2,1)} async-done(((bf16[2880,8]{1,0:T(8,128)(2,1)}), bf16[1440,8]{1,0:T(8,128)(2,1)}) %reduce-scatter.4.cloned.1.call-update) | async-done | bytes 23056
  94.4 1.1 %copy.42 = bf16[8,1440]{1,0:T(8,128)(2,1)S(1)} copy(bf16[8,1440]{0,1:T(8,128)(2,1)} %bitcast.70) | data formatting | bytes 46080
  95.5 0.7 add_convert_fusion
  (8 shorter events, 0.1 us)
Async XLA Ops:
  6.5 1.7 %copy-start = (bf16[8,4,64,256]{3,2,1,0:T(8,128)(2,1)S(1)}, bf16[8,4,64,256]{3,2,1,0:T(8,128)(2,1)}, u32[]{:S(2)}) copy-start(bf16[8,4,64,256]{3,2,1,0:T(8,128)(2,1)} %param.19) | copy-start | bytes 3145732
  6.5 34.6 %all-reduce.2.cloned.1.call-start = ((), (), s32[]{:S(2)}) async-start(), calls=%async_computation.3 | async-start | bytes 188416 | tf_op jit(solution)/shard_map/psum | solution.py:96
  9.4 7.8 %copy-start.3 = (f32[8,4]{0,1:T(4,128)S(1)}, f32[8,4]{0,1:T(4,128)}, u32[]{:S(2)}) copy-start(f32[8,4]{0,1:T(4,128)} %param.25) | copy-start | bytes 388
  9.4 7.9 %copy-start.4 = (s32[8,4]{0,1:T(4,128)S(1)}, s32[8,4]{0,1:T(4,128)}, u32[]{:S(2)}) copy-start(s32[8,4]{0,1:T(4,128)} %param.24) | copy-start | bytes 388
  9.6 8.3 %copy-start.5 = (s32[8,4]{0,1:T(4,128)S(1)}, s32[8,4]{0,1:T(4,128)}, u32[]{:S(2)}) copy-start(s32[8,4]{0,1:T(4,128)} %param.26) | copy-start | bytes 388
  9.6 31.5 %copy-start.1 = (bf16[8,2880]{1,0:T(8,128)(2,1)S(1)}, bf16[8,2880]{1,0:T(8,128)(2,1)}, u32[]{:S(2)}) copy-start(bf16[8,2880]{1,0:T(8,128)(2,1)} %param.15) | copy-start | bytes 138244
  10.4 31.8 %copy-start.2 = (f32[2880]{0:T(1024)S(1)}, f32[2880]{0:T(1024)}, u32[]{:S(2)}) copy-start(f32[2880]{0:T(1024)} %param.23) | copy-start | bytes 34564
  17.2 77.2 %reduce-scatter.4.cloned.1.call-start = ((), (), s32[]{:S(2)}) async-start(), calls=%async_computation.4 | async-start | bytes 1105920
  55.1 7.2 %slice-start = ((s8[4239360]{0:T(1024)(128)(4,1)}), s8[4194304]{0:T(1024)(128)(4,1)S(1)}, s32[]{:S(2)}) async-start(s8[4239360]{0:T(1024)(128)(4,1)} %bitcast.67), calls=%async_computation.5 | async-start | bytes 8388608
  58.8 3.5 %slice-start.1 = ((s8[4239360]{0:T(1024)(128)(4,1)}), s8[45056]{0:T(1024)(128)(4,1)S(1)}, s32[]{:S(2)}) async-start(s8[4239360]{0:T(1024)(128)(4,1)} %bitcast.67), calls=%async_computation.6 | async-start | bytes 90112
Sparse Core Ops, SparseCore 0:
  17.3 23.8 all-reduce.1
  79.4 14.9 reduce-scatter.3
where the time goes:
time: 104 us; the launch traced here: 103 us
  waiting for transfers between devices  38.3 us (37%)
  blocking collectives  27.1 us (26%)
  matrix products  17.2 us (17%)
  between operations  13.6 us (13%)
  other arithmetic  3.95 us (4%)
  local copies, waits for them, and re-layouts  2.93 us (3%)
    psum x1, waiting for transfers between devices, per_device(): attention = lax.psum(partial_sums, 'tensor')  23.1 us
    unnamed x3, waiting for transfers between devices  15.1 us
    all_to_all x1, blocking collectives, per_device(): lax.all_to_all(expert_part, 'expert', split_axis=0, concat_axis=0, tiled=...  14.5 us
    all_to_all x1, blocking collectives, per_device(): lax.all_to_all(outgoing, 'expert', split_axis=0, concat_axis=0, tiled=True)  12.5 us
    dot_general x1, matrix products, per_device(): jnp.dot(attended, out_weight, preferred_element_type=jnp.float32)  4.97 us
    dot_general x1, matrix products, per_device(): jnp.einsum('secd,edf->secf', arrived, gate_weight, preferred_element_type...  3.63 us
    dot_general x1, matrix products, per_device(): jnp.einsum('secd,edf->secf', arrived, up_weight, preferred_element_type=j...  3.5 us
    unnamed x19, local copies, waits for them, and re-layouts  2.39 us
  transfers between devices with their start and end apart: 2, of which 2 were waited for; matrix products, arithmetic and copies ran while one was open for 1% of the time, Pallas kernels for 0%

commit v1 on v0

--- a/solution.py
+++ b/solution.py
@@ -65,6 +65,15 @@
     return (select_experts, weighted_output)
 
 
+def sum_over(values, axis, ranks):
+    step = 1
+    while step < ranks:
+        pairs = [(rank, rank ^ step) for rank in range(ranks)]
+        values = values + lax.ppermute(values.astype(jnp.bfloat16), axis, pairs).astype(jnp.float32)
+        step *= 2
+    return values
+
+
 def per_device(
     hidden_in,
     queries,
@@ -93,7 +102,7 @@
     offset = lax.axis_index("tensor") * slab_width
     attended = attend(queries, new_keys, new_values, cache_keys, cache_values, cache_lengths)
     partial_sums = jnp.dot(attended, out_weight, preferred_element_type=jnp.float32)
-    attention = lax.psum(partial_sums, "tensor")
+    attention = sum_over(partial_sums, "tensor", tensor_ranks)
     residual = hidden_in.astype(jnp.float32) + attention
     normed = apply_norm(residual, norm_gain)
     select_experts, weighted_output = route_tables(
@@ -115,15 +124,17 @@
     expert_part = jnp.einsum(
         "secf,efd->secd", active, down_weight, preferred_element_type=jnp.float32
     )
-    expert_part = expert_part.reshape(expert_ranks, local_experts * capacity, model_width)
+    rows = local_experts * capacity
+    slabs = expert_part.astype(jnp.bfloat16).reshape(expert_ranks, rows, tensor_ranks, slab_width)
+    slabs = slabs.transpose(0, 2, 1, 3).reshape(expert_ranks * tensor_ranks, rows, slab_width)
     kept = lax.dynamic_slice_in_dim(residual, offset, slab_width, 1)
-    returned = lax.all_to_all(expert_part, "expert", split_axis=0, concat_axis=0, tiled=True)
-    returned = returned.reshape(experts * capacity, model_width)
+    returned = lax.all_to_all(
+        slabs, ("expert", "tensor"), split_axis=0, concat_axis=0, tiled=True
+    )
+    returned = returned.reshape(expert_ranks, tensor_ranks, rows, slab_width)
+    returned = jnp.sum(returned.astype(jnp.float32), axis=1).reshape(experts * capacity, slab_width)
     blended = jnp.dot(weighted_output, returned, precision=lax.Precision.HIGHEST)
-    expert_mixture = lax.psum_scatter(
-        blended.astype(jnp.bfloat16), "tensor", scatter_dimension=1, tiled=True
-    ).astype(jnp.float32)
-    return (kept + expert_mixture).astype(jnp.bfloat16)
+    return (kept + blended).astype(jnp.bfloat16)
 
 
 def solution(mesh):

time: 104 us -> 53.4 us (0.51)
  waiting for transfers between devices: 38.3 us -> 9.96 us
  blocking collectives: 27.1 us -> 13.3 us
  between operations: 13.6 us -> 0.16 us
  starting transfers between devices: 0.04 us -> 6.59 us
  matrix products: 17.2 us -> 18.7 us
  other arithmetic: 3.95 us -> 2.47 us
  local copies, waits for them, and re-layouts: 2.93 us -> 1.67 us
    psum x1 -> x0, waiting for transfers between devices: 23.1 us -> none  [per_device(): attention = lax.psum(partial_sums, 'tensor')]
    unnamed x3 -> x0, waiting for transfers between devices: 15.1 us -> none
    all_to_all x1 -> x0, blocking collectives: 14.5 us -> none  [per_device(): lax.all_to_all(expert_part, 'expert', split_axis=0, concat_axis=0, tiled=...]
    all_to_all x0 -> x1, waiting for transfers between devices: none -> 8.71 us  [per_device(): lax.all_to_all(slabs, ('expert', 'tensor'), split_axis=0, concat_axis=0,...]
    dot_general x1, matrix products: 0.81 us -> 6.08 us  [per_device(): jnp.einsum('secf,efd->secd', active, down_weight, preferred_element_type=...]
    all_to_all x0 -> x1, starting transfers between devices: none -> 3.6 us  [per_device(): lax.all_to_all(slabs, ('expert', 'tensor'), split_axis=0, concat_axis=0,...]
    dot_general x1 -> x0, matrix products: 3.5 us -> none  [per_device(): jnp.einsum('secd,edf->secf', arrived, up_weight, preferred_element_type=j...]
    ppermute x0 -> x1, starting transfers between devices: none -> 2.99 us  [sum_over(): lax.ppermute(values.astype(jnp.bfloat16), axis, pairs).astype(jnp.float32)]
where the time goes in v1:
time: 53.4 us; the launch traced here: 52.9 us
  matrix products  18.7 us (35%)
  blocking collectives  13.3 us (25%)
  waiting for transfers between devices  9.96 us (19%)
  starting transfers between devices  6.59 us (12%)
  other arithmetic  2.47 us (5%)
  local copies, waits for them, and re-layouts  1.67 us (3%)
    all_to_all x1, blocking collectives, per_device(): lax.all_to_all(outgoing, 'expert', split_axis=0, concat_axis=0, tiled=True)  13.3 us
    all_to_all x1, waiting for transfers between devices, per_device(): lax.all_to_all(slabs, ('expert', 'tensor'), split_axis=0, concat_axis=0,...  8.71 us
    dot_general x1, matrix products, per_device(): jnp.einsum('secf,efd->secd', active, down_weight, preferred_element_type=...  6.08 us
    dot_general x1, matrix products, per_device(): jnp.dot(attended, out_weight, preferred_element_type=jnp.float32)  4.32 us
    all_to_all x1, starting transfers between devices, per_device(): lax.all_to_all(slabs, ('expert', 'tensor'), split_axis=0, concat_axis=0,...  3.6 us
    dot_general x1, matrix products, per_device(): jnp.einsum('secd,edf->secf', arrived, gate_weight, preferred_element_type...  3.48 us
    ppermute x1, starting transfers between devices, sum_over(): lax.ppermute(values.astype(jnp.bfloat16), axis, pairs).astype(jnp.float32)  2.99 us
    dot_general x1, matrix products, attend(): jnp.einsum('sgqc,sgdc->sgqd', cache_prob, cache_values, preferred_element...  1.68 us
  transfers between devices with their start and end apart: 2, of which 2 were waited for; matrix products, arithmetic and copies ran while one was open for 1% of the time, Pallas kernels for 0%

profile of v1, /device:TPU:0, one launch (start us, length us, event | category | flops | bytes accessed | tf_op | source)
XLA Modules:
  0.0 52.9 jit_solution(12398712222890458173)
XLA Ops:
  0.0 0.0 copy-start
  0.0 0.8 %iota_compare_fusion.2 = pred[8,256]{1,0:T(8,128)(4,1)S(1)} fusion(s32[8]{0:T(128)} %param.21), kind=kLoop, calls=%fused_computation.53 | loop fusion | flops 2048 | bytes 2080 | tf_op jit(solution)/shard_map/lt | solution.py:25
  0.8 0.9 %fusion.52 = f32[8,4,1,4]{3,2,1,0:T(1,128)S(1)} fusion(bf16[8,4,4,64]{3,2,1,0:T(4,128)(2,1)} %bitcast.93, bf16[8,4,64,1]{2,1,0,3:T(4,128)(2,1)} %bitcast.95), kind=kOutput, calls=%fused_computation.50 | convolution fusion | flops 16384 | bytes 20992 | tf_op jit(solution)/shard_map/sgqd,sgd->sgq/dot_general | solution.py:21
  1.7 0.0 copy-done
  1.7 1.1 %fusion.59 = (f32[8,4,4]{2,1,0:T(4,128)S(1)}, f32[8,4,4,256]{3,2,1,0:T(4,128)S(1)}) fusion(bf16[8,4,4,64]{3,2,1,0:T(4,128)(2,1)} %bitcast.94, bf16[8,4,64,256]{3,2,1,0:T(8,128)(2,1)S(1)} %copy-done, pred[8,256]{1,0:T(8,128)(4,1)S(1)} %iota_compare_fusion.2), kind=kOutput, calls=%fused_computation.66 | convolution fusion | flops 4292480 | bytes 1198592 | tf_op jit(solution)/shard_map/sgqd,sgdc->sgqc/dot_general | solution.py:17
  2.8 0.0 copy-start.3
  2.8 0.0 copy-start.4
  2.9 0.0 copy-start.5
  2.9 0.0 copy-start.1
  2.9 0.2 fusion.37
  3.2 0.7 %convert_element_type.69 = f32[8,4,64]{2,1,0:T(4,128)S(1)} convert(bf16[8,4,64]{2,1,0:T(4,128)(2,1)} %param.18) | non-fusion elementwise | flops 2048 | bytes 12288 | tf_op jit(solution)/shard_map/convert_element_type | solution.py:38
  3.9 0.0 copy-start.2
  3.9 1.7 %fusion.28 = bf16[8,4,4,64]{3,2,1,0:T(4,128)(2,1)S(1)} fusion(bf16[8,4,64,256]{3,2,1,0:T(8,128)(2,1)} %param.20, f32[8,4,4,256]{3,2,1,0:T(4,128)S(1)} %get-tuple-element.16, f32[8,4,4]{2,1,0:T(4,128)S(1)} %get-tuple-element.10, f32[8,4,4]{2,1,0:T(4,128)S(1)} %multiply_maximum_fusion, f32[8,4,64]{2,1,0:T(4,128)S(1)} %convert_element_type.69, ...), kind=kOutput, calls=%fused_computation.17 | convolution fusion | flops 4317184 | bytes 1205760 | tf_op jit(solution)/shard_map/sgqc,sgdc->sgqd/dot_general | solution.py:33
  5.5 0.1 reshape.96
  5.6 4.3 %fusion.60 = (bf16[8,2880]{1,0:T(8,128)(2,1)S(1)}, f32[8,2880]{1,0:T(8,128)S(1)}) fusion(bf16[8,1024]{1,0:T(8,128)(2,1)S(1)} %reshape.96, bf16[1024,2880]{0,1:T(8,128)(2,1)} %param.22), kind=kOutput, calls=%fused_computation.67 | convolution fusion | flops 47208960 | bytes 6052864 | tf_op jit(solution)/shard_map/dot_general | solution.py:104
  10.0 3.0 %collective-permute-start = (bf16[8,2880]{1,0:T(8,128)(2,1)S(1)}, bf16[8,2880]{1,0:T(8,128)(2,1)S(1)}, u32[]{:S(2)}, u32[]{:S(2)}) collective-permute-start(bf16[8,2880]{1,0:T(8,128)(2,1)S(1)} %get-tuple-element.17), channel_id=1, source_target_pairs={{0,1},{1,0},{2,3},{3,2},{4,5},{5,4},{6,7},{7,6},{8,9},{9,8},{10,11... | collective-permute-start | bytes 138248 | tf_op jit(solution)/shard_map/ppermute | solution.py:72
  13.0 0.0 copy-done.3
  13.0 0.0 copy-done.4
  13.0 0.1 copy.39
  13.1 0.1 eq.53
  13.2 0.1 fusion.51
  13.2 0.1 reduce_window_sum.11
  13.3 0.2 select_reduce_fusion.1
  13.5 0.1 reduce_sum.67
  13.6 0.1 copy.41
  13.6 0.0 copy-done.5
  13.7 0.1 convert_reduce_fusion.1
  13.8 1.2 %collective-permute-done = bf16[8,2880]{1,0:T(8,128)(2,1)S(1)} collective-permute-done((bf16[8,2880]{1,0:T(8,128)(2,1)S(1)}, bf16[8,2880]{1,0:T(8,128)(2,1)S(1)}, u32[]{:S(2)}, u32[]{:S(2)}) %collective-permute-start) | collective-permute-done | bytes 46112 | tf_op jit(solution)/shard_map/ppermute | solution.py:72
  15.0 0.0 copy-done.1
  15.0 0.1 multiply_reduce_fusion
  15.2 0.0 copy-done.2
  15.2 0.3 convolution_convert_fusion
  15.5 0.1 reshape.97
  15.5 13.3 %all_to_all.10 = bf16[8,4,2880]{2,1,0:T(4,128)(2,1)S(1)} all-to-all(bf16[8,4,2880]{2,1,0:T(4,128)(2,1)S(1)} %reshape.97), channel_id=1, replica_groups=mesh['groups'=2,'expert'=8,'tensor'=2] {'expert'}, dimensions={0} | all-to-all | bytes 368640 | tf_op jit(solution)/shard_map/all_to_all | solution.py:115
  28.9 3.5 %fusion.13 = f32[8,1,4,720]{3,0,2,1:T(8,128)S(1)} fusion(bf16[1,2880,720]{1,2,0:T(8,128)(2,1)} %param.27, bf16[8,4,2880]{2,1,0:T(4,128)(2,1)S(1)} %all_to_all.10), kind=kOutput, calls=%fused_computation.11 | convolution fusion | flops 132710400 | bytes 4423680 | tf_op jit(solution)/shard_map/secd,edf->secf/dot_general | solution.py:117
  32.3 6.1 %fusion.9 = bf16[8,1,4,2880]{3,0,2,1:T(8,128)(2,1)S(1)} fusion(bf16[1,720,2880]{2,1,0:T(8,128)(2,1)} %param.29, bf16[1,2880,720]{1,2,0:T(8,128)(2,1)} %param.28, bf16[8,4,2880]{2,1,0:T(4,128)(2,1)S(1)} %all_to_all.10, f32[8,1,4,720]{3,0,2,1:T(8,128)S(1)} %fusion.13), kind=kOutput, calls=%fused_computation.8 | convolution fusion | flops 265697280 | bytes 8755200 | tf_op jit(solution)/shard_map/secf,efd->secd/dot_general | solution.py:124
  38.4 0.3 reshape.102
  38.7 0.8 %copy.44 = bf16[8,2,4,1440]{3,2,1,0:T(4,128)(2,1)} copy(bf16[8,2,4,1440]{3,1,0,2:T(2,128)(2,1)S(1)} %bitcast.90) | data formatting | bytes 368640 | tf_op jit(solution)/shard_map/transpose | solution.py:129
  39.5 3.6 %all-to-all-start.1 = ((bf16[16,4,1440]{2,1,0:T(4,128)(2,1)}), bf16[16,4,1440]{2,1,0:T(4,128)(2,1)S(1)}, u32[]{:S(2)}, u32[]{:S(2)}) async-start(bf16[16,4,1440]{2,1,0:T(4,128)(2,1)} %bitcast.27), calls=%async_computation.1 | async-start | bytes 393216 | tf_op jit(solution)/shard_map/all_to_all | solution.py:131
  43.1 8.7 %all-to-all-done.1 = bf16[16,4,1440]{2,1,0:T(4,128)(2,1)S(1)} async-done(((bf16[16,4,1440]{2,1,0:T(4,128)(2,1)}), bf16[16,4,1440]{2,1,0:T(4,128)(2,1)S(1)}, u32[]{:S(2)}, u32[]{:S(2)}) %all-to-all-start.1) | async-done | bytes 184352 | tf_op jit(solution)/shard_map/all_to_all | solution.py:131
  51.8 0.1 convert_reduce_fusion
  52.0 0.1 reshape.104
  52.0 0.8 %add_convert_fusion = bf16[8,1440]{1,0:T(8,128)(2,1)} fusion(f32[8,2880]{1,0:T(8,128)S(1)} %get-tuple-element.8, s32[]{:T(128)S(6)} %select_n.21, f32[8,32]{1,0:T(8,128)S(1)} %get-tuple-element.6, f32[32,1440]{1,0:T(8,128)S(1)} %reshape.104), kind=kOutput, calls=%fused_computation.36 | convolution fusion | flops 4446720 | bytes 254468 | tf_op jit(solution)/shard_map/dot_general | solution.py:136
  (7 shorter events, 0.1 us)
Async XLA Ops:
  0.0 1.7 %copy-start = (bf16[8,4,64,256]{3,2,1,0:T(8,128)(2,1)S(1)}, bf16[8,4,64,256]{3,2,1,0:T(8,128)(2,1)}, u32[]{:S(2)}) copy-start(bf16[8,4,64,256]{3,2,1,0:T(8,128)(2,1)} %param.19) | copy-start | bytes 3145732
  2.8 10.1 %copy-start.3 = (f32[8,4]{0,1:T(4,128)S(1)}, f32[8,4]{0,1:T(4,128)}, u32[]{:S(2)}) copy-start(f32[8,4]{0,1:T(4,128)} %param.25) | copy-start | bytes 388
  2.8 10.1 %copy-start.4 = (s32[8,4]{0,1:T(4,128)S(1)}, s32[8,4]{0,1:T(4,128)}, u32[]{:S(2)}) copy-start(s32[8,4]{0,1:T(4,128)} %param.24) | copy-start | bytes 388
  2.9 10.8 %copy-start.5 = (s32[8,4]{0,1:T(4,128)S(1)}, s32[8,4]{0,1:T(4,128)}, u32[]{:S(2)}) copy-start(s32[8,4]{0,1:T(4,128)} %param.26) | copy-start | bytes 388
  2.9 12.1 %copy-start.1 = (bf16[8,2880]{1,0:T(8,128)(2,1)S(1)}, bf16[8,2880]{1,0:T(8,128)(2,1)}, u32[]{:S(2)}) copy-start(bf16[8,2880]{1,0:T(8,128)(2,1)} %param.15) | copy-start | bytes 138244
  3.9 11.3 %copy-start.2 = (f32[2880]{0:T(1024)S(1)}, f32[2880]{0:T(1024)}, u32[]{:S(2)}) copy-start(f32[2880]{0:T(1024)} %param.23) | copy-start | bytes 34564
  10.0 5.0 %collective-permute-start = (bf16[8,2880]{1,0:T(8,128)(2,1)S(1)}, bf16[8,2880]{1,0:T(8,128)(2,1)S(1)}, u32[]{:S(2)}, u32[]{:S(2)}) collective-permute-start(bf16[8,2880]{1,0:T(8,128)(2,1)S(1)} %get-tuple-element.17), channel_id=1, source_target_pairs={{0,1},{1,0},{2,3},{3,2},{4,5},{5,4},{6,7},{7,6},{8,9},{9,8},{10,11... | collective-permute-start | bytes 138248 | tf_op jit(solution)/shard_map/ppermute | solution.py:72
  39.5 12.3 %all-to-all-start.1 = ((bf16[16,4,1440]{2,1,0:T(4,128)(2,1)}), bf16[16,4,1440]{2,1,0:T(4,128)(2,1)S(1)}, u32[]{:S(2)}, u32[]{:S(2)}) async-start(bf16[16,4,1440]{2,1,0:T(4,128)(2,1)} %bitcast.27), calls=%async_computation.1 | async-start | bytes 393216 | tf_op jit(solution)/shard_map/all_to_all | solution.py:131

commit v2 on v0

v2 whole, which is shorter than its diff:
```python
import functools

import jax
import jax.numpy as jnp
from jax import lax
from jax.experimental import pallas as pl
from jax.experimental.pallas import tpu as pltpu
from jax.sharding import PartitionSpec as P

EPSILON = 1e-05
GLU_SLOPE = 1.702
WINDOW_FLOPS = 20_000_000_000


def attend(queries, new_keys, new_values, cache_keys, cache_values, cache_lengths):
    sequence_count, head_count, head_dim = queries.shape
    kv_heads = new_keys.shape[1]
    group_size = head_count // kv_heads
    scaling = 1.0 / head_dim**0.5
    query_rows = queries.reshape(sequence_count, kv_heads, group_size, head_dim)
    scores = (
        jnp.einsum("sgqd,sgdc->sgqc", query_rows, cache_keys, preferred_element_type=jnp.float32)
        * scaling
    )
    own_score = (
        jnp.einsum("sgqd,sgd->sgq", query_rows, new_keys, preferred_element_type=jnp.float32)
        * scaling
    )
    positions = jnp.arange(cache_keys.shape[3], dtype=jnp.int32)
    visible = positions[None, :] < cache_lengths[:, None]
    scores = jnp.where(visible[:, None, None, :], scores, -1e30)
    highest = jnp.maximum(jnp.max(scores, axis=3), own_score)
    cache_exp = jnp.exp(scores - highest[..., None])
    own_exp = jnp.exp(own_score - highest)
    totals = jnp.sum(cache_exp, axis=3) + own_exp
    cache_prob = (cache_exp / totals[..., None]).astype(jnp.bfloat16)
    own_prob = (own_exp / totals).astype(jnp.bfloat16)
    attended = jnp.einsum(
        "sgqc,sgdc->sgqd", cache_prob, cache_values, preferred_element_type=jnp.float32
    )
    attended = (
        attended
        + own_prob.astype(jnp.float32)[..., None] * new_values.astype(jnp.float32)[:, :, None, :]
    )
    return attended.astype(jnp.bfloat16).reshape(sequence_count, head_count * head_dim)


VMEM = pl.BlockSpec(memory_space=pltpu.VMEM)
LAST_DIMS = (((1,), (1,)), ((), ()))
FIRST_DIMS = (((0,), (0,)), ((), ()))
MIB = 1 << 20


def call(kernel, outs, args, flops, moved, limit):
    return pl.pallas_call(
        kernel,
        out_shape=[jax.ShapeDtypeStruct(shape, dtype) for shape, dtype in outs],
        in_specs=[VMEM] * len(args),
        out_specs=[VMEM] * len(outs),
        compiler_params=pltpu.CompilerParams(vmem_limit_bytes=limit),
        cost_estimate=pl.CostEstimate(flops=flops, bytes_accessed=moved, transcendentals=0),
    )(*args)


def route_weights(expert_ids, route_probs, route_order, experts):
    picked = jnp.zeros(expert_ids.shape, jnp.float32)
    for column in range(expert_ids.shape[1]):
        picked = picked + jnp.where(route_order == column, route_probs[:, column : column + 1], 0.0)
    weights = picked / jnp.sum(route_probs, axis=1, keepdims=True)
    named = expert_ids[:, :, None] == jnp.arange(experts, dtype=jnp.int32)[None, None, :]
    return jnp.sum(jnp.where(named, weights[:, :, None], 0.0), axis=1)


def exchange(values, axis, ranks):
    step = 1
    while True:
        pairs = [(rank, rank ^ step) for rank in range(ranks)]
        received = lax.ppermute(values.astype(jnp.bfloat16), axis, pairs)
        step *= 2
        if step >= ranks:
            return values, received
        values = values + received.astype(jnp.float32)


def norm_kernel(mine_ref, received_ref, hidden_ref, gain_ref, table_ref, residual_ref, rows_ref):
    width = hidden_ref.shape[1]
    residual = (
        hidden_ref[...].astype(jnp.float32) + mine_ref[...] + received_ref[...].astype(jnp.float32)
    )
    residual_ref[...] = residual
    mean_square = jnp.mean(residual * residual, axis=1, keepdims=True)
    normed = residual * lax.rsqrt(mean_square + EPSILON) * gain_ref[...]
    rows_ref[:, :width] = normed.astype(jnp.bfloat16)
    rows_ref[:, width:] = table_ref[...]


def expert_kernel(blocks, experts, *refs):
    row_refs = refs[:blocks]
    gate_ref, up_ref, down_ref, mine_ref, other_ref = refs[blocks:]
    local_experts, _, width = down_ref.shape
    rows = jnp.concatenate([ref[:, :width] for ref in row_refs], axis=0)
    table = jnp.concatenate([ref[:, width:] for ref in row_refs], axis=0).astype(jnp.float32)
    column = lax.broadcasted_iota(jnp.int32, table.shape, 1)
    total = None
    for local in range(local_experts):
        expert = lax.axis_index("expert") * local_experts + local
        chosen = (column == expert) | (column == expert + experts)
        weight = jnp.sum(jnp.where(chosen, table, 0.0), axis=1, keepdims=True)
        gate = lax.dot_general(
            gate_ref[local], rows, LAST_DIMS, preferred_element_type=jnp.float32
        )
        up = lax.dot_general(up_ref[local], rows, LAST_DIMS, preferred_element_type=jnp.float32)
        active = (gate * jax.nn.sigmoid(GLU_SLOPE * gate) * (up + 1.0)).astype(jnp.bfloat16)
        part = lax.dot_general(
            active, down_ref[local], FIRST_DIMS, preferred_element_type=jnp.float32
        )
        part = part * weight
        total = part if total is None else total + part
    half = mine_ref.shape[0]
    mine_ref[...] = total[:half]
    if other_ref.shape[0] == half:
        other_ref[...] = total[half:].astype(jnp.bfloat16)


def split_kernel(mine_ref, received_ref, kept_ref, *sent_refs):
    size = kept_ref.shape[0]
    kept_ref[...] = mine_ref[:size] + received_ref[:size].astype(jnp.float32)
    for number, sent_ref in enumerate(sent_refs, 1):
        block = pl.ds(number * size, size)
        total = mine_ref[block] + received_ref[block].astype(jnp.float32)
        sent_ref[...] = total.astype(jnp.bfloat16)


def gather_kernel(kept_ref, *refs):
    *received_refs, total_ref = refs
    total = kept_ref[...]
    for received_ref in received_refs:
        total = total + received_ref[...].astype(jnp.float32)
    total_ref[...] = total


def per_device(
    hidden_in,
    queries,
    new_keys,
    new_values,
    cache_keys,
    cache_values,
    cache_lengths,
    out_weight,
    norm_gain,
    expert_ids,
    route_probs,
    route_order,
    gate_weight,
    up_weight,
    down_weight,
):
    sequences, width = hidden_in.shape
    expert_ranks = lax.axis_size("expert")
    tensor_ranks = lax.axis_size("tensor")
    local_experts, hidden_units = down_weight.shape[:2]
    experts = local_experts * expert_ranks
    inner = 2
    outer = expert_ranks // inner
    slab_width = width // tensor_ranks
    offset = lax.axis_index("tensor") * slab_width
    row_width = -(-(width + 2 * experts) // 128) * 128

    def to_outer(values, step):
        pairs = [(rank, rank ^ (step * inner)) for rank in range(expert_ranks)]
        return lax.ppermute(values, "expert", pairs)

    def to_inner(values):
        return lax.ppermute(values, "expert", [(rank, rank ^ 1) for rank in range(expert_ranks)])

    attended = attend(queries, new_keys, new_values, cache_keys, cache_values, cache_lengths)
    partial_sums = jnp.dot(attended, out_weight, preferred_element_type=jnp.float32)
    mine, received = exchange(partial_sums, "tensor", tensor_ranks)

    weights = route_weights(expert_ids, route_probs, route_order, experts)
    high = weights.astype(jnp.bfloat16)
    low = (weights - high.astype(jnp.float32)).astype(jnp.bfloat16)
    spare = jnp.zeros((sequences, row_width - width - 2 * experts), jnp.bfloat16)
    table = jnp.concatenate([high, low, spare], axis=1)

    block = (sequences, width)
    residual, rows = call(
        norm_kernel,
        [(block, jnp.float32), ((sequences, row_width), jnp.bfloat16)],
        (mine, received, hidden_in, norm_gain.reshape(1, width), table),
        flops=WINDOW_FLOPS,
        moved=sequences * width * 16,
        limit=2 * MIB,
    )

    near = [rows] + [to_outer(rows, step) for step in range(1, outer)]
    far = [to_inner(piece) for piece in near]
    half = (outer * sequences, width)
    mine, other = call(
        functools.partial(expert_kernel, 2 * outer, experts),
        [(half, jnp.float32), (half, jnp.bfloat16)],
        (*near, *far, gate_weight.swapaxes(1, 2), up_weight.swapaxes(1, 2), down_weight),
        flops=12 * half[0] * width * hidden_units * local_experts,
        moved=6 * width * hidden_units * local_experts,
        limit=16 * MIB,
    )
    received = to_inner(other)
    kept, *sent = call(
        split_kernel,
        [(block, jnp.float32)] + [(block, jnp.bfloat16)] * (outer - 1),
        (mine, received),
        flops=half[0] * width,
        moved=half[0] * width * 8,
        limit=4 * MIB,
    )
    returned = [to_outer(piece, step) for step, piece in enumerate(sent, 1)]
    (mixture,) = call(
        gather_kernel,
        [(block, jnp.float32)],
        (kept, *returned),
        flops=half[0] * width,
        moved=half[0] * width * 2,
        limit=2 * MIB,
    )
    mine, received = exchange(mixture, "tensor", tensor_ranks)
    total = residual + mine + received.astype(jnp.float32)
    return lax.dynamic_slice_in_dim(total, offset, slab_width, 1).astype(jnp.bfloat16)


def solution(mesh):
    in_specs = (
        P(("groups", "expert"), None),
        P(("groups", "expert"), "tensor", None),
        P(("groups", "expert"), "tensor", None),
        P(("groups", "expert"), "tensor", None),
        P(("groups", "expert"), "tensor", None, None),
        P(("groups", "expert"), "tensor", None, None),
        P(("groups", "expert")),
        P("tensor", None),
        P(),
        P(("groups", "expert"), None),
        P(("groups", "expert"), None),
        P(("groups", "expert"), None),
        P("expert", None, "tensor"),
        P("expert", None, "tensor"),
        P("expert", "tensor", None),
    )
    out_specs = P(("groups", "expert"), "tensor")
    return jax.shard_map(
        per_device, mesh=mesh, in_specs=in_specs, out_specs=out_specs, check_vma=False
    )
```

time: 104 us -> 50.5 us (0.49)
  blocking collectives: 27.1 us -> 0 us
  waiting for transfers between devices: 38.3 us -> 15.3 us
  starting transfers between devices: 0.04 us -> 13.6 us
  between operations: 13.6 us -> 0.16 us
  matrix products: 17.2 us -> 7.98 us
  local copies, waits for them, and re-layouts: 2.93 us -> 6.82 us
  Pallas kernels: 0 us -> 3.48 us
  other arithmetic: 3.95 us -> 2.68 us
    all_to_all x2 -> x0, blocking collectives: 27.1 us -> none  [the longest x1 14.5 us: per_device(): lax.all_to_all(expert_part, 'expert', split_axis=0, concat_axis=0, tiled=...]
    psum x1 -> x0, waiting for transfers between devices: 23.1 us -> none  [per_device(): attention = lax.psum(partial_sums, 'tensor')]
    ppermute x0 -> x13, waiting for transfers between devices: none -> 15.3 us  [the longest x6 8.54 us: to_outer(): return lax.ppermute(values, 'expert', pairs)]
    unnamed x3 -> x0, waiting for transfers between devices: 15.1 us -> none
    ppermute x0 -> x13, starting transfers between devices: none -> 13.6 us  [the longest x6 8.31 us: to_outer(): return lax.ppermute(values, 'expert', pairs)]
    dot_general x5 -> x0, matrix products: 8.52 us -> none  [the longest x1 3.63 us: per_device(): jnp.einsum('secd,edf->secf', arrived, gate_weight, preferred_element_type...]
    unnamed x19 -> x18, local copies, waits for them, and re-layouts: 2.39 us -> 6.62 us
    pallas_call x0 -> x4, Pallas kernels: none -> 3.48 us  [call(): pl.pallas_call(kernel, out_shape=[jax.ShapeDtypeStruct(shape, dtype) for...]
  transfers between devices with their start and end apart: 2 -> 13, of which waited for: 2 -> 8; matrix products, arithmetic and copies ran while one was open for 1% -> 1% of each run, Pallas kernels for 0% -> 0%
where the time goes in v2:
time: 50.5 us; the launch traced here: 50.1 us
  waiting for transfers between devices  15.3 us (30%)
  starting transfers between devices  13.6 us (27%)
  matrix products  7.98 us (16%)
  local copies, waits for them, and re-layouts  6.82 us (14%)
  Pallas kernels  3.48 us (7%)
  other arithmetic  2.68 us (5%)
    ppermute x6, waiting for transfers between devices, to_outer(): return lax.ppermute(values, 'expert', pairs)  8.54 us
    ppermute x6, starting transfers between devices, to_outer(): return lax.ppermute(values, 'expert', pairs)  8.31 us
    unnamed x18, local copies, waits for them, and re-layouts  6.62 us
    ppermute x2, starting transfers between devices, exchange(): received = lax.ppermute(values.astype(jnp.bfloat16), axis, pairs)  4.55 us
    dot_general x1, matrix products, per_device(): jnp.dot(attended, out_weight, preferred_element_type=jnp.float32)  4.32 us
    ppermute x2, waiting for transfers between devices, exchange(): received = lax.ppermute(values.astype(jnp.bfloat16), axis, pairs)  4.3 us
    pallas_call x4, Pallas kernels, call(): pl.pallas_call(kernel, out_shape=[jax.ShapeDtypeStruct(shape, dtype) for...  3.48 us
    ppermute x5, waiting for transfers between devices, to_inner(): lax.ppermute(values, 'expert', [(rank, rank ^ 1) for rank in range(expert...  2.48 us
  transfers between devices with their start and end apart: 13, of which 8 were waited for; matrix products, arithmetic and copies ran while one was open for 1% of the time, Pallas kernels for 0%

profile of v2, /device:TPU:0, one launch (start us, length us, event | category | flops | bytes accessed | tf_op | source)
XLA Modules:
  0.0 50.1 jit_solution(16684788215772455273)
XLA Ops:
  0.0 0.0 copy-start
  0.0 0.0 copy-start.6
  0.0 0.0 copy-start.7
  0.0 0.0 copy-start.8
  0.0 0.0 copy-start.5
  0.0 0.0 copy-start.4
  0.0 0.8 %iota_compare_fusion.1 = pred[8,256]{1,0:T(8,128)(4,1)S(1)} fusion(s32[8]{0:T(128)} %param.21), kind=kLoop, calls=%fused_computation.19 | loop fusion | flops 2048 | bytes 2080 | tf_op jit(solution)/shard_map/lt | solution.py:30
  0.8 0.9 %fusion.7 = f32[8,4,1,4]{3,2,1,0:T(1,128)S(1)} fusion(bf16[8,4,4,64]{3,2,1,0:T(4,128)(2,1)} %bitcast.24, bf16[8,4,64,1]{2,1,0,3:T(4,128)(2,1)} %bitcast.26), kind=kOutput, calls=%fused_computation.16 | convolution fusion | flops 16384 | bytes 20992 | tf_op jit(solution)/shard_map/sgqd,sgd->sgq/dot_general | solution.py:26
  1.8 0.0 copy-done
  1.8 1.1 %fusion.11 = (f32[8,4,4]{2,1,0:T(4,128)S(1)}, f32[8,4,4,256]{3,2,1,0:T(4,128)S(1)}) fusion(bf16[8,4,4,64]{3,2,1,0:T(4,128)(2,1)} %bitcast.25, bf16[8,4,64,256]{3,2,1,0:T(8,128)(2,1)S(1)} %copy-done, pred[8,256]{1,0:T(8,128)(4,1)S(1)} %iota_compare_fusion.1), kind=kOutput, calls=%fused_computation.29 | convolution fusion | flops 4292480 | bytes 1198592 | tf_op jit(solution)/shard_map/sgqd,sgdc->sgqc/dot_general | solution.py:22
  2.9 0.2 fusion.2
  3.1 0.7 %convert_element_type.39 = f32[8,4,64]{2,1,0:T(4,128)S(1)} convert(bf16[8,4,64]{2,1,0:T(4,128)(2,1)} %param.18) | non-fusion elementwise | flops 2048 | bytes 12288 | tf_op jit(solution)/shard_map/convert_element_type | solution.py:43
  3.8 1.7 %fusion.1 = bf16[8,4,4,64]{3,2,1,0:T(4,128)(2,1)S(1)} fusion(bf16[8,4,64,256]{3,2,1,0:T(8,128)(2,1)} %param.20, f32[8,4,4,256]{3,2,1,0:T(4,128)S(1)} %get-tuple-element.30, f32[8,4,4]{2,1,0:T(4,128)S(1)} %get-tuple-element.24, f32[8,4,4]{2,1,0:T(4,128)S(1)} %multiply_maximum_fusion, f32[8,4,64]{2,1,0:T(4,128)S(1)} %convert_element_type.39, ...), kind=kOutput, calls=%fused_computation.3 | convolution fusion | flops 4317184 | bytes 1205760 | tf_op jit(solution)/shard_map/sgqc,sgdc->sgqd/dot_general | solution.py:38
  5.5 0.1 reshape.34
  5.6 4.3 %fusion.12 = (bf16[8,2880]{1,0:T(8,128)(2,1)S(1)}, f32[8,2880]{1,0:T(8,128)S(1)}) fusion(bf16[8,1024]{1,0:T(8,128)(2,1)S(1)} %reshape.34, bf16[1024,2880]{0,1:T(8,128)(2,1)} %param.22), kind=kOutput, calls=%fused_computation.30 | convolution fusion | flops 47208960 | bytes 6052864 | tf_op jit(solution)/shard_map/dot_general | solution.py:178
  9.9 3.0 %collective-permute-start = (bf16[8,2880]{1,0:T(8,128)(2,1)S(1)}, bf16[8,2880]{1,0:T(8,128)(2,1)S(1)}, u32[]{:S(2)}, u32[]{:S(2)}) collective-permute-start(bf16[8,2880]{1,0:T(8,128)(2,1)S(1)} %get-tuple-element.31), channel_id=1, source_target_pairs={{0,1},{1,0},{2,3},{3,2},{4,5},{5,4},{6,7},{7,6},{8,9},{9,8},{10,11... | collective-permute-start | bytes 138248 | tf_op jit(solution)/shard_map/ppermute | solution.py:78
  12.9 0.0 copy-done.6
  13.0 0.0 copy-done.7
  13.0 0.0 copy-done.8
  13.0 0.1 select_reduce_fusion
  13.1 0.1 pad.2.clone
  13.2 0.1 maximum_maximum_fusion.table_ref
  13.2 0.0 copy-done.5
  13.3 1.7 %collective-permute-done.received_ref = bf16[8,2880]{1,0:T(8,128)(2,1)S(1)} collective-permute-done((bf16[8,2880]{1,0:T(8,128)(2,1)S(1)}, bf16[8,2880]{1,0:T(8,128)(2,1)S(1)}, u32[]{:S(2)}, u32[]{:S(2)}) %collective-permute-start) | collective-permute-done | bytes 46112 | tf_op jit(solution)/shard_map/ppermute | solution.py:78
  15.0 0.0 copy-done.4
  15.0 0.1 shard_map.145
  15.1 2.2 %collective-permute-start.1 = (bf16[8,2944]{1,0:T(8,128)(2,1)S(1)}, bf16[8,2944]{1,0:T(8,128)(2,1)S(1)}, u32[]{:S(2)}, u32[]{:S(2)}) collective-permute-start(bf16[8,2944]{1,0:T(8,128)(2,1)S(1)} %get-tuple-element.14.refs_0_), channel_id=1, source_target_pairs={{0,4},{2,6},{4,0},{6,2},{8,12},{10,14},{12,8},{14,10},{1,5},{3,7},... | collective-permute-start | bytes 141320 | tf_op jit(solution)/shard_map/ppermute | solution.py:172
  17.3 2.6 %collective-permute-start.2 = (bf16[8,2944]{1,0:T(8,128)(2,1)S(1)}, bf16[8,2944]{1,0:T(8,128)(2,1)S(1)}, u32[]{:S(2)}, u32[]{:S(2)}) collective-permute-start(bf16[8,2944]{1,0:T(8,128)(2,1)S(1)} %get-tuple-element.14.refs_0_), channel_id=1, source_target_pairs={{0,8},{2,10},{4,12},{6,14},{8,0},{10,2},{12,4},{14,6},{1,9},{3,11}... | collective-permute-start | bytes 141320 | tf_op jit(solution)/shard_map/ppermute | solution.py:172
  19.9 0.0 collective-permute-start.3
  19.9 0.0 collective-permute-start.4
  19.9 0.0 collective-permute-done.1.refs_1_
  19.9 0.5 %collective-permute-start.5 = (bf16[8,2944]{1,0:T(8,128)(2,1)S(1)}, bf16[8,2944]{1,0:T(8,128)(2,1)S(1)}, u32[]{:S(2)}, u32[]{:S(2)}) collective-permute-start(bf16[8,2944]{1,0:T(8,128)(2,1)S(1)} %collective-permute-done.1.refs_1_), channel_id=1, source_target_pairs={{0,2},{2,0},{4,6},{6,4},{8,10},{10,8},{12,14},{14,12},{1,3},{3,1},... | collective-permute-start | bytes 141320 | tf_op jit(solution)/shard_map/ppermute | solution.py:175
  20.4 2.9 %collective-permute-done.2.refs_2_ = bf16[8,2944]{1,0:T(8,128)(2,1)S(1)} collective-permute-done((bf16[8,2944]{1,0:T(8,128)(2,1)S(1)}, bf16[8,2944]{1,0:T(8,128)(2,1)S(1)}, u32[]{:S(2)}, u32[]{:S(2)}) %collective-permute-start.2) | collective-permute-done | bytes 47136 | tf_op jit(solution)/shard_map/ppermute | solution.py:172
  23.3 0.0 collective-permute-start.6
  23.3 2.5 %collective-permute-done.3.refs_3_ = bf16[8,2944]{1,0:T(8,128)(2,1)S(1)} collective-permute-done((bf16[8,2944]{1,0:T(8,128)(2,1)S(1)}, bf16[8,2944]{1,0:T(8,128)(2,1)S(1)}, u32[]{:S(2)}, u32[]{:S(2)}) %collective-permute-start.3) | collective-permute-done | bytes 47136 | tf_op jit(solution)/shard_map/ppermute | solution.py:172
  25.7 0.0 collective-permute-start.7
  25.7 0.0 collective-permute-done.4.refs_4_
  25.7 0.0 collective-permute-done.5.refs_5_
  25.7 0.0 collective-permute-done.6.refs_6_
  25.8 1.2 %collective-permute-done.7.refs_7_ = bf16[8,2944]{1,0:T(8,128)(2,1)S(1)} collective-permute-done((bf16[8,2944]{1,0:T(8,128)(2,1)S(1)}, bf16[8,2944]{1,0:T(8,128)(2,1)S(1)}, u32[]{:S(2)}, u32[]{:S(2)}) %collective-permute-start.7) | collective-permute-done | bytes 47136 | tf_op jit(solution)/shard_map/ppermute | solution.py:175
  27.0 0.0 copy-start.1
  27.0 2.2 %copy-done.1 = bf16[1,2880,720]{1,2,0:T(8,128)(2,1)S(1)} copy-done((bf16[1,2880,720]{1,2,0:T(8,128)(2,1)S(1)}, bf16[1,2880,720]{1,2,0:T(8,128)(2,1)}, u32[]{:S(2)}) %copy-start.1) | copy-done | bytes 4147224
  29.2 0.0 copy-start.2
  29.2 2.2 %copy-done.2 = bf16[1,2880,720]{1,2,0:T(8,128)(2,1)S(1)} copy-done((bf16[1,2880,720]{1,2,0:T(8,128)(2,1)S(1)}, bf16[1,2880,720]{1,2,0:T(8,128)(2,1)}, u32[]{:S(2)}) %copy-start.2) | copy-done | bytes 4147224
  31.4 0.0 copy-start.3
  31.4 2.2 %copy-done.3 = bf16[1,720,2880]{2,1,0:T(8,128)(2,1)S(1)} copy-done((bf16[1,720,2880]{2,1,0:T(8,128)(2,1)S(1)}, bf16[1,720,2880]{2,1,0:T(8,128)(2,1)}, u32[]{:S(2)}) %copy-start.3) | copy-done | bytes 4147224
  33.6 3.3 %shard_map.146 = (f32[32,2880]{1,0:T(8,128)S(1)}, bf16[32,2880]{1,0:T(8,128)(2,1)S(1)}) custom-call(bf16[8,2944]{1,0:T(8,128)(2,1)S(1)} %get-tuple-element.14.refs_0_, bf16[8,2944]{1,0:T(8,128)(2,1)S(1)} %collective-permute-done.1.refs_1_, bf16[8,2944]{1,0:T(8,128)(2,1)S(1)} %collective-permute-done.2.refs_2_, ...), custom_call_target="tpu_custom_call" | custom-call | flops 796262400 | bytes 12441600 | tf_op jit(solution)/shard_map/pallas_call | solution.py:55
  36.9 0.2 collective-permute-start.8
  37.1 1.3 %collective-permute-done.8.received_ref = bf16[32,2880]{1,0:T(8,128)(2,1)S(1)} collective-permute-done((bf16[32,2880]{1,0:T(8,128)(2,1)S(1)}, bf16[32,2880]{1,0:T(8,128)(2,1)S(1)}, u32[]{:S(2)}, u32[]{:S(2)}) %collective-permute-start.8) | collective-permute-done | bytes 184352 | tf_op jit(solution)/shard_map/ppermute | solution.py:175
  38.4 0.1 collective-permute-start.10
  38.5 1.0 %collective-permute-start.11 = (bf16[8,2880]{1,0:T(8,128)(2,1)S(1)}, bf16[8,2880]{1,0:T(8,128)(2,1)S(1)}, u32[]{:S(2)}, u32[]{:S(2)}) collective-permute-start(bf16[8,2880]{1,0:T(8,128)(2,1)S(1)} %get-tuple-element.20), channel_id=1, source_target_pairs={{0,12},{2,14},{4,8},{6,10},{8,4},{10,6},{12,0},{14,2},{1,13},{3,15... | collective-permute-start | bytes 138248 | tf_op jit(solution)/shard_map/ppermute | solution.py:172
  39.5 2.5 %collective-permute-start.9 = (bf16[8,2880]{1,0:T(8,128)(2,1)S(1)}, bf16[8,2880]{1,0:T(8,128)(2,1)S(1)}, u32[]{:S(2)}, u32[]{:S(2)}) collective-permute-start(bf16[8,2880]{1,0:T(8,128)(2,1)S(1)} %get-tuple-element.18), channel_id=1, source_target_pairs={{0,4},{2,6},{4,0},{6,2},{8,12},{10,14},{12,8},{14,10},{1,5},{3,7},... | collective-permute-start | bytes 138248 | tf_op jit(solution)/shard_map/ppermute | solution.py:172
  42.0 2.7 %collective-permute-done.10.refs_1_ = bf16[8,2880]{1,0:T(8,128)(2,1)S(1)} collective-permute-done((bf16[8,2880]{1,0:T(8,128)(2,1)S(1)}, bf16[8,2880]{1,0:T(8,128)(2,1)S(1)}, u32[]{:S(2)}, u32[]{:S(2)}) %collective-permute-start.10) | collective-permute-done | bytes 46112 | tf_op jit(solution)/shard_map/ppermute | solution.py:172
  44.7 0.0 collective-permute-done.11.refs_2_
  44.7 0.5 %collective-permute-done.9.refs_0_ = bf16[8,2880]{1,0:T(8,128)(2,1)S(1)} collective-permute-done((bf16[8,2880]{1,0:T(8,128)(2,1)S(1)}, bf16[8,2880]{1,0:T(8,128)(2,1)S(1)}, u32[]{:S(2)}, u32[]{:S(2)}) %collective-permute-start.9) | collective-permute-done | bytes 46112 | tf_op jit(solution)/shard_map/ppermute | solution.py:172
  45.2 1.6 %collective-permute-start.12 = (bf16[8,2880]{1,0:T(8,128)(2,1)S(1)}, bf16[8,2880]{1,0:T(8,128)(2,1)S(1)}, u32[]{:S(2)}, u32[]{:S(2)}) collective-permute-start(bf16[8,2880]{1,0:T(8,128)(2,1)S(1)} %convert_element_type.45), channel_id=1, source_target_pairs={{0,1},{1,0},{2,3},{3,2},{4,5},{5,4},{6,7},{7,6},{8,9},{9,8},{10,11... | collective-permute-start | bytes 138248 | tf_op jit(solution)/shard_map/ppermute | solution.py:78
  46.8 2.6 %collective-permute-done.12 = bf16[8,2880]{1,0:T(8,128)(2,1)S(1)} collective-permute-done((bf16[8,2880]{1,0:T(8,128)(2,1)S(1)}, bf16[8,2880]{1,0:T(8,128)(2,1)S(1)}, u32[]{:S(2)}, u32[]{:S(2)}) %collective-permute-start.12) | collective-permute-done | bytes 46112 | tf_op jit(solution)/shard_map/ppermute | solution.py:78
  49.3 0.7 %fusion.6 = bf16[8,1440]{1,0:T(8,128)(2,1)} fusion(f32[8,2880]{1,0:T(8,128)S(1)} %shard_map.148, s32[]{:T(128)S(6)} %select_n.30, f32[8,2880]{1,0:T(8,128)S(1)} %get-tuple-element.13, bf16[8,2880]{1,0:T(8,128)(2,1)S(1)} %collective-permute-done.12), kind=kLoop, calls=%fused_computation.11 | loop fusion | flops 46080 | bytes 138244 | tf_op jit(solution)/shard_map/convert_element_type | solution.py:228
  (11 shorter events, 0.2 us)
Async XLA Ops:
  0.0 1.8 %copy-start = (bf16[8,4,64,256]{3,2,1,0:T(8,128)(2,1)S(1)}, bf16[8,4,64,256]{3,2,1,0:T(8,128)(2,1)}, u32[]{:S(2)}) copy-start(bf16[8,4,64,256]{3,2,1,0:T(8,128)(2,1)} %param.19) | copy-start | bytes 3145732
  0.0 12.9 %copy-start.6 = (f32[8,4]{0,1:T(4,128)S(1)}, f32[8,4]{0,1:T(4,128)}, u32[]{:S(2)}) copy-start(f32[8,4]{0,1:T(4,128)} %param.25) | copy-start | bytes 388
  0.0 13.0 %copy-start.7 = (s32[8,4]{0,1:T(4,128)S(1)}, s32[8,4]{0,1:T(4,128)}, u32[]{:S(2)}) copy-start(s32[8,4]{0,1:T(4,128)} %param.26) | copy-start | bytes 388
  0.0 13.0 %copy-start.8 = (s32[8,4]{0,1:T(4,128)S(1)}, s32[8,4]{0,1:T(4,128)}, u32[]{:S(2)}) copy-start(s32[8,4]{0,1:T(4,128)} %param.24) | copy-start | bytes 388
  0.0 13.2 %copy-start.5 = (f32[2880]{0:T(1024)S(1)}, f32[2880]{0:T(1024)}, u32[]{:S(2)}) copy-start(f32[2880]{0:T(1024)} %param.23) | copy-start | bytes 34564
  0.0 15.0 %copy-start.4 = (bf16[8,2880]{1,0:T(8,128)(2,1)S(1)}, bf16[8,2880]{1,0:T(8,128)(2,1)}, u32[]{:S(2)}) copy-start(bf16[8,2880]{1,0:T(8,128)(2,1)} %hidden_ref.1) | copy-start | bytes 138244
  9.9 5.0 %collective-permute-start = (bf16[8,2880]{1,0:T(8,128)(2,1)S(1)}, bf16[8,2880]{1,0:T(8,128)(2,1)S(1)}, u32[]{:S(2)}, u32[]{:S(2)}) collective-permute-start(bf16[8,2880]{1,0:T(8,128)(2,1)S(1)} %get-tuple-element.31), channel_id=1, source_target_pairs={{0,1},{1,0},{2,3},{3,2},{4,5},{5,4},{6,7},{7,6},{8,9},{9,8},{10,11... | collective-permute-start | bytes 138248 | tf_op jit(solution)/shard_map/ppermute | solution.py:78
  15.1 4.8 %collective-permute-start.1 = (bf16[8,2944]{1,0:T(8,128)(2,1)S(1)}, bf16[8,2944]{1,0:T(8,128)(2,1)S(1)}, u32[]{:S(2)}, u32[]{:S(2)}) collective-permute-start(bf16[8,2944]{1,0:T(8,128)(2,1)S(1)} %get-tuple-element.14.refs_0_), channel_id=1, source_target_pairs={{0,4},{2,6},{4,0},{6,2},{8,12},{10,14},{12,8},{14,10},{1,5},{3,7},... | collective-permute-start | bytes 141320 | tf_op jit(solution)/shard_map/ppermute | solution.py:172
  17.3 6.0 %collective-permute-start.2 = (bf16[8,2944]{1,0:T(8,128)(2,1)S(1)}, bf16[8,2944]{1,0:T(8,128)(2,1)S(1)}, u32[]{:S(2)}, u32[]{:S(2)}) collective-permute-start(bf16[8,2944]{1,0:T(8,128)(2,1)S(1)} %get-tuple-element.14.refs_0_), channel_id=1, source_target_pairs={{0,8},{2,10},{4,12},{6,14},{8,0},{10,2},{12,4},{14,6},{1,9},{3,11}... | collective-permute-start | bytes 141320 | tf_op jit(solution)/shard_map/ppermute | solution.py:172
  19.9 5.9 %collective-permute-start.3 = (bf16[8,2944]{1,0:T(8,128)(2,1)S(1)}, bf16[8,2944]{1,0:T(8,128)(2,1)S(1)}, u32[]{:S(2)}, u32[]{:S(2)}) collective-permute-start(bf16[8,2944]{1,0:T(8,128)(2,1)S(1)} %get-tuple-element.14.refs_0_), channel_id=1, source_target_pairs={{0,12},{2,14},{4,8},{6,10},{8,4},{10,6},{12,0},{14,2},{1,13},{3,15... | collective-permute-start | bytes 141320 | tf_op jit(solution)/shard_map/ppermute | solution.py:172
  19.9 5.9 %collective-permute-start.4 = (bf16[8,2944]{1,0:T(8,128)(2,1)S(1)}, bf16[8,2944]{1,0:T(8,128)(2,1)S(1)}, u32[]{:S(2)}, u32[]{:S(2)}) collective-permute-start(bf16[8,2944]{1,0:T(8,128)(2,1)S(1)} %get-tuple-element.14.refs_0_), channel_id=1, source_target_pairs={{0,2},{2,0},{4,6},{6,4},{8,10},{10,8},{12,14},{14,12},{1,3},{3,1},... | collective-permute-start | bytes 141320 | tf_op jit(solution)/shard_map/ppermute | solution.py:175
  19.9 5.9 %collective-permute-start.5 = (bf16[8,2944]{1,0:T(8,128)(2,1)S(1)}, bf16[8,2944]{1,0:T(8,128)(2,1)S(1)}, u32[]{:S(2)}, u32[]{:S(2)}) collective-permute-start(bf16[8,2944]{1,0:T(8,128)(2,1)S(1)} %collective-permute-done.1.refs_1_), channel_id=1, source_target_pairs={{0,2},{2,0},{4,6},{6,4},{8,10},{10,8},{12,14},{14,12},{1,3},{3,1},... | collective-permute-start | bytes 141320 | tf_op jit(solution)/shard_map/ppermute | solution.py:175
  23.3 2.5 %collective-permute-start.6 = (bf16[8,2944]{1,0:T(8,128)(2,1)S(1)}, bf16[8,2944]{1,0:T(8,128)(2,1)S(1)}, u32[]{:S(2)}, u32[]{:S(2)}) collective-permute-start(bf16[8,2944]{1,0:T(8,128)(2,1)S(1)} %collective-permute-done.2.refs_2_), channel_id=1, source_target_pairs={{0,2},{2,0},{4,6},{6,4},{8,10},{10,8},{12,14},{14,12},{1,3},{3,1},... | collective-permute-start | bytes 141320 | tf_op jit(solution)/shard_map/ppermute | solution.py:175
  25.7 1.2 %collective-permute-start.7 = (bf16[8,2944]{1,0:T(8,128)(2,1)S(1)}, bf16[8,2944]{1,0:T(8,128)(2,1)S(1)}, u32[]{:S(2)}, u32[]{:S(2)}) collective-permute-start(bf16[8,2944]{1,0:T(8,128)(2,1)S(1)} %collective-permute-done.3.refs_3_), channel_id=1, source_target_pairs={{0,2},{2,0},{4,6},{6,4},{8,10},{10,8},{12,14},{14,12},{1,3},{3,1},... | collective-permute-start | bytes 141320 | tf_op jit(solution)/shard_map/ppermute | solution.py:175
  27.0 2.2 %copy-start.1 = (bf16[1,2880,720]{1,2,0:T(8,128)(2,1)S(1)}, bf16[1,2880,720]{1,2,0:T(8,128)(2,1)}, u32[]{:S(2)}) copy-start(bf16[1,2880,720]{1,2,0:T(8,128)(2,1)} %param.27) | copy-start | bytes 12441604
  29.2 2.2 %copy-start.2 = (bf16[1,2880,720]{1,2,0:T(8,128)(2,1)S(1)}, bf16[1,2880,720]{1,2,0:T(8,128)(2,1)}, u32[]{:S(2)}) copy-start(bf16[1,2880,720]{1,2,0:T(8,128)(2,1)} %param.28) | copy-start | bytes 12441604
  31.4 2.2 %copy-start.3 = (bf16[1,720,2880]{2,1,0:T(8,128)(2,1)S(1)}, bf16[1,720,2880]{2,1,0:T(8,128)(2,1)}, u32[]{:S(2)}) copy-start(bf16[1,720,2880]{2,1,0:T(8,128)(2,1)} %refs_10_.1) | copy-start | bytes 12441604
  36.9 1.5 %collective-permute-start.8 = (bf16[32,2880]{1,0:T(8,128)(2,1)S(1)}, bf16[32,2880]{1,0:T(8,128)(2,1)S(1)}, u32[]{:S(2)}, u32[]{:S(2)}) collective-permute-start(bf16[32,2880]{1,0:T(8,128)(2,1)S(1)} %get-tuple-element.16), channel_id=1, source_target_pairs={{0,2},{2,0},{4,6},{6,4},{8,10},{10,8},{12,14},{14,12},{1,3},{3,1},... | collective-permute-start | bytes 552968 | tf_op jit(solution)/shard_map/ppermute | solution.py:175
  38.4 6.2 %collective-permute-start.10 = (bf16[8,2880]{1,0:T(8,128)(2,1)S(1)}, bf16[8,2880]{1,0:T(8,128)(2,1)S(1)}, u32[]{:S(2)}, u32[]{:S(2)}) collective-permute-start(bf16[8,2880]{1,0:T(8,128)(2,1)S(1)} %get-tuple-element.19), channel_id=1, source_target_pairs={{0,8},{2,10},{4,12},{6,14},{8,0},{10,2},{12,4},{14,6},{1,9},{3,11}... | collective-permute-start | bytes 138248 | tf_op jit(solution)/shard_map/ppermute | solution.py:172
  38.5 6.2 %collective-permute-start.11 = (bf16[8,2880]{1,0:T(8,128)(2,1)S(1)}, bf16[8,2880]{1,0:T(8,128)(2,1)S(1)}, u32[]{:S(2)}, u32[]{:S(2)}) collective-permute-start(bf16[8,2880]{1,0:T(8,128)(2,1)S(1)} %get-tuple-element.20), channel_id=1, source_target_pairs={{0,12},{2,14},{4,8},{6,10},{8,4},{10,6},{12,0},{14,2},{1,13},{3,15... | collective-permute-start | bytes 138248 | tf_op jit(solution)/shard_map/ppermute | solution.py:172
  39.5 5.7 %collective-permute-start.9 = (bf16[8,2880]{1,0:T(8,128)(2,1)S(1)}, bf16[8,2880]{1,0:T(8,128)(2,1)S(1)}, u32[]{:S(2)}, u32[]{:S(2)}) collective-permute-start(bf16[8,2880]{1,0:T(8,128)(2,1)S(1)} %get-tuple-element.18), channel_id=1, source_target_pairs={{0,4},{2,6},{4,0},{6,2},{8,12},{10,14},{12,8},{14,10},{1,5},{3,7},... | collective-permute-start | bytes 138248 | tf_op jit(solution)/shard_map/ppermute | solution.py:172
  45.2 4.1 %collective-permute-start.12 = (bf16[8,2880]{1,0:T(8,128)(2,1)S(1)}, bf16[8,2880]{1,0:T(8,128)(2,1)S(1)}, u32[]{:S(2)}, u32[]{:S(2)}) collective-permute-start(bf16[8,2880]{1,0:T(8,128)(2,1)S(1)} %convert_element_type.45), channel_id=1, source_target_pairs={{0,1},{1,0},{2,3},{3,2},{4,5},{5,4},{6,7},{7,6},{8,9},{9,8},{10,11... | collective-permute-start | bytes 138248 | tf_op jit(solution)/shard_map/ppermute | solution.py:78

commit v3 on v2

--- a/solution.py
+++ b/solution.py
@@ -9,7 +9,7 @@
 
 EPSILON = 1e-05
 GLU_SLOPE = 1.702
-WINDOW_FLOPS = 20_000_000_000
+WINDOW_FLOPS = 200_000_000_000
 
 
 def attend(queries, new_keys, new_values, cache_keys, cache_values, cache_lengths):

time: 50.5 us -> 43.8 us (0.87)
  local copies, waits for them, and re-layouts: 6.82 us -> 0.23 us
    unnamed x18, local copies, waits for them, and re-layouts: 6.62 us -> 0.03 us
where the time goes in v3:
time: 43.8 us; the launch traced here: 43.5 us
  waiting for transfers between devices  15.3 us (35%)
  starting transfers between devices  13.6 us (31%)
  matrix products  7.98 us (18%)
  Pallas kernels  3.49 us (8%)
  other arithmetic  2.68 us (6%)
    ppermute x6, waiting for transfers between devices, to_outer(): return lax.ppermute(values, 'expert', pairs)  8.53 us
    ppermute x6, starting transfers between devices, to_outer(): return lax.ppermute(values, 'expert', pairs)  8.31 us
    ppermute x2, starting transfers between devices, exchange(): received = lax.ppermute(values.astype(jnp.bfloat16), axis, pairs)  4.56 us
    dot_general x1, matrix products, per_device(): jnp.dot(attended, out_weight, preferred_element_type=jnp.float32)  4.32 us
    ppermute x2, waiting for transfers between devices, exchange(): received = lax.ppermute(values.astype(jnp.bfloat16), axis, pairs)  4.3 us
    pallas_call x4, Pallas kernels, call(): pl.pallas_call(kernel, out_shape=[jax.ShapeDtypeStruct(shape, dtype) for...  3.49 us
    ppermute x5, waiting for transfers between devices, to_inner(): lax.ppermute(values, 'expert', [(rank, rank ^ 1) for rank in range(expert...  2.49 us
    dot_general x1, matrix products, attend(): jnp.einsum('sgqc,sgdc->sgqd', cache_prob, cache_values, preferred_element...  1.66 us
  transfers between devices with their start and end apart: 13, of which 8 were waited for; matrix products, arithmetic and copies ran while one was open for 1% of the time, Pallas kernels for 0%

profile of v3, /device:TPU:0, one launch (start us, length us, event | category | flops | bytes accessed | tf_op | source)
XLA Modules:
  0.0 43.5 jit_solution(5385147419526697349)
XLA Ops:
  0.0 0.0 copy-start
  0.0 0.0 copy-start.6
  0.0 0.0 copy-start.7
  0.0 0.0 copy-start.8
  0.0 0.0 copy-start.5
  0.0 0.0 copy-start.4
  0.0 0.8 %iota_compare_fusion.1 = pred[8,256]{1,0:T(8,128)(4,1)S(1)} fusion(s32[8]{0:T(128)} %param.21), kind=kLoop, calls=%fused_computation.19 | loop fusion | flops 2048 | bytes 2080 | tf_op jit(solution)/shard_map/lt | solution.py:30
  0.8 0.9 %fusion.7 = f32[8,4,1,4]{3,2,1,0:T(1,128)S(1)} fusion(bf16[8,4,4,64]{3,2,1,0:T(4,128)(2,1)} %bitcast.24, bf16[8,4,64,1]{2,1,0,3:T(4,128)(2,1)} %bitcast.26), kind=kOutput, calls=%fused_computation.16 | convolution fusion | flops 16384 | bytes 20992 | tf_op jit(solution)/shard_map/sgqd,sgd->sgq/dot_general | solution.py:26
  1.8 0.0 copy-done
  1.8 1.1 %fusion.11 = (f32[8,4,4]{2,1,0:T(4,128)S(1)}, f32[8,4,4,256]{3,2,1,0:T(4,128)S(1)}) fusion(bf16[8,4,4,64]{3,2,1,0:T(4,128)(2,1)} %bitcast.25, bf16[8,4,64,256]{3,2,1,0:T(8,128)(2,1)S(1)} %copy-done, pred[8,256]{1,0:T(8,128)(4,1)S(1)} %iota_compare_fusion.1), kind=kOutput, calls=%fused_computation.29 | convolution fusion | flops 4292480 | bytes 1198592 | tf_op jit(solution)/shard_map/sgqd,sgdc->sgqc/dot_general | solution.py:22
  2.9 0.2 fusion.2
  3.1 0.7 %convert_element_type.39 = f32[8,4,64]{2,1,0:T(4,128)S(1)} convert(bf16[8,4,64]{2,1,0:T(4,128)(2,1)} %param.18) | non-fusion elementwise | flops 2048 | bytes 12288 | tf_op jit(solution)/shard_map/convert_element_type | solution.py:43
  3.8 1.7 %fusion.1 = bf16[8,4,4,64]{3,2,1,0:T(4,128)(2,1)S(1)} fusion(bf16[8,4,64,256]{3,2,1,0:T(8,128)(2,1)} %param.20, f32[8,4,4,256]{3,2,1,0:T(4,128)S(1)} %get-tuple-element.30, f32[8,4,4]{2,1,0:T(4,128)S(1)} %get-tuple-element.24, f32[8,4,4]{2,1,0:T(4,128)S(1)} %multiply_maximum_fusion, f32[8,4,64]{2,1,0:T(4,128)S(1)} %convert_element_type.39, ...), kind=kOutput, calls=%fused_computation.3 | convolution fusion | flops 4317184 | bytes 1205760 | tf_op jit(solution)/shard_map/sgqc,sgdc->sgqd/dot_general | solution.py:38
  5.5 0.1 reshape.34
  5.6 4.3 %fusion.12 = (bf16[8,2880]{1,0:T(8,128)(2,1)S(1)}, f32[8,2880]{1,0:T(8,128)S(1)}) fusion(bf16[8,1024]{1,0:T(8,128)(2,1)S(1)} %reshape.34, bf16[1024,2880]{0,1:T(8,128)(2,1)} %param.22), kind=kOutput, calls=%fused_computation.30 | convolution fusion | flops 47208960 | bytes 6052864 | tf_op jit(solution)/shard_map/dot_general | solution.py:178
  9.9 3.0 %collective-permute-start = (bf16[8,2880]{1,0:T(8,128)(2,1)S(1)}, bf16[8,2880]{1,0:T(8,128)(2,1)S(1)}, u32[]{:S(2)}, u32[]{:S(2)}) collective-permute-start(bf16[8,2880]{1,0:T(8,128)(2,1)S(1)} %get-tuple-element.31), channel_id=1, source_target_pairs={{0,1},{1,0},{2,3},{3,2},{4,5},{5,4},{6,7},{7,6},{8,9},{9,8},{10,11... | collective-permute-start | bytes 138248 | tf_op jit(solution)/shard_map/ppermute | solution.py:78
  12.9 0.0 copy-done.6
  13.0 0.0 copy-done.7
  13.0 0.0 copy-done.8
  13.0 0.1 select_reduce_fusion
  13.1 0.1 pad.2.clone
  13.2 0.1 maximum_maximum_fusion.table_ref
  13.2 0.0 copy-done.5
  13.3 1.7 %collective-permute-done.received_ref = bf16[8,2880]{1,0:T(8,128)(2,1)S(1)} collective-permute-done((bf16[8,2880]{1,0:T(8,128)(2,1)S(1)}, bf16[8,2880]{1,0:T(8,128)(2,1)S(1)}, u32[]{:S(2)}, u32[]{:S(2)}) %collective-permute-start) | collective-permute-done | bytes 46112 | tf_op jit(solution)/shard_map/ppermute | solution.py:78
  15.0 0.0 copy-done.4
  15.0 0.0 copy-start.1
  15.0 0.0 copy-start.2
  15.0 0.0 copy-start.3
  15.0 0.1 shard_map.145
  15.1 2.2 %collective-permute-start.1 = (bf16[8,2944]{1,0:T(8,128)(2,1)S(1)}, bf16[8,2944]{1,0:T(8,128)(2,1)S(1)}, u32[]{:S(2)}, u32[]{:S(2)}) collective-permute-start(bf16[8,2944]{1,0:T(8,128)(2,1)S(1)} %get-tuple-element.14.refs_0_), channel_id=1, source_target_pairs={{0,4},{2,6},{4,0},{6,2},{8,12},{10,14},{12,8},{14,10},{1,5},{3,7},... | collective-permute-start | bytes 141320 | tf_op jit(solution)/shard_map/ppermute | solution.py:172
  17.3 2.6 %collective-permute-start.2 = (bf16[8,2944]{1,0:T(8,128)(2,1)S(1)}, bf16[8,2944]{1,0:T(8,128)(2,1)S(1)}, u32[]{:S(2)}, u32[]{:S(2)}) collective-permute-start(bf16[8,2944]{1,0:T(8,128)(2,1)S(1)} %get-tuple-element.14.refs_0_), channel_id=1, source_target_pairs={{0,8},{2,10},{4,12},{6,14},{8,0},{10,2},{12,4},{14,6},{1,9},{3,11}... | collective-permute-start | bytes 141320 | tf_op jit(solution)/shard_map/ppermute | solution.py:172
  19.9 0.0 collective-permute-start.3
  19.9 0.0 collective-permute-start.4
  19.9 0.0 collective-permute-done.1.refs_1_
  19.9 0.5 %collective-permute-start.5 = (bf16[8,2944]{1,0:T(8,128)(2,1)S(1)}, bf16[8,2944]{1,0:T(8,128)(2,1)S(1)}, u32[]{:S(2)}, u32[]{:S(2)}) collective-permute-start(bf16[8,2944]{1,0:T(8,128)(2,1)S(1)} %collective-permute-done.1.refs_1_), channel_id=1, source_target_pairs={{0,2},{2,0},{4,6},{6,4},{8,10},{10,8},{12,14},{14,12},{1,3},{3,1},... | collective-permute-start | bytes 141320 | tf_op jit(solution)/shard_map/ppermute | solution.py:175
  20.4 2.9 %collective-permute-done.2.refs_2_ = bf16[8,2944]{1,0:T(8,128)(2,1)S(1)} collective-permute-done((bf16[8,2944]{1,0:T(8,128)(2,1)S(1)}, bf16[8,2944]{1,0:T(8,128)(2,1)S(1)}, u32[]{:S(2)}, u32[]{:S(2)}) %collective-permute-start.2) | collective-permute-done | bytes 47136 | tf_op jit(solution)/shard_map/ppermute | solution.py:172
  23.3 0.0 collective-permute-start.6
  23.3 2.5 %collective-permute-done.3.refs_3_ = bf16[8,2944]{1,0:T(8,128)(2,1)S(1)} collective-permute-done((bf16[8,2944]{1,0:T(8,128)(2,1)S(1)}, bf16[8,2944]{1,0:T(8,128)(2,1)S(1)}, u32[]{:S(2)}, u32[]{:S(2)}) %collective-permute-start.3) | collective-permute-done | bytes 47136 | tf_op jit(solution)/shard_map/ppermute | solution.py:172
  25.7 0.0 collective-permute-start.7
  25.8 0.0 collective-permute-done.4.refs_4_
  25.8 0.0 collective-permute-done.5.refs_5_
  25.8 0.0 collective-permute-done.6.refs_6_
  25.8 1.2 %collective-permute-done.7.refs_7_ = bf16[8,2944]{1,0:T(8,128)(2,1)S(1)} collective-permute-done((bf16[8,2944]{1,0:T(8,128)(2,1)S(1)}, bf16[8,2944]{1,0:T(8,128)(2,1)S(1)}, u32[]{:S(2)}, u32[]{:S(2)}) %collective-permute-start.7) | collective-permute-done | bytes 47136 | tf_op jit(solution)/shard_map/ppermute | solution.py:175
  27.0 0.0 copy-done.1
  27.0 0.0 copy-done.2
  27.0 0.0 copy-done.3
  27.0 3.3 %shard_map.146 = (f32[32,2880]{1,0:T(8,128)S(1)}, bf16[32,2880]{1,0:T(8,128)(2,1)S(1)}) custom-call(bf16[8,2944]{1,0:T(8,128)(2,1)S(1)} %get-tuple-element.14.refs_0_, bf16[8,2944]{1,0:T(8,128)(2,1)S(1)} %collective-permute-done.1.refs_1_, bf16[8,2944]{1,0:T(8,128)(2,1)S(1)} %collective-permute-done.2.refs_2_, ...), custom_call_target="tpu_custom_call" | custom-call | flops 796262400 | bytes 12441600 | tf_op jit(solution)/shard_map/pallas_call | solution.py:55
  30.3 0.2 collective-permute-start.8
  30.5 1.3 %collective-permute-done.8.received_ref = bf16[32,2880]{1,0:T(8,128)(2,1)S(1)} collective-permute-done((bf16[32,2880]{1,0:T(8,128)(2,1)S(1)}, bf16[32,2880]{1,0:T(8,128)(2,1)S(1)}, u32[]{:S(2)}, u32[]{:S(2)}) %collective-permute-start.8) | collective-permute-done | bytes 184352 | tf_op jit(solution)/shard_map/ppermute | solution.py:175
  31.8 0.1 collective-permute-start.10
  31.9 1.0 %collective-permute-start.11 = (bf16[8,2880]{1,0:T(8,128)(2,1)S(1)}, bf16[8,2880]{1,0:T(8,128)(2,1)S(1)}, u32[]{:S(2)}, u32[]{:S(2)}) collective-permute-start(bf16[8,2880]{1,0:T(8,128)(2,1)S(1)} %get-tuple-element.20), channel_id=1, source_target_pairs={{0,12},{2,14},{4,8},{6,10},{8,4},{10,6},{12,0},{14,2},{1,13},{3,15... | collective-permute-start | bytes 138248 | tf_op jit(solution)/shard_map/ppermute | solution.py:172
  32.9 2.5 %collective-permute-start.9 = (bf16[8,2880]{1,0:T(8,128)(2,1)S(1)}, bf16[8,2880]{1,0:T(8,128)(2,1)S(1)}, u32[]{:S(2)}, u32[]{:S(2)}) collective-permute-start(bf16[8,2880]{1,0:T(8,128)(2,1)S(1)} %get-tuple-element.18), channel_id=1, source_target_pairs={{0,4},{2,6},{4,0},{6,2},{8,12},{10,14},{12,8},{14,10},{1,5},{3,7},... | collective-permute-start | bytes 138248 | tf_op jit(solution)/shard_map/ppermute | solution.py:172
  35.4 2.7 %collective-permute-done.10.refs_1_ = bf16[8,2880]{1,0:T(8,128)(2,1)S(1)} collective-permute-done((bf16[8,2880]{1,0:T(8,128)(2,1)S(1)}, bf16[8,2880]{1,0:T(8,128)(2,1)S(1)}, u32[]{:S(2)}, u32[]{:S(2)}) %collective-permute-start.10) | collective-permute-done | bytes 46112 | tf_op jit(solution)/shard_map/ppermute | solution.py:172
  38.1 0.0 collective-permute-done.11.refs_2_
  38.1 0.5 %collective-permute-done.9.refs_0_ = bf16[8,2880]{1,0:T(8,128)(2,1)S(1)} collective-permute-done((bf16[8,2880]{1,0:T(8,128)(2,1)S(1)}, bf16[8,2880]{1,0:T(8,128)(2,1)S(1)}, u32[]{:S(2)}, u32[]{:S(2)}) %collective-permute-start.9) | collective-permute-done | bytes 46112 | tf_op jit(solution)/shard_map/ppermute | solution.py:172
  38.6 1.6 %collective-permute-start.12 = (bf16[8,2880]{1,0:T(8,128)(2,1)S(1)}, bf16[8,2880]{1,0:T(8,128)(2,1)S(1)}, u32[]{:S(2)}, u32[]{:S(2)}) collective-permute-start(bf16[8,2880]{1,0:T(8,128)(2,1)S(1)} %convert_element_type.45), channel_id=1, source_target_pairs={{0,1},{1,0},{2,3},{3,2},{4,5},{5,4},{6,7},{7,6},{8,9},{9,8},{10,11... | collective-permute-start | bytes 138248 | tf_op jit(solution)/shard_map/ppermute | solution.py:78
  40.2 2.6 %collective-permute-done.12 = bf16[8,2880]{1,0:T(8,128)(2,1)S(1)} collective-permute-done((bf16[8,2880]{1,0:T(8,128)(2,1)S(1)}, bf16[8,2880]{1,0:T(8,128)(2,1)S(1)}, u32[]{:S(2)}, u32[]{:S(2)}) %collective-permute-start.12) | collective-permute-done | bytes 46112 | tf_op jit(solution)/shard_map/ppermute | solution.py:78
  42.8 0.7 %fusion.6 = bf16[8,1440]{1,0:T(8,128)(2,1)} fusion(f32[8,2880]{1,0:T(8,128)S(1)} %shard_map.148, s32[]{:T(128)S(6)} %select_n.30, f32[8,2880]{1,0:T(8,128)S(1)} %get-tuple-element.13, bf16[8,2880]{1,0:T(8,128)(2,1)S(1)} %collective-permute-done.12), kind=kLoop, calls=%fused_computation.11 | loop fusion | flops 46080 | bytes 138244 | tf_op jit(solution)/shard_map/convert_element_type | solution.py:228
  (11 shorter events, 0.2 us)
Async XLA Ops:
  0.0 1.8 %copy-start = (bf16[8,4,64,256]{3,2,1,0:T(8,128)(2,1)S(1)}, bf16[8,4,64,256]{3,2,1,0:T(8,128)(2,1)}, u32[]{:S(2)}) copy-start(bf16[8,4,64,256]{3,2,1,0:T(8,128)(2,1)} %param.19) | copy-start | bytes 3145732
  0.0 12.9 %copy-start.6 = (f32[8,4]{0,1:T(4,128)S(1)}, f32[8,4]{0,1:T(4,128)}, u32[]{:S(2)}) copy-start(f32[8,4]{0,1:T(4,128)} %param.25) | copy-start | bytes 388
  0.0 13.0 %copy-start.7 = (s32[8,4]{0,1:T(4,128)S(1)}, s32[8,4]{0,1:T(4,128)}, u32[]{:S(2)}) copy-start(s32[8,4]{0,1:T(4,128)} %param.26) | copy-start | bytes 388
  0.0 13.0 %copy-start.8 = (s32[8,4]{0,1:T(4,128)S(1)}, s32[8,4]{0,1:T(4,128)}, u32[]{:S(2)}) copy-start(s32[8,4]{0,1:T(4,128)} %param.24) | copy-start | bytes 388
  0.0 13.2 %copy-start.5 = (f32[2880]{0:T(1024)S(1)}, f32[2880]{0:T(1024)}, u32[]{:S(2)}) copy-start(f32[2880]{0:T(1024)} %param.23) | copy-start | bytes 34564
  0.0 15.0 %copy-start.4 = (bf16[8,2880]{1,0:T(8,128)(2,1)S(1)}, bf16[8,2880]{1,0:T(8,128)(2,1)}, u32[]{:S(2)}) copy-start(bf16[8,2880]{1,0:T(8,128)(2,1)} %hidden_ref.1) | copy-start | bytes 138244
  9.9 5.0 %collective-permute-start = (bf16[8,2880]{1,0:T(8,128)(2,1)S(1)}, bf16[8,2880]{1,0:T(8,128)(2,1)S(1)}, u32[]{:S(2)}, u32[]{:S(2)}) collective-permute-start(bf16[8,2880]{1,0:T(8,128)(2,1)S(1)} %get-tuple-element.31), channel_id=1, source_target_pairs={{0,1},{1,0},{2,3},{3,2},{4,5},{5,4},{6,7},{7,6},{8,9},{9,8},{10,11... | collective-permute-start | bytes 138248 | tf_op jit(solution)/shard_map/ppermute | solution.py:78
  15.0 12.0 %copy-start.1 = (bf16[1,2880,720]{1,2,0:T(8,128)(2,1)S(1)}, bf16[1,2880,720]{1,2,0:T(8,128)(2,1)}, u32[]{:S(2)}) copy-start(bf16[1,2880,720]{1,2,0:T(8,128)(2,1)} %param.27) | copy-start | bytes 12441604
  15.0 12.0 %copy-start.2 = (bf16[1,2880,720]{1,2,0:T(8,128)(2,1)S(1)}, bf16[1,2880,720]{1,2,0:T(8,128)(2,1)}, u32[]{:S(2)}) copy-start(bf16[1,2880,720]{1,2,0:T(8,128)(2,1)} %param.28) | copy-start | bytes 12441604
  15.0 12.0 %copy-start.3 = (bf16[1,720,2880]{2,1,0:T(8,128)(2,1)S(1)}, bf16[1,720,2880]{2,1,0:T(8,128)(2,1)}, u32[]{:S(2)}) copy-start(bf16[1,720,2880]{2,1,0:T(8,128)(2,1)} %refs_10_.1) | copy-start | bytes 12441604
  15.1 4.8 %collective-permute-start.1 = (bf16[8,2944]{1,0:T(8,128)(2,1)S(1)}, bf16[8,2944]{1,0:T(8,128)(2,1)S(1)}, u32[]{:S(2)}, u32[]{:S(2)}) collective-permute-start(bf16[8,2944]{1,0:T(8,128)(2,1)S(1)} %get-tuple-element.14.refs_0_), channel_id=1, source_target_pairs={{0,4},{2,6},{4,0},{6,2},{8,12},{10,14},{12,8},{14,10},{1,5},{3,7},... | collective-permute-start | bytes 141320 | tf_op jit(solution)/shard_map/ppermute | solution.py:172
  17.3 6.0 %collective-permute-start.2 = (bf16[8,2944]{1,0:T(8,128)(2,1)S(1)}, bf16[8,2944]{1,0:T(8,128)(2,1)S(1)}, u32[]{:S(2)}, u32[]{:S(2)}) collective-permute-start(bf16[8,2944]{1,0:T(8,128)(2,1)S(1)} %get-tuple-element.14.refs_0_), channel_id=1, source_target_pairs={{0,8},{2,10},{4,12},{6,14},{8,0},{10,2},{12,4},{14,6},{1,9},{3,11}... | collective-permute-start | bytes 141320 | tf_op jit(solution)/shard_map/ppermute | solution.py:172
  19.9 5.9 %collective-permute-start.3 = (bf16[8,2944]{1,0:T(8,128)(2,1)S(1)}, bf16[8,2944]{1,0:T(8,128)(2,1)S(1)}, u32[]{:S(2)}, u32[]{:S(2)}) collective-permute-start(bf16[8,2944]{1,0:T(8,128)(2,1)S(1)} %get-tuple-element.14.refs_0_), channel_id=1, source_target_pairs={{0,12},{2,14},{4,8},{6,10},{8,4},{10,6},{12,0},{14,2},{1,13},{3,15... | collective-permute-start | bytes 141320 | tf_op jit(solution)/shard_map/ppermute | solution.py:172
  19.9 5.9 %collective-permute-start.4 = (bf16[8,2944]{1,0:T(8,128)(2,1)S(1)}, bf16[8,2944]{1,0:T(8,128)(2,1)S(1)}, u32[]{:S(2)}, u32[]{:S(2)}) collective-permute-start(bf16[8,2944]{1,0:T(8,128)(2,1)S(1)} %get-tuple-element.14.refs_0_), channel_id=1, source_target_pairs={{0,2},{2,0},{4,6},{6,4},{8,10},{10,8},{12,14},{14,12},{1,3},{3,1},... | collective-permute-start | bytes 141320 | tf_op jit(solution)/shard_map/ppermute | solution.py:175
  19.9 5.9 %collective-permute-start.5 = (bf16[8,2944]{1,0:T(8,128)(2,1)S(1)}, bf16[8,2944]{1,0:T(8,128)(2,1)S(1)}, u32[]{:S(2)}, u32[]{:S(2)}) collective-permute-start(bf16[8,2944]{1,0:T(8,128)(2,1)S(1)} %collective-permute-done.1.refs_1_), channel_id=1, source_target_pairs={{0,2},{2,0},{4,6},{6,4},{8,10},{10,8},{12,14},{14,12},{1,3},{3,1},... | collective-permute-start | bytes 141320 | tf_op jit(solution)/shard_map/ppermute | solution.py:175
  23.3 2.5 %collective-permute-start.6 = (bf16[8,2944]{1,0:T(8,128)(2,1)S(1)}, bf16[8,2944]{1,0:T(8,128)(2,1)S(1)}, u32[]{:S(2)}, u32[]{:S(2)}) collective-permute-start(bf16[8,2944]{1,0:T(8,128)(2,1)S(1)} %collective-permute-done.2.refs_2_), channel_id=1, source_target_pairs={{0,2},{2,0},{4,6},{6,4},{8,10},{10,8},{12,14},{14,12},{1,3},{3,1},... | collective-permute-start | bytes 141320 | tf_op jit(solution)/shard_map/ppermute | solution.py:175
  25.7 1.2 %collective-permute-start.7 = (bf16[8,2944]{1,0:T(8,128)(2,1)S(1)}, bf16[8,2944]{1,0:T(8,128)(2,1)S(1)}, u32[]{:S(2)}, u32[]{:S(2)}) collective-permute-start(bf16[8,2944]{1,0:T(8,128)(2,1)S(1)} %collective-permute-done.3.refs_3_), channel_id=1, source_target_pairs={{0,2},{2,0},{4,6},{6,4},{8,10},{10,8},{12,14},{14,12},{1,3},{3,1},... | collective-permute-start | bytes 141320 | tf_op jit(solution)/shard_map/ppermute | solution.py:175
  30.3 1.5 %collective-permute-start.8 = (bf16[32,2880]{1,0:T(8,128)(2,1)S(1)}, bf16[32,2880]{1,0:T(8,128)(2,1)S(1)}, u32[]{:S(2)}, u32[]{:S(2)}) collective-permute-start(bf16[32,2880]{1,0:T(8,128)(2,1)S(1)} %get-tuple-element.16), channel_id=1, source_target_pairs={{0,2},{2,0},{4,6},{6,4},{8,10},{10,8},{12,14},{14,12},{1,3},{3,1},... | collective-permute-start | bytes 552968 | tf_op jit(solution)/shard_map/ppermute | solution.py:175
  31.8 6.2 %collective-permute-start.10 = (bf16[8,2880]{1,0:T(8,128)(2,1)S(1)}, bf16[8,2880]{1,0:T(8,128)(2,1)S(1)}, u32[]{:S(2)}, u32[]{:S(2)}) collective-permute-start(bf16[8,2880]{1,0:T(8,128)(2,1)S(1)} %get-tuple-element.19), channel_id=1, source_target_pairs={{0,8},{2,10},{4,12},{6,14},{8,0},{10,2},{12,4},{14,6},{1,9},{3,11}... | collective-permute-start | bytes 138248 | tf_op jit(solution)/shard_map/ppermute | solution.py:172
  31.9 6.2 %collective-permute-start.11 = (bf16[8,2880]{1,0:T(8,128)(2,1)S(1)}, bf16[8,2880]{1,0:T(8,128)(2,1)S(1)}, u32[]{:S(2)}, u32[]{:S(2)}) collective-permute-start(bf16[8,2880]{1,0:T(8,128)(2,1)S(1)} %get-tuple-element.20), channel_id=1, source_target_pairs={{0,12},{2,14},{4,8},{6,10},{8,4},{10,6},{12,0},{14,2},{1,13},{3,15... | collective-permute-start | bytes 138248 | tf_op jit(solution)/shard_map/ppermute | solution.py:172
  32.9 5.7 %collective-permute-start.9 = (bf16[8,2880]{1,0:T(8,128)(2,1)S(1)}, bf16[8,2880]{1,0:T(8,128)(2,1)S(1)}, u32[]{:S(2)}, u32[]{:S(2)}) collective-permute-start(bf16[8,2880]{1,0:T(8,128)(2,1)S(1)} %get-tuple-element.18), channel_id=1, source_target_pairs={{0,4},{2,6},{4,0},{6,2},{8,12},{10,14},{12,8},{14,10},{1,5},{3,7},... | collective-permute-start | bytes 138248 | tf_op jit(solution)/shard_map/ppermute | solution.py:172
  38.6 4.1 %collective-permute-start.12 = (bf16[8,2880]{1,0:T(8,128)(2,1)S(1)}, bf16[8,2880]{1,0:T(8,128)(2,1)S(1)}, u32[]{:S(2)}, u32[]{:S(2)}) collective-permute-start(bf16[8,2880]{1,0:T(8,128)(2,1)S(1)} %convert_element_type.45), channel_id=1, source_target_pairs={{0,1},{1,0},{2,3},{3,2},{4,5},{5,4},{6,7},{7,6},{8,9},{9,8},{10,11... | collective-permute-start | bytes 138248 | tf_op jit(solution)/shard_map/ppermute | solution.py:78

commit v4 on v3

--- a/solution.py
+++ b/solution.py
@@ -62,6 +62,161 @@
     )(*args)
 
 
+def mm(left, right, dims=(((1,), (0,)), ((), ()))):
+    return lax.dot_general(left, right, dims, preferred_element_type=jnp.float32)
+
+
+def iota(shape, dim):
+    return lax.broadcasted_iota(jnp.int32, shape, dim)
+
+
+def attend_kernel(
+    lengths_ref,
+    queries_ref,
+    new_keys_ref,
+    new_values_ref,
+    keys_hbm,
+    values_hbm,
+    weight_hbm,
+    mine_ref,
+    sent_ref,
+    keys_ref,
+    values_ref,
+    weight_ref,
+    own_keys_ref,
+    own_values_ref,
+    attended_ref,
+    arrived,
+):
+    sequences, heads, head_dim = queries_ref.shape
+    kv_heads = new_keys_ref.shape[1]
+    group = heads // kv_heads
+    span = kv_heads * head_dim
+    lanes = group * head_dim
+    copies = [
+        pltpu.make_async_copy(keys_hbm, keys_ref, arrived.at[0]),
+        pltpu.make_async_copy(values_hbm, values_ref, arrived.at[1]),
+        pltpu.make_async_copy(weight_hbm, weight_ref, arrived.at[2]),
+    ]
+    for copy in copies:
+        copy.start()
+
+    rows = sequences * heads
+    scaling = 1.0 / head_dim**0.5
+    queries = queries_ref[...].reshape(rows, head_dim)
+    for sequence in range(sequences):
+        block = pl.ds(sequence * kv_heads, kv_heads)
+        own_keys_ref[block] = new_keys_ref[sequence].astype(jnp.float32)
+        own_values_ref[block] = new_values_ref[sequence].astype(jnp.float32)
+    own_keys = own_keys_ref[...].astype(jnp.bfloat16)
+    own_values = own_values_ref[...].astype(jnp.bfloat16)
+
+    spread = (iota((head_dim, span), 0) == iota((head_dim, span), 1) % head_dim).astype(
+        jnp.bfloat16
+    )
+    same_head = iota((rows, span), 1) // head_dim == iota((rows, span), 0) % heads // group
+    wide = jnp.where(same_head, mm(queries, spread), 0.0).astype(jnp.bfloat16)
+    pairs = (rows, sequences * kv_heads)
+    own_pair = iota(pairs, 1) == iota(pairs, 0) // group
+    own_score = (
+        jnp.sum(jnp.where(own_pair, mm(queries, own_keys, LAST_DIMS), 0.0), axis=1, keepdims=True)
+        * scaling
+    )
+
+    copies[0].wait()
+    slots = keys_ref.shape[2]
+    scores = []
+    for sequence in range(sequences):
+        block = slice(sequence * heads, (sequence + 1) * heads)
+        score = mm(wide[block], keys_ref[sequence]) * scaling
+        visible = iota((heads, slots), 1) < lengths_ref[sequence]
+        scores.append(jnp.where(visible, score, -1e30))
+    scores = jnp.concatenate(scores, axis=0)
+    highest = jnp.maximum(jnp.max(scores, axis=1, keepdims=True), own_score)
+    cache_exp = jnp.exp(scores - highest)
+    own_exp = jnp.exp(own_score - highest)
+    totals = jnp.sum(cache_exp, axis=1, keepdims=True) + own_exp
+    cache_prob = (cache_exp / totals).astype(jnp.bfloat16)
+    own_prob = own_exp / totals
+    own_prob = jnp.where(own_pair, own_prob, 0.0).astype(jnp.bfloat16)
+    own_part = mm(own_prob, mm(own_values, spread).astype(jnp.bfloat16))
+
+    copies[1].wait()
+    attended = [
+        mm(
+            cache_prob[sequence * heads : (sequence + 1) * heads],
+            values_ref[sequence],
+            LAST_DIMS,
+        )
+        for sequence in range(sequences)
+    ]
+    attended = jnp.concatenate(attended, axis=0) + own_part
+    attended = jnp.where(same_head, attended, 0.0).astype(jnp.bfloat16)
+    repeat = (iota((span, lanes), 0) % head_dim == iota((span, lanes), 1) % head_dim).astype(
+        jnp.bfloat16
+    )
+    own_lanes = iota((rows, lanes), 1) // head_dim == iota((rows, lanes), 0) % group
+    placed = jnp.where(own_lanes, mm(attended, repeat), 0.0).astype(jnp.bfloat16)
+    sums = (kv_heads * sequences, rows)
+    chosen = (iota(sums, 0) % sequences == iota(sums, 1) // heads) & (
+        iota(sums, 0) // sequences == iota(sums, 1) % heads // group
+    )
+    by_head = mm(chosen.astype(jnp.bfloat16), placed)
+    for head in range(kv_heads):
+        attended_ref[:, head * lanes : (head + 1) * lanes] = by_head[
+            head * sequences : (head + 1) * sequences
+        ].astype(jnp.bfloat16)
+    attended = attended_ref[...]
+
+    copies[2].wait()
+    part = mm(weight_ref[...], attended, LAST_DIMS).T
+    mine_ref[...] = part
+    sent_ref[...] = part.astype(jnp.bfloat16)
+
+
+def attend_and_project(
+    queries, new_keys, new_values, cache_keys, cache_values, cache_lengths, out_weight
+):
+    sequences, heads, head_dim = queries.shape
+    kv_heads, slots = cache_keys.shape[1], cache_keys.shape[3]
+    depth, width = out_weight.shape
+    span = kv_heads * head_dim
+    caches = (sequences, span, slots)
+    hbm = pl.BlockSpec(memory_space=pltpu.HBM)
+    return pl.pallas_call(
+        attend_kernel,
+        out_shape=[
+            jax.ShapeDtypeStruct((sequences, width), jnp.float32),
+            jax.ShapeDtypeStruct((sequences, width), jnp.bfloat16),
+        ],
+        in_specs=[pl.BlockSpec(memory_space=pltpu.SMEM)] + [VMEM] * 3 + [hbm] * 3,
+        out_specs=[VMEM] * 2,
+        scratch_shapes=[
+            pltpu.VMEM(caches, jnp.bfloat16),
+            pltpu.VMEM(caches, jnp.bfloat16),
+            pltpu.VMEM((width, depth), jnp.bfloat16),
+            pltpu.VMEM((sequences * kv_heads, head_dim), jnp.float32),
+            pltpu.VMEM((sequences * kv_heads, head_dim), jnp.float32),
+            pltpu.VMEM((sequences, depth), jnp.bfloat16),
+            pltpu.SemaphoreType.DMA((3,)),
+        ],
+        compiler_params=pltpu.CompilerParams(vmem_limit_bytes=60 * MIB),
+        cost_estimate=pl.CostEstimate(
+            flops=2 * sequences * width * depth,
+            bytes_accessed=2 * (width * depth + 2 * sequences * span * slots),
+            transcendentals=sequences * heads * slots,
+        ),
+    )(
+        cache_lengths,
+        queries,
+        new_keys,
+        new_values,
+        cache_keys.reshape(caches),
+        cache_values.reshape(caches),
+        out_weight.T,
+    )
+
+
 def route_weights(expert_ids, route_probs, route_order, experts):
     picked = jnp.zeros(expert_ids.shape, jnp.float32)
     for column in range(expert_ids.shape[1]):
@@ -71,15 +226,16 @@
     return jnp.sum(jnp.where(named, weights[:, :, None], 0.0), axis=1)
 
 
-def exchange(values, axis, ranks):
+def exchange(values, sent, axis, ranks):
     step = 1
     while True:
         pairs = [(rank, rank ^ step) for rank in range(ranks)]
-        received = lax.ppermute(values.astype(jnp.bfloat16), axis, pairs)
+        received = lax.ppermute(sent, axis, pairs)
         step *= 2
         if step >= ranks:
             return values, received
         values = values + received.astype(jnp.float32)
+        sent = values.astype(jnp.bfloat16)
 
 
 def norm_kernel(mine_ref, received_ref, hidden_ref, gain_ref, table_ref, residual_ref, rows_ref):
@@ -174,9 +330,13 @@
     def to_inner(values):
         return lax.ppermute(values, "expert", [(rank, rank ^ 1) for rank in range(expert_ranks)])
 
-    attended = attend(queries, new_keys, new_values, cache_keys, cache_values, cache_lengths)
-    partial_sums = jnp.dot(attended, out_weight, preferred_element_type=jnp.float32)
-    mine, received = exchange(partial_sums, "tensor", tensor_ranks)
+    operands = (queries, new_keys, new_values, cache_keys, cache_values, cache_lengths)
+    if queries.shape[1] % 16 == 0:
+        mine, sent = attend_and_project(*operands, out_weight)
+    else:
+        mine = jnp.dot(attend(*operands), out_weight, preferred_element_type=jnp.float32)
+        sent = mine.astype(jnp.bfloat16)
+    mine, received = exchange(mine, sent, "tensor", tensor_ranks)
 
     weights = route_weights(expert_ids, route_probs, route_order, experts)
     high = weights.astype(jnp.bfloat16)
@@ -223,7 +383,7 @@
         moved=half[0] * width * 2,
         limit=2 * MIB,
     )
-    mine, received = exchange(mixture, "tensor", tensor_ranks)
+    mine, received = exchange(mixture, mixture.astype(jnp.bfloat16), "tensor", tensor_ranks)
     total = residual + mine + received.astype(jnp.float32)
     return lax.dynamic_slice_in_dim(total, offset, slab_width, 1).astype(jnp.bfloat16)
 

time: 43.8 us -> 41.7 us (0.952)
  matrix products: 7.98 us -> 0 us
  Pallas kernels: 3.49 us -> 10.3 us
  other arithmetic: 2.68 us -> 0.91 us
  local copies, waits for them, and re-layouts: 0.23 us -> 1.01 us
    dot_general x4 -> x0, matrix products: 7.98 us -> none  [the longest x1 4.32 us: per_device(): jnp.dot(attended, out_weight, preferred_element_type=jnp.float32)]
    pallas_call x0 -> x1, Pallas kernels: none -> 6.83 us  [attend_and_project(): pl.pallas_call(attend_kernel, out_shape=[jax.ShapeDtypeStruct((sequences,...]
    unnamed x18, local copies, waits for them, and re-layouts: 0.03 us -> 0.92 us
    lt x1 -> x0, other arithmetic: 0.81 us -> none  [attend(): visible = positions[None, :] < cache_lengths[:, None]]
    convert_element_type x3 -> x1, other arithmetic: 0.74 us -> 0.01 us  [per_device(): mixture.astype(jnp.bfloat16)]
where the time goes in v4:
time: 41.7 us; the launch traced here: 41.5 us
  waiting for transfers between devices  15.5 us (37%)
  starting transfers between devices  13.6 us (33%)
  Pallas kernels  10.3 us (25%)
  local copies, waits for them, and re-layouts  1.01 us (2%)
  other arithmetic  0.91 us (2%)
    ppermute x6, waiting for transfers between devices, to_outer(): return lax.ppermute(values, 'expert', pairs)  8.53 us
    ppermute x6, starting transfers between devices, to_outer(): return lax.ppermute(values, 'expert', pairs)  8.31 us
    pallas_call x1, Pallas kernels, attend_and_project(): pl.pallas_call(attend_kernel, out_shape=[jax.ShapeDtypeStruct((sequences,...  6.83 us
    ppermute x2, starting transfers between devices, exchange(): received = lax.ppermute(sent, axis, pairs)  4.59 us
    ppermute x2, waiting for transfers between devices, exchange(): received = lax.ppermute(sent, axis, pairs)  4.5 us
    pallas_call x4, Pallas kernels, call(): pl.pallas_call(kernel, out_shape=[jax.ShapeDtypeStruct(shape, dtype) for...  3.49 us
    ppermute x5, waiting for transfers between devices, to_inner(): lax.ppermute(values, 'expert', [(rank, rank ^ 1) for rank in range(expert...  2.49 us
    unnamed x18, local copies, waits for them, and re-layouts  0.92 us
  transfers between devices with their start and end apart: 13, of which 8 were waited for; matrix products, arithmetic and copies ran while one was open for 1% of the time, Pallas kernels for 0%

profile of v4, /device:TPU:0, one launch (start us, length us, event | category | flops | bytes accessed | tf_op | source)
XLA Modules:
  0.0 41.5 jit_solution(17787944364524075758)
XLA Ops:
  0.0 0.0 copy-start.6
  0.0 0.0 copy-start.7
  0.0 0.0 copy-start.8
  0.0 0.0 copy-start.5
  0.0 0.0 copy-start.4
  0.0 6.8 %shard_map.145 = (f32[8,2880]{1,0:T(8,128)}, bf16[8,2880]{1,0:T(8,128)(2,1)}) custom-call(s32[8]{0:T(128)} %lengths_ref.1, bf16[8,16,64]{2,1,0:T(8,128)(2,1)} %queries_ref.1, bf16[8,4,64]{2,1,0:T(4,128)(2,1)} %new_keys_ref.1, bf16[8,4,64]{2,1,0:T(4,128)(2,1)} %new_values_ref.1, bf16[8,256,256]{2,1,0:T(8,128)(2,1)} %bitcast.16, ...), custom_call_target="tpu_custom_call" | custom-call | flops 47185920 | bytes 7995392 | tf_op jit(solution)/shard_map/pallas_call | solution.py:186
  6.9 3.0 %collective-permute-start = (bf16[8,2880]{1,0:T(8,128)(2,1)}, bf16[8,2880]{1,0:T(8,128)(2,1)S(1)}, u32[]{:S(2)}, u32[]{:S(2)}) collective-permute-start(bf16[8,2880]{1,0:T(8,128)(2,1)} %get-tuple-element.16), channel_id=1, source_target_pairs={{0,1},{1,0},{2,3},{3,2},{4,5},{5,4},{6,7},{7,6},{8,9},{9,8},{10,11... | collective-permute-start | bytes 138248 | tf_op jit(solution)/shard_map/ppermute | solution.py:233
  9.9 0.0 copy-done.6
  9.9 0.0 copy-done.7
  9.9 0.0 copy-done.8
  9.9 0.1 select_reduce_fusion
  10.0 0.1 pad.2.clone
  10.1 0.1 maximum_maximum_fusion.table_ref
  10.2 0.0 copy-done.5
  10.2 1.9 %collective-permute-done.received_ref = bf16[8,2880]{1,0:T(8,128)(2,1)S(1)} collective-permute-done((bf16[8,2880]{1,0:T(8,128)(2,1)}, bf16[8,2880]{1,0:T(8,128)(2,1)S(1)}, u32[]{:S(2)}, u32[]{:S(2)}) %collective-permute-start) | collective-permute-done | bytes 46112 | tf_op jit(solution)/shard_map/ppermute | solution.py:233
  12.1 0.0 copy-done.4
  12.1 0.0 copy-start.3
  12.1 0.9 %copy-done.3 = f32[8,2880]{1,0:T(8,128)S(1)} copy-done((f32[8,2880]{1,0:T(8,128)S(1)}, f32[8,2880]{1,0:T(8,128)}, u32[]{:S(2)}) %copy-start.3) | copy-done | bytes 92184
  13.0 0.0 copy-start
  13.0 0.0 copy-start.1
  13.0 0.0 copy-start.2
  13.0 0.1 shard_map.146
  13.2 2.2 %collective-permute-start.1 = (bf16[8,2944]{1,0:T(8,128)(2,1)S(1)}, bf16[8,2944]{1,0:T(8,128)(2,1)S(1)}, u32[]{:S(2)}, u32[]{:S(2)}) collective-permute-start(bf16[8,2944]{1,0:T(8,128)(2,1)S(1)} %get-tuple-element.18.refs_0_), channel_id=1, source_target_pairs={{0,4},{2,6},{4,0},{6,2},{8,12},{10,14},{12,8},{14,10},{1,5},{3,7},... | collective-permute-start | bytes 141320 | tf_op jit(solution)/shard_map/ppermute | solution.py:328
  15.4 2.6 %collective-permute-start.2 = (bf16[8,2944]{1,0:T(8,128)(2,1)S(1)}, bf16[8,2944]{1,0:T(8,128)(2,1)S(1)}, u32[]{:S(2)}, u32[]{:S(2)}) collective-permute-start(bf16[8,2944]{1,0:T(8,128)(2,1)S(1)} %get-tuple-element.18.refs_0_), channel_id=1, source_target_pairs={{0,8},{2,10},{4,12},{6,14},{8,0},{10,2},{12,4},{14,6},{1,9},{3,11}... | collective-permute-start | bytes 141320 | tf_op jit(solution)/shard_map/ppermute | solution.py:328
  17.9 0.0 collective-permute-start.3
  17.9 0.0 collective-permute-start.4
  17.9 0.0 collective-permute-done.1.refs_1_
  17.9 0.5 %collective-permute-start.5 = (bf16[8,2944]{1,0:T(8,128)(2,1)S(1)}, bf16[8,2944]{1,0:T(8,128)(2,1)S(1)}, u32[]{:S(2)}, u32[]{:S(2)}) collective-permute-start(bf16[8,2944]{1,0:T(8,128)(2,1)S(1)} %collective-permute-done.1.refs_1_), channel_id=1, source_target_pairs={{0,2},{2,0},{4,6},{6,4},{8,10},{10,8},{12,14},{14,12},{1,3},{3,1},... | collective-permute-start | bytes 141320 | tf_op jit(solution)/shard_map/ppermute | solution.py:331
  18.5 2.9 %collective-permute-done.2.refs_2_ = bf16[8,2944]{1,0:T(8,128)(2,1)S(1)} collective-permute-done((bf16[8,2944]{1,0:T(8,128)(2,1)S(1)}, bf16[8,2944]{1,0:T(8,128)(2,1)S(1)}, u32[]{:S(2)}, u32[]{:S(2)}) %collective-permute-start.2) | collective-permute-done | bytes 47136 | tf_op jit(solution)/shard_map/ppermute | solution.py:328
  21.3 0.0 collective-permute-start.6
  21.3 2.5 %collective-permute-done.3.refs_3_ = bf16[8,2944]{1,0:T(8,128)(2,1)S(1)} collective-permute-done((bf16[8,2944]{1,0:T(8,128)(2,1)S(1)}, bf16[8,2944]{1,0:T(8,128)(2,1)S(1)}, u32[]{:S(2)}, u32[]{:S(2)}) %collective-permute-start.3) | collective-permute-done | bytes 47136 | tf_op jit(solution)/shard_map/ppermute | solution.py:328
  23.8 0.0 collective-permute-start.7
  23.8 0.0 collective-permute-done.4.refs_4_
  23.8 0.0 collective-permute-done.5.refs_5_
  23.8 0.0 collective-permute-done.6.refs_6_
  23.8 1.2 %collective-permute-done.7.refs_7_ = bf16[8,2944]{1,0:T(8,128)(2,1)S(1)} collective-permute-done((bf16[8,2944]{1,0:T(8,128)(2,1)S(1)}, bf16[8,2944]{1,0:T(8,128)(2,1)S(1)}, u32[]{:S(2)}, u32[]{:S(2)}) %collective-permute-start.7) | collective-permute-done | bytes 47136 | tf_op jit(solution)/shard_map/ppermute | solution.py:331
  25.0 0.0 copy-done
  25.0 0.0 copy-done.1
  25.0 0.0 copy-done.2
  25.0 3.3 %shard_map.147 = (f32[32,2880]{1,0:T(8,128)S(1)}, bf16[32,2880]{1,0:T(8,128)(2,1)S(1)}) custom-call(bf16[8,2944]{1,0:T(8,128)(2,1)S(1)} %get-tuple-element.18.refs_0_, bf16[8,2944]{1,0:T(8,128)(2,1)S(1)} %collective-permute-done.1.refs_1_, bf16[8,2944]{1,0:T(8,128)(2,1)S(1)} %collective-permute-done.2.refs_2_, ...), custom_call_target="tpu_custom_call" | custom-call | flops 796262400 | bytes 12441600 | tf_op jit(solution)/shard_map/pallas_call | solution.py:55
  28.3 0.2 collective-permute-start.8
  28.6 1.3 %collective-permute-done.8.received_ref = bf16[32,2880]{1,0:T(8,128)(2,1)S(1)} collective-permute-done((bf16[32,2880]{1,0:T(8,128)(2,1)S(1)}, bf16[32,2880]{1,0:T(8,128)(2,1)S(1)}, u32[]{:S(2)}, u32[]{:S(2)}) %collective-permute-start.8) | collective-permute-done | bytes 184352 | tf_op jit(solution)/shard_map/ppermute | solution.py:331
  29.9 0.1 collective-permute-start.10
  30.0 1.0 %collective-permute-start.11 = (bf16[8,2880]{1,0:T(8,128)(2,1)S(1)}, bf16[8,2880]{1,0:T(8,128)(2,1)S(1)}, u32[]{:S(2)}, u32[]{:S(2)}) collective-permute-start(bf16[8,2880]{1,0:T(8,128)(2,1)S(1)} %get-tuple-element.24), channel_id=1, source_target_pairs={{0,12},{2,14},{4,8},{6,10},{8,4},{10,6},{12,0},{14,2},{1,13},{3,15... | collective-permute-start | bytes 138248 | tf_op jit(solution)/shard_map/ppermute | solution.py:328
  31.0 2.5 %collective-permute-start.9 = (bf16[8,2880]{1,0:T(8,128)(2,1)S(1)}, bf16[8,2880]{1,0:T(8,128)(2,1)S(1)}, u32[]{:S(2)}, u32[]{:S(2)}) collective-permute-start(bf16[8,2880]{1,0:T(8,128)(2,1)S(1)} %get-tuple-element.22), channel_id=1, source_target_pairs={{0,4},{2,6},{4,0},{6,2},{8,12},{10,14},{12,8},{14,10},{1,5},{3,7},... | collective-permute-start | bytes 138248 | tf_op jit(solution)/shard_map/ppermute | solution.py:328
  33.4 2.7 %collective-permute-done.10.refs_1_ = bf16[8,2880]{1,0:T(8,128)(2,1)S(1)} collective-permute-done((bf16[8,2880]{1,0:T(8,128)(2,1)S(1)}, bf16[8,2880]{1,0:T(8,128)(2,1)S(1)}, u32[]{:S(2)}, u32[]{:S(2)}) %collective-permute-start.10) | collective-permute-done | bytes 46112 | tf_op jit(solution)/shard_map/ppermute | solution.py:328
  36.1 0.0 collective-permute-done.11.refs_2_
  36.1 0.5 %collective-permute-done.9.refs_0_ = bf16[8,2880]{1,0:T(8,128)(2,1)S(1)} collective-permute-done((bf16[8,2880]{1,0:T(8,128)(2,1)S(1)}, bf16[8,2880]{1,0:T(8,128)(2,1)S(1)}, u32[]{:S(2)}, u32[]{:S(2)}) %collective-permute-start.9) | collective-permute-done | bytes 46112 | tf_op jit(solution)/shard_map/ppermute | solution.py:328
  36.7 1.6 %collective-permute-start.12 = (bf16[8,2880]{1,0:T(8,128)(2,1)S(1)}, bf16[8,2880]{1,0:T(8,128)(2,1)S(1)}, u32[]{:S(2)}, u32[]{:S(2)}) collective-permute-start(bf16[8,2880]{1,0:T(8,128)(2,1)S(1)} %convert_element_type.21), channel_id=1, source_target_pairs={{0,1},{1,0},{2,3},{3,2},{4,5},{5,4},{6,7},{7,6},{8,9},{9,8},{10,11... | collective-permute-start | bytes 138248 | tf_op jit(solution)/shard_map/ppermute | solution.py:233
  38.2 2.6 %collective-permute-done.12 = bf16[8,2880]{1,0:T(8,128)(2,1)S(1)} collective-permute-done((bf16[8,2880]{1,0:T(8,128)(2,1)S(1)}, bf16[8,2880]{1,0:T(8,128)(2,1)S(1)}, u32[]{:S(2)}, u32[]{:S(2)}) %collective-permute-start.12) | collective-permute-done | bytes 46112 | tf_op jit(solution)/shard_map/ppermute | solution.py:233
  40.8 0.7 %fusion.1 = bf16[8,1440]{1,0:T(8,128)(2,1)} fusion(f32[8,2880]{1,0:T(8,128)S(1)} %shard_map.149, s32[]{:T(128)S(6)} %select_n.25, f32[8,2880]{1,0:T(8,128)S(1)} %get-tuple-element.17, bf16[8,2880]{1,0:T(8,128)(2,1)S(1)} %collective-permute-done.12), kind=kLoop, calls=%fused_computation.2 | loop fusion | flops 46080 | bytes 138244 | tf_op jit(solution)/shard_map/convert_element_type | solution.py:388
  (9 shorter events, 0.1 us)
Async XLA Ops:
  0.0 9.9 %copy-start.6 = (f32[8,4]{0,1:T(4,128)S(1)}, f32[8,4]{0,1:T(4,128)}, u32[]{:S(2)}) copy-start(f32[8,4]{0,1:T(4,128)} %param.25) | copy-start | bytes 388
  0.0 9.9 %copy-start.7 = (s32[8,4]{0,1:T(4,128)S(1)}, s32[8,4]{0,1:T(4,128)}, u32[]{:S(2)}) copy-start(s32[8,4]{0,1:T(4,128)} %param.26) | copy-start | bytes 388
  0.0 9.9 %copy-start.8 = (s32[8,4]{0,1:T(4,128)S(1)}, s32[8,4]{0,1:T(4,128)}, u32[]{:S(2)}) copy-start(s32[8,4]{0,1:T(4,128)} %param.24) | copy-start | bytes 388
  0.0 10.2 %copy-start.5 = (f32[2880]{0:T(1024)S(1)}, f32[2880]{0:T(1024)}, u32[]{:S(2)}) copy-start(f32[2880]{0:T(1024)} %param.23) | copy-start | bytes 34564
  0.0 12.1 %copy-start.4 = (bf16[8,2880]{1,0:T(8,128)(2,1)S(1)}, bf16[8,2880]{1,0:T(8,128)(2,1)}, u32[]{:S(2)}) copy-start(bf16[8,2880]{1,0:T(8,128)(2,1)} %hidden_ref.1) | copy-start | bytes 138244
  6.9 5.3 %collective-permute-start = (bf16[8,2880]{1,0:T(8,128)(2,1)}, bf16[8,2880]{1,0:T(8,128)(2,1)S(1)}, u32[]{:S(2)}, u32[]{:S(2)}) collective-permute-start(bf16[8,2880]{1,0:T(8,128)(2,1)} %get-tuple-element.16), channel_id=1, source_target_pairs={{0,1},{1,0},{2,3},{3,2},{4,5},{5,4},{6,7},{7,6},{8,9},{9,8},{10,11... | collective-permute-start | bytes 138248 | tf_op jit(solution)/shard_map/ppermute | solution.py:233
  12.1 0.9 %copy-start.3 = (f32[8,2880]{1,0:T(8,128)S(1)}, f32[8,2880]{1,0:T(8,128)}, u32[]{:S(2)}) copy-start(f32[8,2880]{1,0:T(8,128)} %get-tuple-element.15.mine_ref) | copy-start | bytes 276484
  13.0 12.0 %copy-start = (bf16[1,2880,720]{1,2,0:T(8,128)(2,1)S(1)}, bf16[1,2880,720]{1,2,0:T(8,128)(2,1)}, u32[]{:S(2)}) copy-start(bf16[1,2880,720]{1,2,0:T(8,128)(2,1)} %param.27) | copy-start | bytes 12441604
  13.0 12.0 %copy-start.1 = (bf16[1,2880,720]{1,2,0:T(8,128)(2,1)S(1)}, bf16[1,2880,720]{1,2,0:T(8,128)(2,1)}, u32[]{:S(2)}) copy-start(bf16[1,2880,720]{1,2,0:T(8,128)(2,1)} %param.28) | copy-start | bytes 12441604
  13.0 12.0 %copy-start.2 = (bf16[1,720,2880]{2,1,0:T(8,128)(2,1)S(1)}, bf16[1,720,2880]{2,1,0:T(8,128)(2,1)}, u32[]{:S(2)}) copy-start(bf16[1,720,2880]{2,1,0:T(8,128)(2,1)} %refs_10_.1) | copy-start | bytes 12441604
  13.2 4.8 %collective-permute-start.1 = (bf16[8,2944]{1,0:T(8,128)(2,1)S(1)}, bf16[8,2944]{1,0:T(8,128)(2,1)S(1)}, u32[]{:S(2)}, u32[]{:S(2)}) collective-permute-start(bf16[8,2944]{1,0:T(8,128)(2,1)S(1)} %get-tuple-element.18.refs_0_), channel_id=1, source_target_pairs={{0,4},{2,6},{4,0},{6,2},{8,12},{10,14},{12,8},{14,10},{1,5},{3,7},... | collective-permute-start | bytes 141320 | tf_op jit(solution)/shard_map/ppermute | solution.py:328
  15.4 6.0 %collective-permute-start.2 = (bf16[8,2944]{1,0:T(8,128)(2,1)S(1)}, bf16[8,2944]{1,0:T(8,128)(2,1)S(1)}, u32[]{:S(2)}, u32[]{:S(2)}) collective-permute-start(bf16[8,2944]{1,0:T(8,128)(2,1)S(1)} %get-tuple-element.18.refs_0_), channel_id=1, source_target_pairs={{0,8},{2,10},{4,12},{6,14},{8,0},{10,2},{12,4},{14,6},{1,9},{3,11}... | collective-permute-start | bytes 141320 | tf_op jit(solution)/shard_map/ppermute | solution.py:328
  17.9 5.9 %collective-permute-start.3 = (bf16[8,2944]{1,0:T(8,128)(2,1)S(1)}, bf16[8,2944]{1,0:T(8,128)(2,1)S(1)}, u32[]{:S(2)}, u32[]{:S(2)}) collective-permute-start(bf16[8,2944]{1,0:T(8,128)(2,1)S(1)} %get-tuple-element.18.refs_0_), channel_id=1, source_target_pairs={{0,12},{2,14},{4,8},{6,10},{8,4},{10,6},{12,0},{14,2},{1,13},{3,15... | collective-permute-start | bytes 141320 | tf_op jit(solution)/shard_map/ppermute | solution.py:328
  17.9 5.9 %collective-permute-start.4 = (bf16[8,2944]{1,0:T(8,128)(2,1)S(1)}, bf16[8,2944]{1,0:T(8,128)(2,1)S(1)}, u32[]{:S(2)}, u32[]{:S(2)}) collective-permute-start(bf16[8,2944]{1,0:T(8,128)(2,1)S(1)} %get-tuple-element.18.refs_0_), channel_id=1, source_target_pairs={{0,2},{2,0},{4,6},{6,4},{8,10},{10,8},{12,14},{14,12},{1,3},{3,1},... | collective-permute-start | bytes 141320 | tf_op jit(solution)/shard_map/ppermute | solution.py:331
  17.9 5.9 %collective-permute-start.5 = (bf16[8,2944]{1,0:T(8,128)(2,1)S(1)}, bf16[8,2944]{1,0:T(8,128)(2,1)S(1)}, u32[]{:S(2)}, u32[]{:S(2)}) collective-permute-start(bf16[8,2944]{1,0:T(8,128)(2,1)S(1)} %collective-permute-done.1.refs_1_), channel_id=1, source_target_pairs={{0,2},{2,0},{4,6},{6,4},{8,10},{10,8},{12,14},{14,12},{1,3},{3,1},... | collective-permute-start | bytes 141320 | tf_op jit(solution)/shard_map/ppermute | solution.py:331
  21.3 2.5 %collective-permute-start.6 = (bf16[8,2944]{1,0:T(8,128)(2,1)S(1)}, bf16[8,2944]{1,0:T(8,128)(2,1)S(1)}, u32[]{:S(2)}, u32[]{:S(2)}) collective-permute-start(bf16[8,2944]{1,0:T(8,128)(2,1)S(1)} %collective-permute-done.2.refs_2_), channel_id=1, source_target_pairs={{0,2},{2,0},{4,6},{6,4},{8,10},{10,8},{12,14},{14,12},{1,3},{3,1},... | collective-permute-start | bytes 141320 | tf_op jit(solution)/shard_map/ppermute | solution.py:331
  23.8 1.2 %collective-permute-start.7 = (bf16[8,2944]{1,0:T(8,128)(2,1)S(1)}, bf16[8,2944]{1,0:T(8,128)(2,1)S(1)}, u32[]{:S(2)}, u32[]{:S(2)}) collective-permute-start(bf16[8,2944]{1,0:T(8,128)(2,1)S(1)} %collective-permute-done.3.refs_3_), channel_id=1, source_target_pairs={{0,2},{2,0},{4,6},{6,4},{8,10},{10,8},{12,14},{14,12},{1,3},{3,1},... | collective-permute-start | bytes 141320 | tf_op jit(solution)/shard_map/ppermute | solution.py:331
  28.3 1.5 %collective-permute-start.8 = (bf16[32,2880]{1,0:T(8,128)(2,1)S(1)}, bf16[32,2880]{1,0:T(8,128)(2,1)S(1)}, u32[]{:S(2)}, u32[]{:S(2)}) collective-permute-start(bf16[32,2880]{1,0:T(8,128)(2,1)S(1)} %get-tuple-element.20), channel_id=1, source_target_pairs={{0,2},{2,0},{4,6},{6,4},{8,10},{10,8},{12,14},{14,12},{1,3},{3,1},... | collective-permute-start | bytes 552968 | tf_op jit(solution)/shard_map/ppermute | solution.py:331
  29.9 6.2 %collective-permute-start.10 = (bf16[8,2880]{1,0:T(8,128)(2,1)S(1)}, bf16[8,2880]{1,0:T(8,128)(2,1)S(1)}, u32[]{:S(2)}, u32[]{:S(2)}) collective-permute-start(bf16[8,2880]{1,0:T(8,128)(2,1)S(1)} %get-tuple-element.23), channel_id=1, source_target_pairs={{0,8},{2,10},{4,12},{6,14},{8,0},{10,2},{12,4},{14,6},{1,9},{3,11}... | collective-permute-start | bytes 138248 | tf_op jit(solution)/shard_map/ppermute | solution.py:328
  30.0 6.2 %collective-permute-start.11 = (bf16[8,2880]{1,0:T(8,128)(2,1)S(1)}, bf16[8,2880]{1,0:T(8,128)(2,1)S(1)}, u32[]{:S(2)}, u32[]{:S(2)}) collective-permute-start(bf16[8,2880]{1,0:T(8,128)(2,1)S(1)} %get-tuple-element.24), channel_id=1, source_target_pairs={{0,12},{2,14},{4,8},{6,10},{8,4},{10,6},{12,0},{14,2},{1,13},{3,15... | collective-permute-start | bytes 138248 | tf_op jit(solution)/shard_map/ppermute | solution.py:328
  31.0 5.6 %collective-permute-start.9 = (bf16[8,2880]{1,0:T(8,128)(2,1)S(1)}, bf16[8,2880]{1,0:T(8,128)(2,1)S(1)}, u32[]{:S(2)}, u32[]{:S(2)}) collective-permute-start(bf16[8,2880]{1,0:T(8,128)(2,1)S(1)} %get-tuple-element.22), channel_id=1, source_target_pairs={{0,4},{2,6},{4,0},{6,2},{8,12},{10,14},{12,8},{14,10},{1,5},{3,7},... | collective-permute-start | bytes 138248 | tf_op jit(solution)/shard_map/ppermute | solution.py:328
  36.7 4.1 %collective-permute-start.12 = (bf16[8,2880]{1,0:T(8,128)(2,1)S(1)}, bf16[8,2880]{1,0:T(8,128)(2,1)S(1)}, u32[]{:S(2)}, u32[]{:S(2)}) collective-permute-start(bf16[8,2880]{1,0:T(8,128)(2,1)S(1)} %convert_element_type.21), channel_id=1, source_target_pairs={{0,1},{1,0},{2,3},{3,2},{4,5},{5,4},{6,7},{7,6},{8,9},{9,8},{10,11... | collective-permute-start | bytes 138248 | tf_op jit(solution)/shard_map/ppermute | solution.py:233

commit v5 on v4

--- a/solution.py
+++ b/solution.py
@@ -71,15 +71,19 @@
 
 
 def attend_kernel(
-    lengths_ref,
-    queries_ref,
-    new_keys_ref,
-    new_values_ref,
+    lengths_hbm,
+    queries_hbm,
+    new_keys_hbm,
+    new_values_hbm,
     keys_hbm,
     values_hbm,
     weight_hbm,
     mine_ref,
     sent_ref,
+    lengths_ref,
+    queries_ref,
+    new_keys_ref,
+    new_values_ref,
     keys_ref,
     values_ref,
     weight_ref,
@@ -93,16 +97,26 @@
     group = heads // kv_heads
     span = kv_heads * head_dim
     lanes = group * head_dim
+    moves = (
+        (lengths_hbm, lengths_ref),
+        (queries_hbm, queries_ref),
+        (new_keys_hbm, new_keys_ref),
+        (new_values_hbm, new_values_ref),
+        (keys_hbm, keys_ref),
+        (values_hbm, values_ref),
+        (weight_hbm, weight_ref),
+    )
     copies = [
-        pltpu.make_async_copy(keys_hbm, keys_ref, arrived.at[0]),
-        pltpu.make_async_copy(values_hbm, values_ref, arrived.at[1]),
-        pltpu.make_async_copy(weight_hbm, weight_ref, arrived.at[2]),
+        pltpu.make_async_copy(source, target, arrived.at[number])
+        for number, (source, target) in enumerate(moves)
     ]
     for copy in copies:
         copy.start()
 
     rows = sequences * heads
     scaling = 1.0 / head_dim**0.5
+    for copy in copies[:4]:
+        copy.wait()
     queries = queries_ref[...].reshape(rows, head_dim)
     for sequence in range(sequences):
         block = pl.ds(sequence * kv_heads, kv_heads)
@@ -123,7 +137,7 @@
         * scaling
     )
 
-    copies[0].wait()
+    copies[4].wait()
     slots = keys_ref.shape[2]
     scores = []
     for sequence in range(sequences):
@@ -141,7 +155,7 @@
     own_prob = jnp.where(own_pair, own_prob, 0.0).astype(jnp.bfloat16)
     own_part = mm(own_prob, mm(own_values, spread).astype(jnp.bfloat16))
 
-    copies[1].wait()
+    copies[5].wait()
     attended = [
         mm(
             cache_prob[sequence * heads : (sequence + 1) * heads],
@@ -168,7 +182,7 @@
         ].astype(jnp.bfloat16)
     attended = attended_ref[...]
 
-    copies[2].wait()
+    copies[6].wait()
     part = mm(weight_ref[...], attended, LAST_DIMS).T
     mine_ref[...] = part
     sent_ref[...] = part.astype(jnp.bfloat16)
@@ -183,30 +197,7 @@
     span = kv_heads * head_dim
     caches = (sequences, span, slots)
     hbm = pl.BlockSpec(memory_space=pltpu.HBM)
-    return pl.pallas_call(
-        attend_kernel,
-        out_shape=[
-            jax.ShapeDtypeStruct((sequences, width), jnp.float32),
-            jax.ShapeDtypeStruct((sequences, width), jnp.bfloat16),
-        ],
-        in_specs=[pl.BlockSpec(memory_space=pltpu.SMEM)] + [VMEM] * 3 + [hbm] * 3,
-        out_specs=[VMEM] * 2,
-        scratch_shapes=[
-            pltpu.VMEM(caches, jnp.bfloat16),
-            pltpu.VMEM(caches, jnp.bfloat16),
-            pltpu.VMEM((width, depth), jnp.bfloat16),
-            pltpu.VMEM((sequences * kv_heads, head_dim), jnp.float32),
-            pltpu.VMEM((sequences * kv_heads, head_dim), jnp.float32),
-            pltpu.VMEM((sequences, depth), jnp.bfloat16),
-            pltpu.SemaphoreType.DMA((3,)),
-        ],
-        compiler_params=pltpu.CompilerParams(vmem_limit_bytes=60 * MIB),
-        cost_estimate=pl.CostEstimate(
-            flops=2 * sequences * width * depth,
-            bytes_accessed=2 * (width * depth + 2 * sequences * span * slots),
-            transcendentals=sequences * heads * slots,
-        ),
-    )(
+    arrays = (
         cache_lengths,
         queries,
         new_keys,
@@ -215,6 +206,29 @@
         cache_values.reshape(caches),
         out_weight.T,
     )
+    return pl.pallas_call(
+        attend_kernel,
+        out_shape=[
+            jax.ShapeDtypeStruct((sequences, width), jnp.float32),
+            jax.ShapeDtypeStruct((sequences, width), jnp.bfloat16),
+        ],
+        in_specs=[hbm] * len(arrays),
+        out_specs=[VMEM] * 2,
+        scratch_shapes=[pltpu.SMEM(cache_lengths.shape, cache_lengths.dtype)]
+        + [pltpu.VMEM(array.shape, array.dtype) for array in arrays[1:]]
+        + [
+            pltpu.VMEM((sequences * kv_heads, head_dim), jnp.float32),
+            pltpu.VMEM((sequences * kv_heads, head_dim), jnp.float32),
+            pltpu.VMEM((sequences, depth), jnp.bfloat16),
+            pltpu.SemaphoreType.DMA((len(arrays),)),
+        ],
+        compiler_params=pltpu.CompilerParams(vmem_limit_bytes=53 * MIB),
+        cost_estimate=pl.CostEstimate(
+            flops=2 * sequences * width * depth,
+            bytes_accessed=2 * (width * depth + 2 * sequences * span * slots),
+            transcendentals=sequences * heads * slots,
+        ),
+    )(*[pltpu.with_memory_space_constraint(array, pltpu.HBM) for array in arrays])
 
 
 def route_weights(expert_ids, route_probs, route_order, experts):

time: 41.7 us -> 39.2 us (0.940)
  Pallas kernels: 10.3 us -> 8.94 us
  local copies, waits for them, and re-layouts: 1.01 us -> 0.12 us
    pallas_call x1, Pallas kernels: 6.83 us -> 5.45 us  [attend_and_project(): pl.pallas_call(attend_kernel, out_shape=[jax.ShapeDtypeStruct((sequences,...]
    unnamed x18 -> x16, local copies, waits for them, and re-layouts: 0.92 us -> 0.03 us
where the time goes in v5:
time: 39.2 us; the launch traced here: 39 us
  waiting for transfers between devices  15.3 us (39%)
  starting transfers between devices  13.6 us (35%)
  Pallas kernels  8.94 us (23%)
  other arithmetic  0.91 us (2%)
    ppermute x6, waiting for transfers between devices, to_outer(): return lax.ppermute(values, 'expert', pairs)  8.53 us
    ppermute x6, starting transfers between devices, to_outer(): return lax.ppermute(values, 'expert', pairs)  8.3 us
    pallas_call x1, Pallas kernels, attend_and_project(): pl.pallas_call(attend_kernel, out_shape=[jax.ShapeDtypeStruct((sequences,...  5.45 us
    ppermute x2, starting transfers between devices, exchange(): received = lax.ppermute(sent, axis, pairs)  4.59 us
    ppermute x2, waiting for transfers between devices, exchange(): received = lax.ppermute(sent, axis, pairs)  4.3 us
    pallas_call x4, Pallas kernels, call(): pl.pallas_call(kernel, out_shape=[jax.ShapeDtypeStruct(shape, dtype) for...  3.49 us
    ppermute x5, waiting for transfers between devices, to_inner(): lax.ppermute(values, 'expert', [(rank, rank ^ 1) for rank in range(expert...  2.49 us
  transfers between devices with their start and end apart: 13, of which 8 were waited for; matrix products, arithmetic and copies ran while one was open for 1% of the time, Pallas kernels for 0%

profile of v5, /device:TPU:0, one launch (start us, length us, event | category | flops | bytes accessed | tf_op | source)
XLA Modules:
  0.0 39.0 jit_solution(13723618724822817915)
XLA Ops:
  0.0 0.0 copy-start.5
  0.0 0.0 copy-start.6
  0.0 0.0 copy-start.7
  0.0 0.0 copy-start.4
  0.0 0.0 copy-start.3
  0.0 5.4 %shard_map.145 = (f32[8,2880]{1,0:T(8,128)S(1)}, bf16[8,2880]{1,0:T(8,128)(2,1)S(1)}) custom-call(s32[8]{0:T(128)} %lengths_hbm.1, bf16[8,16,64]{2,1,0:T(8,128)(2,1)} %queries_hbm.1, bf16[8,4,64]{2,1,0:T(4,128)(2,1)} %new_keys_hbm.1, bf16[8,4,64]{2,1,0:T(4,128)(2,1)} %new_values_hbm.1, bf16[8,256,256]{2,1,0:T(8,128)(2,1)} %bitcast.16, ...), custom_call_target="tpu_custom_call" | custom-call | flops 47185920 | bytes 7995392 | tf_op jit(solution)/shard_map/pallas_call | solution.py:209
  5.5 3.0 %collective-permute-start = (bf16[8,2880]{1,0:T(8,128)(2,1)S(1)}, bf16[8,2880]{1,0:T(8,128)(2,1)S(1)}, u32[]{:S(2)}, u32[]{:S(2)}) collective-permute-start(bf16[8,2880]{1,0:T(8,128)(2,1)S(1)} %get-tuple-element.16), channel_id=1, source_target_pairs={{0,1},{1,0},{2,3},{3,2},{4,5},{5,4},{6,7},{7,6},{8,9},{9,8},{10,11... | collective-permute-start | bytes 138248 | tf_op jit(solution)/shard_map/ppermute | solution.py:247
  8.5 0.0 copy-done.5
  8.5 0.0 copy-done.6
  8.6 0.0 copy-done.7
  8.6 0.1 select_reduce_fusion
  8.7 0.1 pad.2.clone
  8.7 0.1 maximum_maximum_fusion.table_ref
  8.8 0.0 copy-done.4
  8.8 1.7 %collective-permute-done.received_ref = bf16[8,2880]{1,0:T(8,128)(2,1)S(1)} collective-permute-done((bf16[8,2880]{1,0:T(8,128)(2,1)S(1)}, bf16[8,2880]{1,0:T(8,128)(2,1)S(1)}, u32[]{:S(2)}, u32[]{:S(2)}) %collective-permute-start) | collective-permute-done | bytes 46112 | tf_op jit(solution)/shard_map/ppermute | solution.py:247
  10.6 0.0 copy-done.3
  10.6 0.0 copy-start
  10.6 0.0 copy-start.1
  10.6 0.0 copy-start.2
  10.6 0.1 shard_map.146
  10.7 2.2 %collective-permute-start.1 = (bf16[8,2944]{1,0:T(8,128)(2,1)S(1)}, bf16[8,2944]{1,0:T(8,128)(2,1)S(1)}, u32[]{:S(2)}, u32[]{:S(2)}) collective-permute-start(bf16[8,2944]{1,0:T(8,128)(2,1)S(1)} %get-tuple-element.18.refs_0_), channel_id=1, source_target_pairs={{0,4},{2,6},{4,0},{6,2},{8,12},{10,14},{12,8},{14,10},{1,5},{3,7},... | collective-permute-start | bytes 141320 | tf_op jit(solution)/shard_map/ppermute | solution.py:342
  12.9 2.6 %collective-permute-start.2 = (bf16[8,2944]{1,0:T(8,128)(2,1)S(1)}, bf16[8,2944]{1,0:T(8,128)(2,1)S(1)}, u32[]{:S(2)}, u32[]{:S(2)}) collective-permute-start(bf16[8,2944]{1,0:T(8,128)(2,1)S(1)} %get-tuple-element.18.refs_0_), channel_id=1, source_target_pairs={{0,8},{2,10},{4,12},{6,14},{8,0},{10,2},{12,4},{14,6},{1,9},{3,11}... | collective-permute-start | bytes 141320 | tf_op jit(solution)/shard_map/ppermute | solution.py:342
  15.5 0.0 collective-permute-start.3
  15.5 0.0 collective-permute-start.4
  15.5 0.0 collective-permute-done.1.refs_1_
  15.5 0.5 %collective-permute-start.5 = (bf16[8,2944]{1,0:T(8,128)(2,1)S(1)}, bf16[8,2944]{1,0:T(8,128)(2,1)S(1)}, u32[]{:S(2)}, u32[]{:S(2)}) collective-permute-start(bf16[8,2944]{1,0:T(8,128)(2,1)S(1)} %collective-permute-done.1.refs_1_), channel_id=1, source_target_pairs={{0,2},{2,0},{4,6},{6,4},{8,10},{10,8},{12,14},{14,12},{1,3},{3,1},... | collective-permute-start | bytes 141320 | tf_op jit(solution)/shard_map/ppermute | solution.py:345
  16.0 2.9 %collective-permute-done.2.refs_2_ = bf16[8,2944]{1,0:T(8,128)(2,1)S(1)} collective-permute-done((bf16[8,2944]{1,0:T(8,128)(2,1)S(1)}, bf16[8,2944]{1,0:T(8,128)(2,1)S(1)}, u32[]{:S(2)}, u32[]{:S(2)}) %collective-permute-start.2) | collective-permute-done | bytes 47136 | tf_op jit(solution)/shard_map/ppermute | solution.py:342
  18.8 0.0 collective-permute-start.6
  18.8 2.5 %collective-permute-done.3.refs_3_ = bf16[8,2944]{1,0:T(8,128)(2,1)S(1)} collective-permute-done((bf16[8,2944]{1,0:T(8,128)(2,1)S(1)}, bf16[8,2944]{1,0:T(8,128)(2,1)S(1)}, u32[]{:S(2)}, u32[]{:S(2)}) %collective-permute-start.3) | collective-permute-done | bytes 47136 | tf_op jit(solution)/shard_map/ppermute | solution.py:342
  21.3 0.0 collective-permute-start.7
  21.3 0.0 collective-permute-done.4.refs_4_
  21.3 0.0 collective-permute-done.5.refs_5_
  21.3 0.0 collective-permute-done.6.refs_6_
  21.3 1.2 %collective-permute-done.7.refs_7_ = bf16[8,2944]{1,0:T(8,128)(2,1)S(1)} collective-permute-done((bf16[8,2944]{1,0:T(8,128)(2,1)S(1)}, bf16[8,2944]{1,0:T(8,128)(2,1)S(1)}, u32[]{:S(2)}, u32[]{:S(2)}) %collective-permute-start.7) | collective-permute-done | bytes 47136 | tf_op jit(solution)/shard_map/ppermute | solution.py:345
  22.5 0.0 copy-done
  22.6 0.0 copy-done.1
  22.6 0.0 copy-done.2
  22.6 3.3 %shard_map.147 = (f32[32,2880]{1,0:T(8,128)S(1)}, bf16[32,2880]{1,0:T(8,128)(2,1)S(1)}) custom-call(bf16[8,2944]{1,0:T(8,128)(2,1)S(1)} %get-tuple-element.18.refs_0_, bf16[8,2944]{1,0:T(8,128)(2,1)S(1)} %collective-permute-done.1.refs_1_, bf16[8,2944]{1,0:T(8,128)(2,1)S(1)} %collective-permute-done.2.refs_2_, ...), custom_call_target="tpu_custom_call" | custom-call | flops 796262400 | bytes 12441600 | tf_op jit(solution)/shard_map/pallas_call | solution.py:55
  25.9 0.2 collective-permute-start.8
  26.1 1.3 %collective-permute-done.8.received_ref = bf16[32,2880]{1,0:T(8,128)(2,1)S(1)} collective-permute-done((bf16[32,2880]{1,0:T(8,128)(2,1)S(1)}, bf16[32,2880]{1,0:T(8,128)(2,1)S(1)}, u32[]{:S(2)}, u32[]{:S(2)}) %collective-permute-start.8) | collective-permute-done | bytes 184352 | tf_op jit(solution)/shard_map/ppermute | solution.py:345
  27.4 0.1 collective-permute-start.10
  27.5 1.0 %collective-permute-start.11 = (bf16[8,2880]{1,0:T(8,128)(2,1)S(1)}, bf16[8,2880]{1,0:T(8,128)(2,1)S(1)}, u32[]{:S(2)}, u32[]{:S(2)}) collective-permute-start(bf16[8,2880]{1,0:T(8,128)(2,1)S(1)} %get-tuple-element.24), channel_id=1, source_target_pairs={{0,12},{2,14},{4,8},{6,10},{8,4},{10,6},{12,0},{14,2},{1,13},{3,15... | collective-permute-start | bytes 138248 | tf_op jit(solution)/shard_map/ppermute | solution.py:342
  28.5 2.5 %collective-permute-start.9 = (bf16[8,2880]{1,0:T(8,128)(2,1)S(1)}, bf16[8,2880]{1,0:T(8,128)(2,1)S(1)}, u32[]{:S(2)}, u32[]{:S(2)}) collective-permute-start(bf16[8,2880]{1,0:T(8,128)(2,1)S(1)} %get-tuple-element.22), channel_id=1, source_target_pairs={{0,4},{2,6},{4,0},{6,2},{8,12},{10,14},{12,8},{14,10},{1,5},{3,7},... | collective-permute-start | bytes 138248 | tf_op jit(solution)/shard_map/ppermute | solution.py:342
  31.0 2.7 %collective-permute-done.10.refs_1_ = bf16[8,2880]{1,0:T(8,128)(2,1)S(1)} collective-permute-done((bf16[8,2880]{1,0:T(8,128)(2,1)S(1)}, bf16[8,2880]{1,0:T(8,128)(2,1)S(1)}, u32[]{:S(2)}, u32[]{:S(2)}) %collective-permute-start.10) | collective-permute-done | bytes 46112 | tf_op jit(solution)/shard_map/ppermute | solution.py:342
  33.6 0.0 collective-permute-done.11.refs_2_
  33.6 0.5 %collective-permute-done.9.refs_0_ = bf16[8,2880]{1,0:T(8,128)(2,1)S(1)} collective-permute-done((bf16[8,2880]{1,0:T(8,128)(2,1)S(1)}, bf16[8,2880]{1,0:T(8,128)(2,1)S(1)}, u32[]{:S(2)}, u32[]{:S(2)}) %collective-permute-start.9) | collective-permute-done | bytes 46112 | tf_op jit(solution)/shard_map/ppermute | solution.py:342
  34.2 1.6 %collective-permute-start.12 = (bf16[8,2880]{1,0:T(8,128)(2,1)S(1)}, bf16[8,2880]{1,0:T(8,128)(2,1)S(1)}, u32[]{:S(2)}, u32[]{:S(2)}) collective-permute-start(bf16[8,2880]{1,0:T(8,128)(2,1)S(1)} %convert_element_type.21), channel_id=1, source_target_pairs={{0,1},{1,0},{2,3},{3,2},{4,5},{5,4},{6,7},{7,6},{8,9},{9,8},{10,11... | collective-permute-start | bytes 138248 | tf_op jit(solution)/shard_map/ppermute | solution.py:247
  35.7 2.6 %collective-permute-done.12 = bf16[8,2880]{1,0:T(8,128)(2,1)S(1)} collective-permute-done((bf16[8,2880]{1,0:T(8,128)(2,1)S(1)}, bf16[8,2880]{1,0:T(8,128)(2,1)S(1)}, u32[]{:S(2)}, u32[]{:S(2)}) %collective-permute-start.12) | collective-permute-done | bytes 46112 | tf_op jit(solution)/shard_map/ppermute | solution.py:247
  38.3 0.7 %fusion.1 = bf16[8,1440]{1,0:T(8,128)(2,1)} fusion(f32[8,2880]{1,0:T(8,128)S(1)} %shard_map.149, s32[]{:T(128)S(6)} %select_n.25, f32[8,2880]{1,0:T(8,128)S(1)} %get-tuple-element.17, bf16[8,2880]{1,0:T(8,128)(2,1)S(1)} %collective-permute-done.12), kind=kLoop, calls=%fused_computation.2 | loop fusion | flops 46080 | bytes 138244 | tf_op jit(solution)/shard_map/convert_element_type | solution.py:402
  (9 shorter events, 0.1 us)
Async XLA Ops:
  0.0 8.5 %copy-start.5 = (f32[8,4]{0,1:T(4,128)S(1)}, f32[8,4]{0,1:T(4,128)}, u32[]{:S(2)}) copy-start(f32[8,4]{0,1:T(4,128)} %param.25) | copy-start | bytes 388
  0.0 8.5 %copy-start.6 = (s32[8,4]{0,1:T(4,128)S(1)}, s32[8,4]{0,1:T(4,128)}, u32[]{:S(2)}) copy-start(s32[8,4]{0,1:T(4,128)} %param.26) | copy-start | bytes 388
  0.0 8.5 %copy-start.7 = (s32[8,4]{0,1:T(4,128)S(1)}, s32[8,4]{0,1:T(4,128)}, u32[]{:S(2)}) copy-start(s32[8,4]{0,1:T(4,128)} %param.24) | copy-start | bytes 388
  0.0 8.8 %copy-start.4 = (f32[2880]{0:T(1024)S(1)}, f32[2880]{0:T(1024)}, u32[]{:S(2)}) copy-start(f32[2880]{0:T(1024)} %param.23) | copy-start | bytes 34564
  0.0 10.5 %copy-start.3 = (bf16[8,2880]{1,0:T(8,128)(2,1)S(1)}, bf16[8,2880]{1,0:T(8,128)(2,1)}, u32[]{:S(2)}) copy-start(bf16[8,2880]{1,0:T(8,128)(2,1)} %hidden_ref.1) | copy-start | bytes 138244
  5.5 5.1 %collective-permute-start = (bf16[8,2880]{1,0:T(8,128)(2,1)S(1)}, bf16[8,2880]{1,0:T(8,128)(2,1)S(1)}, u32[]{:S(2)}, u32[]{:S(2)}) collective-permute-start(bf16[8,2880]{1,0:T(8,128)(2,1)S(1)} %get-tuple-element.16), channel_id=1, source_target_pairs={{0,1},{1,0},{2,3},{3,2},{4,5},{5,4},{6,7},{7,6},{8,9},{9,8},{10,11... | collective-permute-start | bytes 138248 | tf_op jit(solution)/shard_map/ppermute | solution.py:247
  10.6 12.0 %copy-start = (bf16[1,2880,720]{1,2,0:T(8,128)(2,1)S(1)}, bf16[1,2880,720]{1,2,0:T(8,128)(2,1)}, u32[]{:S(2)}) copy-start(bf16[1,2880,720]{1,2,0:T(8,128)(2,1)} %param.27) | copy-start | bytes 12441604
  10.6 12.0 %copy-start.1 = (bf16[1,2880,720]{1,2,0:T(8,128)(2,1)S(1)}, bf16[1,2880,720]{1,2,0:T(8,128)(2,1)}, u32[]{:S(2)}) copy-start(bf16[1,2880,720]{1,2,0:T(8,128)(2,1)} %param.28) | copy-start | bytes 12441604
  10.6 12.0 %copy-start.2 = (bf16[1,720,2880]{2,1,0:T(8,128)(2,1)S(1)}, bf16[1,720,2880]{2,1,0:T(8,128)(2,1)}, u32[]{:S(2)}) copy-start(bf16[1,720,2880]{2,1,0:T(8,128)(2,1)} %refs_10_.1) | copy-start | bytes 12441604
  10.7 4.8 %collective-permute-start.1 = (bf16[8,2944]{1,0:T(8,128)(2,1)S(1)}, bf16[8,2944]{1,0:T(8,128)(2,1)S(1)}, u32[]{:S(2)}, u32[]{:S(2)}) collective-permute-start(bf16[8,2944]{1,0:T(8,128)(2,1)S(1)} %get-tuple-element.18.refs_0_), channel_id=1, source_target_pairs={{0,4},{2,6},{4,0},{6,2},{8,12},{10,14},{12,8},{14,10},{1,5},{3,7},... | collective-permute-start | bytes 141320 | tf_op jit(solution)/shard_map/ppermute | solution.py:342
  12.9 6.0 %collective-permute-start.2 = (bf16[8,2944]{1,0:T(8,128)(2,1)S(1)}, bf16[8,2944]{1,0:T(8,128)(2,1)S(1)}, u32[]{:S(2)}, u32[]{:S(2)}) collective-permute-start(bf16[8,2944]{1,0:T(8,128)(2,1)S(1)} %get-tuple-element.18.refs_0_), channel_id=1, source_target_pairs={{0,8},{2,10},{4,12},{6,14},{8,0},{10,2},{12,4},{14,6},{1,9},{3,11}... | collective-permute-start | bytes 141320 | tf_op jit(solution)/shard_map/ppermute | solution.py:342
  15.5 5.9 %collective-permute-start.3 = (bf16[8,2944]{1,0:T(8,128)(2,1)S(1)}, bf16[8,2944]{1,0:T(8,128)(2,1)S(1)}, u32[]{:S(2)}, u32[]{:S(2)}) collective-permute-start(bf16[8,2944]{1,0:T(8,128)(2,1)S(1)} %get-tuple-element.18.refs_0_), channel_id=1, source_target_pairs={{0,12},{2,14},{4,8},{6,10},{8,4},{10,6},{12,0},{14,2},{1,13},{3,15... | collective-permute-start | bytes 141320 | tf_op jit(solution)/shard_map/ppermute | solution.py:342
  15.5 5.9 %collective-permute-start.4 = (bf16[8,2944]{1,0:T(8,128)(2,1)S(1)}, bf16[8,2944]{1,0:T(8,128)(2,1)S(1)}, u32[]{:S(2)}, u32[]{:S(2)}) collective-permute-start(bf16[8,2944]{1,0:T(8,128)(2,1)S(1)} %get-tuple-element.18.refs_0_), channel_id=1, source_target_pairs={{0,2},{2,0},{4,6},{6,4},{8,10},{10,8},{12,14},{14,12},{1,3},{3,1},... | collective-permute-start | bytes 141320 | tf_op jit(solution)/shard_map/ppermute | solution.py:345
  15.5 5.9 %collective-permute-start.5 = (bf16[8,2944]{1,0:T(8,128)(2,1)S(1)}, bf16[8,2944]{1,0:T(8,128)(2,1)S(1)}, u32[]{:S(2)}, u32[]{:S(2)}) collective-permute-start(bf16[8,2944]{1,0:T(8,128)(2,1)S(1)} %collective-permute-done.1.refs_1_), channel_id=1, source_target_pairs={{0,2},{2,0},{4,6},{6,4},{8,10},{10,8},{12,14},{14,12},{1,3},{3,1},... | collective-permute-start | bytes 141320 | tf_op jit(solution)/shard_map/ppermute | solution.py:345
  18.8 2.5 %collective-permute-start.6 = (bf16[8,2944]{1,0:T(8,128)(2,1)S(1)}, bf16[8,2944]{1,0:T(8,128)(2,1)S(1)}, u32[]{:S(2)}, u32[]{:S(2)}) collective-permute-start(bf16[8,2944]{1,0:T(8,128)(2,1)S(1)} %collective-permute-done.2.refs_2_), channel_id=1, source_target_pairs={{0,2},{2,0},{4,6},{6,4},{8,10},{10,8},{12,14},{14,12},{1,3},{3,1},... | collective-permute-start | bytes 141320 | tf_op jit(solution)/shard_map/ppermute | solution.py:345
  21.3 1.2 %collective-permute-start.7 = (bf16[8,2944]{1,0:T(8,128)(2,1)S(1)}, bf16[8,2944]{1,0:T(8,128)(2,1)S(1)}, u32[]{:S(2)}, u32[]{:S(2)}) collective-permute-start(bf16[8,2944]{1,0:T(8,128)(2,1)S(1)} %collective-permute-done.3.refs_3_), channel_id=1, source_target_pairs={{0,2},{2,0},{4,6},{6,4},{8,10},{10,8},{12,14},{14,12},{1,3},{3,1},... | collective-permute-start | bytes 141320 | tf_op jit(solution)/shard_map/ppermute | solution.py:345
  25.9 1.5 %collective-permute-start.8 = (bf16[32,2880]{1,0:T(8,128)(2,1)S(1)}, bf16[32,2880]{1,0:T(8,128)(2,1)S(1)}, u32[]{:S(2)}, u32[]{:S(2)}) collective-permute-start(bf16[32,2880]{1,0:T(8,128)(2,1)S(1)} %get-tuple-element.20), channel_id=1, source_target_pairs={{0,2},{2,0},{4,6},{6,4},{8,10},{10,8},{12,14},{14,12},{1,3},{3,1},... | collective-permute-start | bytes 552968 | tf_op jit(solution)/shard_map/ppermute | solution.py:345
  27.4 6.2 %collective-permute-start.10 = (bf16[8,2880]{1,0:T(8,128)(2,1)S(1)}, bf16[8,2880]{1,0:T(8,128)(2,1)S(1)}, u32[]{:S(2)}, u32[]{:S(2)}) collective-permute-start(bf16[8,2880]{1,0:T(8,128)(2,1)S(1)} %get-tuple-element.23), channel_id=1, source_target_pairs={{0,8},{2,10},{4,12},{6,14},{8,0},{10,2},{12,4},{14,6},{1,9},{3,11}... | collective-permute-start | bytes 138248 | tf_op jit(solution)/shard_map/ppermute | solution.py:342
  27.5 6.2 %collective-permute-start.11 = (bf16[8,2880]{1,0:T(8,128)(2,1)S(1)}, bf16[8,2880]{1,0:T(8,128)(2,1)S(1)}, u32[]{:S(2)}, u32[]{:S(2)}) collective-permute-start(bf16[8,2880]{1,0:T(8,128)(2,1)S(1)} %get-tuple-element.24), channel_id=1, source_target_pairs={{0,12},{2,14},{4,8},{6,10},{8,4},{10,6},{12,0},{14,2},{1,13},{3,15... | collective-permute-start | bytes 138248 | tf_op jit(solution)/shard_map/ppermute | solution.py:342
  28.5 5.7 %collective-permute-start.9 = (bf16[8,2880]{1,0:T(8,128)(2,1)S(1)}, bf16[8,2880]{1,0:T(8,128)(2,1)S(1)}, u32[]{:S(2)}, u32[]{:S(2)}) collective-permute-start(bf16[8,2880]{1,0:T(8,128)(2,1)S(1)} %get-tuple-element.22), channel_id=1, source_target_pairs={{0,4},{2,6},{4,0},{6,2},{8,12},{10,14},{12,8},{14,10},{1,5},{3,7},... | collective-permute-start | bytes 138248 | tf_op jit(solution)/shard_map/ppermute | solution.py:342
  34.2 4.1 %collective-permute-start.12 = (bf16[8,2880]{1,0:T(8,128)(2,1)S(1)}, bf16[8,2880]{1,0:T(8,128)(2,1)S(1)}, u32[]{:S(2)}, u32[]{:S(2)}) collective-permute-start(bf16[8,2880]{1,0:T(8,128)(2,1)S(1)} %convert_element_type.21), channel_id=1, source_target_pairs={{0,1},{1,0},{2,3},{3,2},{4,5},{5,4},{6,7},{7,6},{8,9},{9,8},{10,11... | collective-permute-start | bytes 138248 | tf_op jit(solution)/shard_map/ppermute | solution.py:247

commit v6 on v5

--- a/solution.py
+++ b/solution.py
@@ -264,9 +264,15 @@
     rows_ref[:, width:] = table_ref[...]
 
 
-def expert_kernel(blocks, experts, *refs):
-    row_refs = refs[:blocks]
-    gate_ref, up_ref, down_ref, mine_ref, other_ref = refs[blocks:]
+def pack_kernel(*refs):
+    *piece_refs, packed_ref = refs
+    size = piece_refs[0].shape[0]
+    for number, piece_ref in enumerate(piece_refs):
+        packed_ref[pl.ds(number * size, size)] = piece_ref[...]
+
+
+def expert_kernel(experts, *refs):
+    *row_refs, gate_ref, up_ref, down_ref, mine_ref, other_ref = refs
     local_experts, _, width = down_ref.shape
     rows = jnp.concatenate([ref[:, :width] for ref in row_refs], axis=0)
     table = jnp.concatenate([ref[:, width:] for ref in row_refs], axis=0).astype(jnp.float32)
@@ -288,8 +294,7 @@
         total = part if total is None else total + part
     half = mine_ref.shape[0]
     mine_ref[...] = total[:half]
-    if other_ref.shape[0] == half:
-        other_ref[...] = total[half:].astype(jnp.bfloat16)
+    other_ref[...] = total[half:].astype(jnp.bfloat16)
 
 
 def split_kernel(mine_ref, received_ref, kept_ref, *sent_refs):
@@ -368,13 +373,23 @@
         limit=2 * MIB,
     )
 
-    near = [rows] + [to_outer(rows, step) for step in range(1, outer)]
-    far = [to_inner(piece) for piece in near]
+    near = [rows]
+    for step in range(1, outer):
+        near.append(to_outer(rows, step))
+    (near,) = call(
+        pack_kernel,
+        [((outer * sequences, row_width), jnp.bfloat16)],
+        near,
+        flops=sequences,
+        moved=4 * outer * sequences * row_width,
+        limit=2 * MIB,
+    )
+    far = to_inner(near)
     half = (outer * sequences, width)
     mine, other = call(
-        functools.partial(expert_kernel, 2 * outer, experts),
+        functools.partial(expert_kernel, experts),
         [(half, jnp.float32), (half, jnp.bfloat16)],
-        (*near, *far, gate_weight.swapaxes(1, 2), up_weight.swapaxes(1, 2), down_weight),
+        (near, far, gate_weight.swapaxes(1, 2), up_weight.swapaxes(1, 2), down_weight),
         flops=12 * half[0] * width * hidden_units * local_experts,
         moved=6 * width * hidden_units * local_experts,
         limit=16 * MIB,
@@ -388,7 +403,9 @@
         moved=half[0] * width * 8,
         limit=4 * MIB,
     )
-    returned = [to_outer(piece, step) for step, piece in enumerate(sent, 1)]
+    returned = []
+    for step, piece in enumerate(sent, 1):
+        returned.append(to_outer(piece, step))
     (mixture,) = call(
         gather_kernel,
         [(block, jnp.float32)],
@@ -421,6 +438,7 @@
         P("expert", "tensor", None),
     )
     out_specs = P(("groups", "expert"), "tensor")
+
     return jax.shard_map(
         per_device, mesh=mesh, in_specs=in_specs, out_specs=out_specs, check_vma=False
     )

time: 39.2 us -> 40 us (1.020)
  starting transfers between devices: 13.6 us -> 14.1 us
    ppermute x6, starting transfers between devices: 8.3 us -> 9.2 us  [to_outer(): return lax.ppermute(values, 'expert', pairs)]
    ppermute x5 -> x2, starting transfers between devices: 0.73 us -> 0.27 us  [to_inner(): lax.ppermute(values, 'expert', [(rank, rank ^ 1) for rank in range(expert...]
    ppermute x5 -> x2, waiting for transfers between devices: 2.49 us -> 2.71 us  [to_inner(): lax.ppermute(values, 'expert', [(rank, rank ^ 1) for rank in range(expert...]
    pallas_call x4 -> x5, Pallas kernels: 3.49 us -> 3.5 us  [call(): pl.pallas_call(kernel, out_shape=[jax.ShapeDtypeStruct(shape, dtype) for...]
  transfers between devices with their start and end apart: 13 -> 10, of which waited for: 8 -> 8; matrix products, arithmetic and copies ran while one was open for 1% -> 1% of each run, Pallas kernels for 0% -> 0%
where the time goes in v6:
time: 40 us; the launch traced here: 39.9 us
  waiting for transfers between devices  15.7 us (39%)
  starting transfers between devices  14.1 us (35%)
  Pallas kernels  8.94 us (22%)
  other arithmetic  0.91 us (2%)
    ppermute x6, starting transfers between devices, to_outer(): return lax.ppermute(values, 'expert', pairs)  9.2 us
    ppermute x6, waiting for transfers between devices, to_outer(): return lax.ppermute(values, 'expert', pairs)  8.72 us
    pallas_call x1, Pallas kernels, attend_and_project(): pl.pallas_call(attend_kernel, out_shape=[jax.ShapeDtypeStruct((sequences,...  5.45 us
    ppermute x2, starting transfers between devices, exchange(): received = lax.ppermute(sent, axis, pairs)  4.59 us
    ppermute x2, waiting for transfers between devices, exchange(): received = lax.ppermute(sent, axis, pairs)  4.3 us
    pallas_call x5, Pallas kernels, call(): pl.pallas_call(kernel, out_shape=[jax.ShapeDtypeStruct(shape, dtype) for...  3.5 us
    ppermute x2, waiting for transfers between devices, to_inner(): lax.ppermute(values, 'expert', [(rank, rank ^ 1) for rank in range(expert...  2.71 us
  transfers between devices with their start and end apart: 10, of which 8 were waited for; matrix products, arithmetic and copies ran while one was open for 1% of the time, Pallas kernels for 0%

profile of v6, /device:TPU:0, one launch (start us, length us, event | category | flops | bytes accessed | tf_op | source)
XLA Modules:
  0.0 39.9 jit_solution(17713718931978109244)
XLA Ops:
  0.0 0.0 copy-start.5
  0.0 0.0 copy-start.6
  0.0 0.0 copy-start.7
  0.0 0.0 copy-start.4
  0.0 0.0 copy-start.3
  0.0 5.4 %shard_map.145 = (f32[8,2880]{1,0:T(8,128)S(1)}, bf16[8,2880]{1,0:T(8,128)(2,1)S(1)}) custom-call(s32[8]{0:T(128)} %lengths_hbm.1, bf16[8,16,64]{2,1,0:T(8,128)(2,1)} %queries_hbm.1, bf16[8,4,64]{2,1,0:T(4,128)(2,1)} %new_keys_hbm.1, bf16[8,4,64]{2,1,0:T(4,128)(2,1)} %new_values_hbm.1, bf16[8,256,256]{2,1,0:T(8,128)(2,1)} %bitcast.16, ...), custom_call_target="tpu_custom_call" | custom-call | flops 47185920 | bytes 7995392 | tf_op jit(solution)/shard_map/pallas_call | solution.py:209
  5.5 3.0 %collective-permute-start = (bf16[8,2880]{1,0:T(8,128)(2,1)S(1)}, bf16[8,2880]{1,0:T(8,128)(2,1)S(1)}, u32[]{:S(2)}, u32[]{:S(2)}) collective-permute-start(bf16[8,2880]{1,0:T(8,128)(2,1)S(1)} %get-tuple-element.16), channel_id=1, source_target_pairs={{0,1},{1,0},{2,3},{3,2},{4,5},{5,4},{6,7},{7,6},{8,9},{9,8},{10,11... | collective-permute-start | bytes 138248 | tf_op jit(solution)/shard_map/ppermute | solution.py:247
  8.5 0.0 copy-done.5
  8.5 0.0 copy-done.6
  8.6 0.0 copy-done.7
  8.6 0.1 select_reduce_fusion
  8.7 0.1 pad.2.clone
  8.7 0.1 maximum_maximum_fusion.table_ref
  8.8 0.0 copy-done.4
  8.8 1.7 %collective-permute-done.received_ref = bf16[8,2880]{1,0:T(8,128)(2,1)S(1)} collective-permute-done((bf16[8,2880]{1,0:T(8,128)(2,1)S(1)}, bf16[8,2880]{1,0:T(8,128)(2,1)S(1)}, u32[]{:S(2)}, u32[]{:S(2)}) %collective-permute-start) | collective-permute-done | bytes 46112 | tf_op jit(solution)/shard_map/ppermute | solution.py:247
  10.6 0.0 copy-done.3
  10.6 0.0 copy-start
  10.6 0.0 copy-start.1
  10.6 0.0 copy-start.2
  10.6 0.1 shard_map.146
  10.7 2.2 %collective-permute-start.1 = (bf16[8,2944]{1,0:T(8,128)(2,1)S(1)}, bf16[8,2944]{1,0:T(8,128)(2,1)S(1)}, u32[]{:S(2)}, u32[]{:S(2)}) collective-permute-start(bf16[8,2944]{1,0:T(8,128)(2,1)S(1)} %get-tuple-element.18.refs_0_), channel_id=1, source_target_pairs={{0,4},{2,6},{4,0},{6,2},{8,12},{10,14},{12,8},{14,10},{1,5},{3,7},... | collective-permute-start | bytes 141320 | tf_op jit(solution)/shard_map/ppermute | solution.py:347
  12.9 2.6 %collective-permute-start.2 = (bf16[8,2944]{1,0:T(8,128)(2,1)S(1)}, bf16[8,2944]{1,0:T(8,128)(2,1)S(1)}, u32[]{:S(2)}, u32[]{:S(2)}) collective-permute-start(bf16[8,2944]{1,0:T(8,128)(2,1)S(1)} %get-tuple-element.18.refs_0_), channel_id=1, source_target_pairs={{0,8},{2,10},{4,12},{6,14},{8,0},{10,2},{12,4},{14,6},{1,9},{3,11}... | collective-permute-start | bytes 141320 | tf_op jit(solution)/shard_map/ppermute | solution.py:347
  15.5 0.0 collective-permute-start.3
  15.5 0.0 collective-permute-done.1.refs_1_
  15.5 3.4 %collective-permute-done.2.refs_2_ = bf16[8,2944]{1,0:T(8,128)(2,1)S(1)} collective-permute-done((bf16[8,2944]{1,0:T(8,128)(2,1)S(1)}, bf16[8,2944]{1,0:T(8,128)(2,1)S(1)}, u32[]{:S(2)}, u32[]{:S(2)}) %collective-permute-start.2) | collective-permute-done | bytes 47136 | tf_op jit(solution)/shard_map/ppermute | solution.py:347
  18.8 2.5 %collective-permute-done.3.refs_3_ = bf16[8,2944]{1,0:T(8,128)(2,1)S(1)} collective-permute-done((bf16[8,2944]{1,0:T(8,128)(2,1)S(1)}, bf16[8,2944]{1,0:T(8,128)(2,1)S(1)}, u32[]{:S(2)}, u32[]{:S(2)}) %collective-permute-start.3) | collective-permute-done | bytes 47136 | tf_op jit(solution)/shard_map/ppermute | solution.py:347
  21.3 0.1 collective-permute-start.4
  21.4 1.4 %collective-permute-done.4.refs_1_ = bf16[32,2944]{1,0:T(8,128)(2,1)S(1)} collective-permute-done((bf16[32,2944]{1,0:T(8,128)(2,1)S(1)}, bf16[32,2944]{1,0:T(8,128)(2,1)S(1)}, u32[]{:S(2)}, u32[]{:S(2)}) %collective-permute-start.4) | collective-permute-done | bytes 188448 | tf_op jit(solution)/shard_map/ppermute | solution.py:350
  22.8 0.0 copy-done
  22.8 0.0 copy-done.1
  22.8 0.0 copy-done.2
  22.8 3.3 %shard_map.148 = (f32[32,2880]{1,0:T(8,128)S(1)}, bf16[32,2880]{1,0:T(8,128)(2,1)S(1)}) custom-call(bf16[32,2944]{1,0:T(8,128)(2,1)S(1)} %shard_map.147.refs_0_, bf16[32,2944]{1,0:T(8,128)(2,1)S(1)} %collective-permute-done.4.refs_1_, bf16[1,720,2880]{2,1,0:T(8,128)(2,1)S(1)} %bitcast.13, bf16[1,720,2880]{2,1,0:T(8,128)(2,1)S(1)} %bitcast.14, ...), custom_call_target="tpu_custom_call" | custom-call | flops 796262400 | bytes 12441600 | tf_op jit(solution)/shard_map/pallas_call | solution.py:55
  26.1 0.2 collective-permute-start.5
  26.3 1.3 %collective-permute-done.5.received_ref = bf16[32,2880]{1,0:T(8,128)(2,1)S(1)} collective-permute-done((bf16[32,2880]{1,0:T(8,128)(2,1)S(1)}, bf16[32,2880]{1,0:T(8,128)(2,1)S(1)}, u32[]{:S(2)}, u32[]{:S(2)}) %collective-permute-start.5) | collective-permute-done | bytes 184352 | tf_op jit(solution)/shard_map/ppermute | solution.py:350
  27.7 0.1 collective-permute-start.6
  27.8 1.1 %collective-permute-start.7 = (bf16[8,2880]{1,0:T(8,128)(2,1)S(1)}, bf16[8,2880]{1,0:T(8,128)(2,1)S(1)}, u32[]{:S(2)}, u32[]{:S(2)}) collective-permute-start(bf16[8,2880]{1,0:T(8,128)(2,1)S(1)} %get-tuple-element.23), channel_id=1, source_target_pairs={{0,8},{2,10},{4,12},{6,14},{8,0},{10,2},{12,4},{14,6},{1,9},{3,11}... | collective-permute-start | bytes 138248 | tf_op jit(solution)/shard_map/ppermute | solution.py:347
  28.8 3.3 %collective-permute-start.8 = (bf16[8,2880]{1,0:T(8,128)(2,1)S(1)}, bf16[8,2880]{1,0:T(8,128)(2,1)S(1)}, u32[]{:S(2)}, u32[]{:S(2)}) collective-permute-start(bf16[8,2880]{1,0:T(8,128)(2,1)S(1)} %get-tuple-element.24), channel_id=1, source_target_pairs={{0,12},{2,14},{4,8},{6,10},{8,4},{10,6},{12,0},{14,2},{1,13},{3,15... | collective-permute-start | bytes 138248 | tf_op jit(solution)/shard_map/ppermute | solution.py:347
  32.1 0.2 collective-permute-done.6.refs_0_
  32.3 2.6 %collective-permute-done.7.refs_1_ = bf16[8,2880]{1,0:T(8,128)(2,1)S(1)} collective-permute-done((bf16[8,2880]{1,0:T(8,128)(2,1)S(1)}, bf16[8,2880]{1,0:T(8,128)(2,1)S(1)}, u32[]{:S(2)}, u32[]{:S(2)}) %collective-permute-start.7) | collective-permute-done | bytes 46112 | tf_op jit(solution)/shard_map/ppermute | solution.py:347
  35.0 0.0 collective-permute-done.8.refs_2_
  35.0 1.6 %collective-permute-start.9 = (bf16[8,2880]{1,0:T(8,128)(2,1)S(1)}, bf16[8,2880]{1,0:T(8,128)(2,1)S(1)}, u32[]{:S(2)}, u32[]{:S(2)}) collective-permute-start(bf16[8,2880]{1,0:T(8,128)(2,1)S(1)} %convert_element_type.21), channel_id=1, source_target_pairs={{0,1},{1,0},{2,3},{3,2},{4,5},{5,4},{6,7},{7,6},{8,9},{9,8},{10,11... | collective-permute-start | bytes 138248 | tf_op jit(solution)/shard_map/ppermute | solution.py:247
  36.6 2.6 %collective-permute-done.9 = bf16[8,2880]{1,0:T(8,128)(2,1)S(1)} collective-permute-done((bf16[8,2880]{1,0:T(8,128)(2,1)S(1)}, bf16[8,2880]{1,0:T(8,128)(2,1)S(1)}, u32[]{:S(2)}, u32[]{:S(2)}) %collective-permute-start.9) | collective-permute-done | bytes 46112 | tf_op jit(solution)/shard_map/ppermute | solution.py:247
  39.2 0.7 %fusion.1 = bf16[8,1440]{1,0:T(8,128)(2,1)} fusion(f32[8,2880]{1,0:T(8,128)S(1)} %shard_map.150, s32[]{:T(128)S(6)} %select_n.25, f32[8,2880]{1,0:T(8,128)S(1)} %get-tuple-element.17, bf16[8,2880]{1,0:T(8,128)(2,1)S(1)} %collective-permute-done.9), kind=kLoop, calls=%fused_computation.2 | loop fusion | flops 46080 | bytes 138244 | tf_op jit(solution)/shard_map/convert_element_type | solution.py:419
  (10 shorter events, 0.2 us)
Async XLA Ops:
  0.0 8.5 %copy-start.5 = (f32[8,4]{0,1:T(4,128)S(1)}, f32[8,4]{0,1:T(4,128)}, u32[]{:S(2)}) copy-start(f32[8,4]{0,1:T(4,128)} %param.25) | copy-start | bytes 388
  0.0 8.5 %copy-start.6 = (s32[8,4]{0,1:T(4,128)S(1)}, s32[8,4]{0,1:T(4,128)}, u32[]{:S(2)}) copy-start(s32[8,4]{0,1:T(4,128)} %param.26) | copy-start | bytes 388
  0.0 8.5 %copy-start.7 = (s32[8,4]{0,1:T(4,128)S(1)}, s32[8,4]{0,1:T(4,128)}, u32[]{:S(2)}) copy-start(s32[8,4]{0,1:T(4,128)} %param.24) | copy-start | bytes 388
  0.0 8.8 %copy-start.4 = (f32[2880]{0:T(1024)S(1)}, f32[2880]{0:T(1024)}, u32[]{:S(2)}) copy-start(f32[2880]{0:T(1024)} %param.23) | copy-start | bytes 34564
  0.0 10.5 %copy-start.3 = (bf16[8,2880]{1,0:T(8,128)(2,1)S(1)}, bf16[8,2880]{1,0:T(8,128)(2,1)}, u32[]{:S(2)}) copy-start(bf16[8,2880]{1,0:T(8,128)(2,1)} %hidden_ref.1) | copy-start | bytes 138244
  5.5 5.1 %collective-permute-start = (bf16[8,2880]{1,0:T(8,128)(2,1)S(1)}, bf16[8,2880]{1,0:T(8,128)(2,1)S(1)}, u32[]{:S(2)}, u32[]{:S(2)}) collective-permute-start(bf16[8,2880]{1,0:T(8,128)(2,1)S(1)} %get-tuple-element.16), channel_id=1, source_target_pairs={{0,1},{1,0},{2,3},{3,2},{4,5},{5,4},{6,7},{7,6},{8,9},{9,8},{10,11... | collective-permute-start | bytes 138248 | tf_op jit(solution)/shard_map/ppermute | solution.py:247
  10.6 12.3 %copy-start = (bf16[1,2880,720]{1,2,0:T(8,128)(2,1)S(1)}, bf16[1,2880,720]{1,2,0:T(8,128)(2,1)}, u32[]{:S(2)}) copy-start(bf16[1,2880,720]{1,2,0:T(8,128)(2,1)} %param.27) | copy-start | bytes 12441604
  10.6 12.3 %copy-start.1 = (bf16[1,2880,720]{1,2,0:T(8,128)(2,1)S(1)}, bf16[1,2880,720]{1,2,0:T(8,128)(2,1)}, u32[]{:S(2)}) copy-start(bf16[1,2880,720]{1,2,0:T(8,128)(2,1)} %param.28) | copy-start | bytes 12441604
  10.6 12.3 %copy-start.2 = (bf16[1,720,2880]{2,1,0:T(8,128)(2,1)S(1)}, bf16[1,720,2880]{2,1,0:T(8,128)(2,1)}, u32[]{:S(2)}) copy-start(bf16[1,720,2880]{2,1,0:T(8,128)(2,1)} %refs_4_.1) | copy-start | bytes 12441604
  10.7 4.8 %collective-permute-start.1 = (bf16[8,2944]{1,0:T(8,128)(2,1)S(1)}, bf16[8,2944]{1,0:T(8,128)(2,1)S(1)}, u32[]{:S(2)}, u32[]{:S(2)}) collective-permute-start(bf16[8,2944]{1,0:T(8,128)(2,1)S(1)} %get-tuple-element.18.refs_0_), channel_id=1, source_target_pairs={{0,4},{2,6},{4,0},{6,2},{8,12},{10,14},{12,8},{14,10},{1,5},{3,7},... | collective-permute-start | bytes 141320 | tf_op jit(solution)/shard_map/ppermute | solution.py:347
  12.9 6.0 %collective-permute-start.2 = (bf16[8,2944]{1,0:T(8,128)(2,1)S(1)}, bf16[8,2944]{1,0:T(8,128)(2,1)S(1)}, u32[]{:S(2)}, u32[]{:S(2)}) collective-permute-start(bf16[8,2944]{1,0:T(8,128)(2,1)S(1)} %get-tuple-element.18.refs_0_), channel_id=1, source_target_pairs={{0,8},{2,10},{4,12},{6,14},{8,0},{10,2},{12,4},{14,6},{1,9},{3,11}... | collective-permute-start | bytes 141320 | tf_op jit(solution)/shard_map/ppermute | solution.py:347
  15.5 5.9 %collective-permute-start.3 = (bf16[8,2944]{1,0:T(8,128)(2,1)S(1)}, bf16[8,2944]{1,0:T(8,128)(2,1)S(1)}, u32[]{:S(2)}, u32[]{:S(2)}) collective-permute-start(bf16[8,2944]{1,0:T(8,128)(2,1)S(1)} %get-tuple-element.18.refs_0_), channel_id=1, source_target_pairs={{0,12},{2,14},{4,8},{6,10},{8,4},{10,6},{12,0},{14,2},{1,13},{3,15... | collective-permute-start | bytes 141320 | tf_op jit(solution)/shard_map/ppermute | solution.py:347
  21.3 1.5 %collective-permute-start.4 = (bf16[32,2944]{1,0:T(8,128)(2,1)S(1)}, bf16[32,2944]{1,0:T(8,128)(2,1)S(1)}, u32[]{:S(2)}, u32[]{:S(2)}) collective-permute-start(bf16[32,2944]{1,0:T(8,128)(2,1)S(1)} %shard_map.147.refs_0_), channel_id=1, source_target_pairs={{0,2},{2,0},{4,6},{6,4},{8,10},{10,8},{12,14},{14,12},{1,3},{3,1},... | collective-permute-start | bytes 565256 | tf_op jit(solution)/shard_map/ppermute | solution.py:350
  26.1 1.5 %collective-permute-start.5 = (bf16[32,2880]{1,0:T(8,128)(2,1)S(1)}, bf16[32,2880]{1,0:T(8,128)(2,1)S(1)}, u32[]{:S(2)}, u32[]{:S(2)}) collective-permute-start(bf16[32,2880]{1,0:T(8,128)(2,1)S(1)} %get-tuple-element.20), channel_id=1, source_target_pairs={{0,2},{2,0},{4,6},{6,4},{8,10},{10,8},{12,14},{14,12},{1,3},{3,1},... | collective-permute-start | bytes 552968 | tf_op jit(solution)/shard_map/ppermute | solution.py:350
  27.7 4.7 %collective-permute-start.6 = (bf16[8,2880]{1,0:T(8,128)(2,1)S(1)}, bf16[8,2880]{1,0:T(8,128)(2,1)S(1)}, u32[]{:S(2)}, u32[]{:S(2)}) collective-permute-start(bf16[8,2880]{1,0:T(8,128)(2,1)S(1)} %get-tuple-element.22), channel_id=1, source_target_pairs={{0,4},{2,6},{4,0},{6,2},{8,12},{10,14},{12,8},{14,10},{1,5},{3,7},... | collective-permute-start | bytes 138248 | tf_op jit(solution)/shard_map/ppermute | solution.py:347
  27.8 7.2 %collective-permute-start.7 = (bf16[8,2880]{1,0:T(8,128)(2,1)S(1)}, bf16[8,2880]{1,0:T(8,128)(2,1)S(1)}, u32[]{:S(2)}, u32[]{:S(2)}) collective-permute-start(bf16[8,2880]{1,0:T(8,128)(2,1)S(1)} %get-tuple-element.23), channel_id=1, source_target_pairs={{0,8},{2,10},{4,12},{6,14},{8,0},{10,2},{12,4},{14,6},{1,9},{3,11}... | collective-permute-start | bytes 138248 | tf_op jit(solution)/shard_map/ppermute | solution.py:347
  28.8 6.2 %collective-permute-start.8 = (bf16[8,2880]{1,0:T(8,128)(2,1)S(1)}, bf16[8,2880]{1,0:T(8,128)(2,1)S(1)}, u32[]{:S(2)}, u32[]{:S(2)}) collective-permute-start(bf16[8,2880]{1,0:T(8,128)(2,1)S(1)} %get-tuple-element.24), channel_id=1, source_target_pairs={{0,12},{2,14},{4,8},{6,10},{8,4},{10,6},{12,0},{14,2},{1,13},{3,15... | collective-permute-start | bytes 138248 | tf_op jit(solution)/shard_map/ppermute | solution.py:347
  35.0 4.1 %collective-permute-start.9 = (bf16[8,2880]{1,0:T(8,128)(2,1)S(1)}, bf16[8,2880]{1,0:T(8,128)(2,1)S(1)}, u32[]{:S(2)}, u32[]{:S(2)}) collective-permute-start(bf16[8,2880]{1,0:T(8,128)(2,1)S(1)} %convert_element_type.21), channel_id=1, source_target_pairs={{0,1},{1,0},{2,3},{3,2},{4,5},{5,4},{6,7},{7,6},{8,9},{9,8},{10,11... | collective-permute-start | bytes 138248 | tf_op jit(solution)/shard_map/ppermute | solution.py:247

commit v7 on v6

--- a/solution.py
+++ b/solution.py
@@ -71,6 +71,7 @@
 
 
 def attend_kernel(
+    pieces,
     lengths_hbm,
     queries_hbm,
     new_keys_hbm,
@@ -104,7 +105,7 @@
         (new_values_hbm, new_values_ref),
         (keys_hbm, keys_ref),
         (values_hbm, values_ref),
-        (weight_hbm, weight_ref),
+        *((weight_hbm.at[pl.ds(*piece)], weight_ref.at[pl.ds(*piece)]) for piece in pieces),
     )
     copies = [
         pltpu.make_async_copy(source, target, arrived.at[number])
@@ -182,10 +183,11 @@
         ].astype(jnp.bfloat16)
     attended = attended_ref[...]
 
-    copies[6].wait()
-    part = mm(weight_ref[...], attended, LAST_DIMS).T
-    mine_ref[...] = part
-    sent_ref[...] = part.astype(jnp.bfloat16)
+    for copy, (start, size) in zip(copies[6:], pieces):
+        copy.wait()
+        part = mm(attended, weight_ref[pl.ds(start, size)], LAST_DIMS)
+        mine_ref[:, start : start + size] = part
+        sent_ref[:, start : start + size] = part.astype(jnp.bfloat16)
 
 
 def attend_and_project(
@@ -206,8 +208,10 @@
         cache_values.reshape(caches),
         out_weight.T,
     )
+    first = -(-width // 512) * 256
+    pieces = ((0, first), (first, width - first))
     return pl.pallas_call(
-        attend_kernel,
+        functools.partial(attend_kernel, pieces),
         out_shape=[
             jax.ShapeDtypeStruct((sequences, width), jnp.float32),
             jax.ShapeDtypeStruct((sequences, width), jnp.bfloat16),
@@ -220,7 +224,7 @@
             pltpu.VMEM((sequences * kv_heads, head_dim), jnp.float32),
             pltpu.VMEM((sequences * kv_heads, head_dim), jnp.float32),
             pltpu.VMEM((sequences, depth), jnp.bfloat16),
-            pltpu.SemaphoreType.DMA((len(arrays),)),
+            pltpu.SemaphoreType.DMA((len(arrays) - 1 + len(pieces),)),
         ],
         compiler_params=pltpu.CompilerParams(vmem_limit_bytes=53 * MIB),
         cost_estimate=pl.CostEstimate(
@@ -306,12 +310,25 @@
         sent_ref[...] = total.astype(jnp.bfloat16)
 
 
-def gather_kernel(kept_ref, *refs):
-    *received_refs, total_ref = refs
+def return_kernel(received, residual_ref, *refs):
+    kept_ref, *received_refs = refs[: 1 + received]
+    base_ref, *sent_refs = refs[1 + received :]
     total = kept_ref[...]
     for received_ref in received_refs:
         total = total + received_ref[...].astype(jnp.float32)
-    total_ref[...] = total
+    width = base_ref.shape[1]
+    rank = lax.axis_index("tensor")
+
+    def slab_of(values, owner):
+        slab = values[:, :width]
+        for number in range(1, values.shape[1] // width):
+            piece = values[:, number * width : (number + 1) * width]
+            slab = jnp.where(owner == number, piece, slab)
+        return slab
+
+    base_ref[...] = slab_of(total + residual_ref[...], rank)
+    for step, sent_ref in enumerate(sent_refs, 1):
+        sent_ref[...] = slab_of(total, rank ^ step).astype(jnp.bfloat16)
 
 
 def per_device(
@@ -338,8 +355,6 @@
     experts = local_experts * expert_ranks
     inner = 2
     outer = expert_ranks // inner
-    slab_width = width // tensor_ranks
-    offset = lax.axis_index("tensor") * slab_width
     row_width = -(-(width + 2 * experts) // 128) * 128
 
     def to_outer(values, step):
@@ -406,17 +421,19 @@
     returned = []
     for step, piece in enumerate(sent, 1):
         returned.append(to_outer(piece, step))
-    (mixture,) = call(
-        gather_kernel,
-        [(block, jnp.float32)],
-        (kept, *returned),
+    slab = (sequences, width // tensor_ranks)
+    total, *sent = call(
+        functools.partial(return_kernel, len(returned)),
+        [(slab, jnp.float32)] + [(slab, jnp.bfloat16)] * (tensor_ranks - 1),
+        (residual, kept, *returned),
         flops=half[0] * width,
         moved=half[0] * width * 2,
         limit=2 * MIB,
     )
-    mine, received = exchange(mixture, mixture.astype(jnp.bfloat16), "tensor", tensor_ranks)
-    total = residual + mine + received.astype(jnp.float32)
-    return lax.dynamic_slice_in_dim(total, offset, slab_width, 1).astype(jnp.bfloat16)
+    for step, piece in enumerate(sent, 1):
+        pairs = [(rank, rank ^ step) for rank in range(tensor_ranks)]
+        total = total + lax.ppermute(piece, "tensor", pairs).astype(jnp.float32)
+    return total.astype(jnp.bfloat16)
 
 
 def solution(mesh):

time: 40 us -> 38.6 us (0.965)
  waiting for transfers between devices: 15.7 us -> 14.8 us
  Pallas kernels: 8.94 us -> 8.47 us
    ppermute x2 -> x1, waiting for transfers between devices: 4.3 us -> 1.72 us  [exchange(): received = lax.ppermute(sent, axis, pairs)]
    ppermute x0 -> x1, waiting for transfers between devices: none -> 2.34 us  [per_device(): total = total + lax.ppermute(piece, 'tensor', pairs).astype(jnp.float32)]
    ppermute x0 -> x1, starting transfers between devices: none -> 1.55 us  [per_device(): total = total + lax.ppermute(piece, 'tensor', pairs).astype(jnp.float32)]
    ppermute x2 -> x1, starting transfers between devices: 4.59 us -> 3.04 us  [exchange(): received = lax.ppermute(sent, axis, pairs)]
    ppermute x6, waiting for transfers between devices: 8.72 us -> 8.01 us  [to_outer(): return lax.ppermute(values, 'expert', pairs)]
    pallas_call x1, Pallas kernels: 5.45 us -> 4.84 us  [attend_and_project(): pl.pallas_call(functools.partial(attend_kernel, pieces), out_shape=[jax.S...]
  transfers between devices with their start and end apart: 10 -> 10, of which waited for: 8 -> 9; matrix products, arithmetic and copies ran while one was open for 1% -> 1% of each run, Pallas kernels for 0% -> 0%
where the time goes in v7:
time: 38.6 us; the launch traced here: 38.4 us
  waiting for transfers between devices  14.8 us (38%)
  starting transfers between devices  14.2 us (37%)
  Pallas kernels  8.47 us (22%)
  other arithmetic  0.81 us (2%)
    ppermute x6, starting transfers between devices, to_outer(): return lax.ppermute(values, 'expert', pairs)  9.29 us
    ppermute x6, waiting for transfers between devices, to_outer(): return lax.ppermute(values, 'expert', pairs)  8.01 us
    pallas_call x1, Pallas kernels, attend_and_project(): pl.pallas_call(functools.partial(attend_kernel, pieces), out_shape=[jax.S...  4.84 us
    pallas_call x5, Pallas kernels, call(): pl.pallas_call(kernel, out_shape=[jax.ShapeDtypeStruct(shape, dtype) for...  3.63 us
    ppermute x1, starting transfers between devices, exchange(): received = lax.ppermute(sent, axis, pairs)  3.04 us
    ppermute x2, waiting for transfers between devices, to_inner(): lax.ppermute(values, 'expert', [(rank, rank ^ 1) for rank in range(expert...  2.71 us
    ppermute x1, waiting for transfers between devices, per_device(): total = total + lax.ppermute(piece, 'tensor', pairs).astype(jnp.float32)  2.34 us
    ppermute x1, waiting for transfers between devices, exchange(): received = lax.ppermute(sent, axis, pairs)  1.72 us
  transfers between devices with their start and end apart: 10, of which 9 were waited for; matrix products, arithmetic and copies ran while one was open for 1% of the time, Pallas kernels for 0%

profile of v7, /device:TPU:0, one launch (start us, length us, event | category | flops | bytes accessed | tf_op | source)
XLA Modules:
  0.0 38.4 jit_solution(6788612323001064913)
XLA Ops:
  0.0 0.0 copy-start.5
  0.0 0.0 copy-start.6
  0.0 0.0 copy-start.7
  0.0 0.0 copy-start.4
  0.0 0.0 copy-start.3
  0.0 4.8 %shard_map.145 = (f32[8,2880]{1,0:T(8,128)S(1)}, bf16[8,2880]{1,0:T(8,128)(2,1)S(1)}) custom-call(s32[8]{0:T(128)} %lengths_hbm.1, bf16[8,16,64]{2,1,0:T(8,128)(2,1)} %queries_hbm.1, bf16[8,4,64]{2,1,0:T(4,128)(2,1)} %new_keys_hbm.1, bf16[8,4,64]{2,1,0:T(4,128)(2,1)} %new_values_hbm.1, bf16[8,256,256]{2,1,0:T(8,128)(2,1)} %bitcast.16, ...), custom_call_target="tpu_custom_call" | custom-call | flops 47185920 | bytes 7995392 | tf_op jit(solution)/shard_map/pallas_call | solution.py:213
  4.9 3.0 %collective-permute-start = (bf16[8,2880]{1,0:T(8,128)(2,1)S(1)}, bf16[8,2880]{1,0:T(8,128)(2,1)S(1)}, u32[]{:S(2)}, u32[]{:S(2)}) collective-permute-start(bf16[8,2880]{1,0:T(8,128)(2,1)S(1)} %get-tuple-element.18), channel_id=1, source_target_pairs={{0,1},{1,0},{2,3},{3,2},{4,5},{5,4},{6,7},{7,6},{8,9},{9,8},{10,11... | collective-permute-start | bytes 138248 | tf_op jit(solution)/shard_map/ppermute | solution.py:251
  7.9 0.0 copy-done.5
  7.9 0.0 copy-done.6
  7.9 0.0 copy-done.7
  8.0 0.1 select_reduce_fusion
  8.1 0.1 pad.2.clone
  8.1 0.1 maximum_maximum_fusion.table_ref
  8.2 0.0 copy-done.4
  8.2 1.7 %collective-permute-done.received_ref = bf16[8,2880]{1,0:T(8,128)(2,1)S(1)} collective-permute-done((bf16[8,2880]{1,0:T(8,128)(2,1)S(1)}, bf16[8,2880]{1,0:T(8,128)(2,1)S(1)}, u32[]{:S(2)}, u32[]{:S(2)}) %collective-permute-start) | collective-permute-done | bytes 46112 | tf_op jit(solution)/shard_map/ppermute | solution.py:251
  9.9 0.0 copy-done.3
  10.0 0.0 copy-start
  10.0 0.0 copy-start.1
  10.0 0.0 copy-start.2
  10.0 0.1 shard_map.146
  10.1 4.2 %collective-permute-start.3 = (bf16[8,2944]{1,0:T(8,128)(2,1)S(1)}, bf16[8,2944]{1,0:T(8,128)(2,1)S(1)}, u32[]{:S(2)}, u32[]{:S(2)}) collective-permute-start(bf16[8,2944]{1,0:T(8,128)(2,1)S(1)} %get-tuple-element.20.refs_0_), channel_id=1, source_target_pairs={{0,12},{2,14},{4,8},{6,10},{8,4},{10,6},{12,0},{14,2},{1,13},{3,15... | collective-permute-start | bytes 141320 | tf_op jit(solution)/shard_map/ppermute | solution.py:362
  14.3 0.0 collective-permute-start.2
  14.3 0.6 %collective-permute-start.1 = (bf16[8,2944]{1,0:T(8,128)(2,1)S(1)}, bf16[8,2944]{1,0:T(8,128)(2,1)S(1)}, u32[]{:S(2)}, u32[]{:S(2)}) collective-permute-start(bf16[8,2944]{1,0:T(8,128)(2,1)S(1)} %get-tuple-element.20.refs_0_), channel_id=1, source_target_pairs={{0,4},{2,6},{4,0},{6,2},{8,12},{10,14},{12,8},{14,10},{1,5},{3,7},... | collective-permute-start | bytes 141320 | tf_op jit(solution)/shard_map/ppermute | solution.py:362
  14.9 1.4 %collective-permute-done.3.refs_3_ = bf16[8,2944]{1,0:T(8,128)(2,1)S(1)} collective-permute-done((bf16[8,2944]{1,0:T(8,128)(2,1)S(1)}, bf16[8,2944]{1,0:T(8,128)(2,1)S(1)}, u32[]{:S(2)}, u32[]{:S(2)}) %collective-permute-start.3) | collective-permute-done | bytes 47136 | tf_op jit(solution)/shard_map/ppermute | solution.py:362
  16.3 2.9 %collective-permute-done.2.refs_2_ = bf16[8,2944]{1,0:T(8,128)(2,1)S(1)} collective-permute-done((bf16[8,2944]{1,0:T(8,128)(2,1)S(1)}, bf16[8,2944]{1,0:T(8,128)(2,1)S(1)}, u32[]{:S(2)}, u32[]{:S(2)}) %collective-permute-start.2) | collective-permute-done | bytes 47136 | tf_op jit(solution)/shard_map/ppermute | solution.py:362
  19.3 0.0 collective-permute-done.1.refs_1_
  19.3 0.1 collective-permute-start.4
  19.4 1.4 %collective-permute-done.4.refs_1_ = bf16[32,2944]{1,0:T(8,128)(2,1)S(1)} collective-permute-done((bf16[32,2944]{1,0:T(8,128)(2,1)S(1)}, bf16[32,2944]{1,0:T(8,128)(2,1)S(1)}, u32[]{:S(2)}, u32[]{:S(2)}) %collective-permute-start.4) | collective-permute-done | bytes 188448 | tf_op jit(solution)/shard_map/ppermute | solution.py:365
  20.8 0.0 copy-done
  20.8 0.0 copy-done.1
  20.8 0.0 copy-done.2
  20.8 3.3 %shard_map.148 = (f32[32,2880]{1,0:T(8,128)S(1)}, bf16[32,2880]{1,0:T(8,128)(2,1)S(1)}) custom-call(bf16[32,2944]{1,0:T(8,128)(2,1)S(1)} %shard_map.147.refs_0_, bf16[32,2944]{1,0:T(8,128)(2,1)S(1)} %collective-permute-done.4.refs_1_, bf16[1,720,2880]{2,1,0:T(8,128)(2,1)S(1)} %bitcast.13, bf16[1,720,2880]{2,1,0:T(8,128)(2,1)S(1)} %bitcast.14, ...), custom_call_target="tpu_custom_call" | custom-call | flops 796262400 | bytes 12441600 | tf_op jit(solution)/shard_map/pallas_call | solution.py:55
  24.1 0.2 collective-permute-start.5
  24.3 1.3 %collective-permute-done.5.received_ref = bf16[32,2880]{1,0:T(8,128)(2,1)S(1)} collective-permute-done((bf16[32,2880]{1,0:T(8,128)(2,1)S(1)}, bf16[32,2880]{1,0:T(8,128)(2,1)S(1)}, u32[]{:S(2)}, u32[]{:S(2)}) %collective-permute-start.5) | collective-permute-done | bytes 184352 | tf_op jit(solution)/shard_map/ppermute | solution.py:365
  25.6 0.2 collective-permute-start.6
  25.8 2.0 %collective-permute-start.7 = (bf16[8,2880]{1,0:T(8,128)(2,1)S(1)}, bf16[8,2880]{1,0:T(8,128)(2,1)S(1)}, u32[]{:S(2)}, u32[]{:S(2)}) collective-permute-start(bf16[8,2880]{1,0:T(8,128)(2,1)S(1)} %get-tuple-element.25), channel_id=1, source_target_pairs={{0,8},{2,10},{4,12},{6,14},{8,0},{10,2},{12,4},{14,6},{1,9},{3,11}... | collective-permute-start | bytes 138248 | tf_op jit(solution)/shard_map/ppermute | solution.py:362
  27.8 2.3 %collective-permute-start.8 = (bf16[8,2880]{1,0:T(8,128)(2,1)S(1)}, bf16[8,2880]{1,0:T(8,128)(2,1)S(1)}, u32[]{:S(2)}, u32[]{:S(2)}) collective-permute-start(bf16[8,2880]{1,0:T(8,128)(2,1)S(1)} %get-tuple-element.26), channel_id=1, source_target_pairs={{0,12},{2,14},{4,8},{6,10},{8,4},{10,6},{12,0},{14,2},{1,13},{3,15... | collective-permute-start | bytes 138248 | tf_op jit(solution)/shard_map/ppermute | solution.py:362
  30.1 0.2 collective-permute-done.6.refs_1_
  30.3 1.0 %collective-permute-done.7.refs_2_ = bf16[8,2880]{1,0:T(8,128)(2,1)S(1)} collective-permute-done((bf16[8,2880]{1,0:T(8,128)(2,1)S(1)}, bf16[8,2880]{1,0:T(8,128)(2,1)S(1)}, u32[]{:S(2)}, u32[]{:S(2)}) %collective-permute-start.7) | collective-permute-done | bytes 46112 | tf_op jit(solution)/shard_map/ppermute | solution.py:362
  31.2 2.5 %collective-permute-done.8.refs_3_ = bf16[8,2880]{1,0:T(8,128)(2,1)S(1)} collective-permute-done((bf16[8,2880]{1,0:T(8,128)(2,1)S(1)}, bf16[8,2880]{1,0:T(8,128)(2,1)S(1)}, u32[]{:S(2)}, u32[]{:S(2)}) %collective-permute-start.8) | collective-permute-done | bytes 46112 | tf_op jit(solution)/shard_map/ppermute | solution.py:362
  33.8 0.2 shard_map.150
  33.9 1.6 %collective-permute-start.9 = (bf16[8,1440]{1,0:T(8,128)(2,1)S(1)}, bf16[8,1440]{1,0:T(8,128)(2,1)S(1)}, u32[]{:S(2)}, u32[]{:S(2)}) collective-permute-start(bf16[8,1440]{1,0:T(8,128)(2,1)S(1)} %get-tuple-element.28), channel_id=1, source_target_pairs={{0,1},{1,0},{2,3},{3,2},{4,5},{5,4},{6,7},{7,6},{8,9},{9,8},{10,11... | collective-permute-start | bytes 69128 | tf_op jit(solution)/shard_map/ppermute | solution.py:435
  35.5 2.3 %collective-permute-done.9 = bf16[8,1440]{1,0:T(8,128)(2,1)S(1)} collective-permute-done((bf16[8,1440]{1,0:T(8,128)(2,1)S(1)}, bf16[8,1440]{1,0:T(8,128)(2,1)S(1)}, u32[]{:S(2)}, u32[]{:S(2)}) %collective-permute-start.9) | collective-permute-done | bytes 23072 | tf_op jit(solution)/shard_map/ppermute | solution.py:435
  37.8 0.6 %add_convert_fusion = bf16[8,1440]{1,0:T(8,128)(2,1)} fusion(f32[8,1440]{1,0:T(8,128)S(1)} %get-tuple-element.27, bf16[8,1440]{1,0:T(8,128)(2,1)S(1)} %collective-permute-done.9), kind=kLoop, calls=%fused_computation | loop fusion | flops 34560 | bytes 92160 | tf_op jit(solution)/shard_map/convert_element_type | solution.py:436
  (8 shorter events, 0.1 us)
Async XLA Ops:
  0.0 7.9 %copy-start.5 = (f32[8,4]{0,1:T(4,128)S(1)}, f32[8,4]{0,1:T(4,128)}, u32[]{:S(2)}) copy-start(f32[8,4]{0,1:T(4,128)} %param.25) | copy-start | bytes 388
  0.0 7.9 %copy-start.6 = (s32[8,4]{0,1:T(4,128)S(1)}, s32[8,4]{0,1:T(4,128)}, u32[]{:S(2)}) copy-start(s32[8,4]{0,1:T(4,128)} %param.26) | copy-start | bytes 388
  0.0 7.9 %copy-start.7 = (s32[8,4]{0,1:T(4,128)S(1)}, s32[8,4]{0,1:T(4,128)}, u32[]{:S(2)}) copy-start(s32[8,4]{0,1:T(4,128)} %param.24) | copy-start | bytes 388
  0.0 8.2 %copy-start.4 = (f32[2880]{0:T(1024)S(1)}, f32[2880]{0:T(1024)}, u32[]{:S(2)}) copy-start(f32[2880]{0:T(1024)} %param.23) | copy-start | bytes 34564
  0.0 9.9 %copy-start.3 = (bf16[8,2880]{1,0:T(8,128)(2,1)S(1)}, bf16[8,2880]{1,0:T(8,128)(2,1)}, u32[]{:S(2)}) copy-start(bf16[8,2880]{1,0:T(8,128)(2,1)} %hidden_ref.1) | copy-start | bytes 138244
  4.9 5.1 %collective-permute-start = (bf16[8,2880]{1,0:T(8,128)(2,1)S(1)}, bf16[8,2880]{1,0:T(8,128)(2,1)S(1)}, u32[]{:S(2)}, u32[]{:S(2)}) collective-permute-start(bf16[8,2880]{1,0:T(8,128)(2,1)S(1)} %get-tuple-element.18), channel_id=1, source_target_pairs={{0,1},{1,0},{2,3},{3,2},{4,5},{5,4},{6,7},{7,6},{8,9},{9,8},{10,11... | collective-permute-start | bytes 138248 | tf_op jit(solution)/shard_map/ppermute | solution.py:251
  10.0 10.8 %copy-start = (bf16[1,2880,720]{1,2,0:T(8,128)(2,1)S(1)}, bf16[1,2880,720]{1,2,0:T(8,128)(2,1)}, u32[]{:S(2)}) copy-start(bf16[1,2880,720]{1,2,0:T(8,128)(2,1)} %param.27) | copy-start | bytes 12441604
  10.0 10.8 %copy-start.1 = (bf16[1,2880,720]{1,2,0:T(8,128)(2,1)S(1)}, bf16[1,2880,720]{1,2,0:T(8,128)(2,1)}, u32[]{:S(2)}) copy-start(bf16[1,2880,720]{1,2,0:T(8,128)(2,1)} %param.28) | copy-start | bytes 12441604
  10.0 10.8 %copy-start.2 = (bf16[1,720,2880]{2,1,0:T(8,128)(2,1)S(1)}, bf16[1,720,2880]{2,1,0:T(8,128)(2,1)}, u32[]{:S(2)}) copy-start(bf16[1,720,2880]{2,1,0:T(8,128)(2,1)} %refs_4_.1) | copy-start | bytes 12441604
  10.1 6.2 %collective-permute-start.3 = (bf16[8,2944]{1,0:T(8,128)(2,1)S(1)}, bf16[8,2944]{1,0:T(8,128)(2,1)S(1)}, u32[]{:S(2)}, u32[]{:S(2)}) collective-permute-start(bf16[8,2944]{1,0:T(8,128)(2,1)S(1)} %get-tuple-element.20.refs_0_), channel_id=1, source_target_pairs={{0,12},{2,14},{4,8},{6,10},{8,4},{10,6},{12,0},{14,2},{1,13},{3,15... | collective-permute-start | bytes 141320 | tf_op jit(solution)/shard_map/ppermute | solution.py:362
  14.3 5.0 %collective-permute-start.2 = (bf16[8,2944]{1,0:T(8,128)(2,1)S(1)}, bf16[8,2944]{1,0:T(8,128)(2,1)S(1)}, u32[]{:S(2)}, u32[]{:S(2)}) collective-permute-start(bf16[8,2944]{1,0:T(8,128)(2,1)S(1)} %get-tuple-element.20.refs_0_), channel_id=1, source_target_pairs={{0,8},{2,10},{4,12},{6,14},{8,0},{10,2},{12,4},{14,6},{1,9},{3,11}... | collective-permute-start | bytes 141320 | tf_op jit(solution)/shard_map/ppermute | solution.py:362
  14.3 5.0 %collective-permute-start.1 = (bf16[8,2944]{1,0:T(8,128)(2,1)S(1)}, bf16[8,2944]{1,0:T(8,128)(2,1)S(1)}, u32[]{:S(2)}, u32[]{:S(2)}) collective-permute-start(bf16[8,2944]{1,0:T(8,128)(2,1)S(1)} %get-tuple-element.20.refs_0_), channel_id=1, source_target_pairs={{0,4},{2,6},{4,0},{6,2},{8,12},{10,14},{12,8},{14,10},{1,5},{3,7},... | collective-permute-start | bytes 141320 | tf_op jit(solution)/shard_map/ppermute | solution.py:362
  19.3 1.5 %collective-permute-start.4 = (bf16[32,2944]{1,0:T(8,128)(2,1)S(1)}, bf16[32,2944]{1,0:T(8,128)(2,1)S(1)}, u32[]{:S(2)}, u32[]{:S(2)}) collective-permute-start(bf16[32,2944]{1,0:T(8,128)(2,1)S(1)} %shard_map.147.refs_0_), channel_id=1, source_target_pairs={{0,2},{2,0},{4,6},{6,4},{8,10},{10,8},{12,14},{14,12},{1,3},{3,1},... | collective-permute-start | bytes 565256 | tf_op jit(solution)/shard_map/ppermute | solution.py:365
  24.1 1.5 %collective-permute-start.5 = (bf16[32,2880]{1,0:T(8,128)(2,1)S(1)}, bf16[32,2880]{1,0:T(8,128)(2,1)S(1)}, u32[]{:S(2)}, u32[]{:S(2)}) collective-permute-start(bf16[32,2880]{1,0:T(8,128)(2,1)S(1)} %get-tuple-element.22), channel_id=1, source_target_pairs={{0,2},{2,0},{4,6},{6,4},{8,10},{10,8},{12,14},{14,12},{1,3},{3,1},... | collective-permute-start | bytes 552968 | tf_op jit(solution)/shard_map/ppermute | solution.py:365
  25.6 4.6 %collective-permute-start.6 = (bf16[8,2880]{1,0:T(8,128)(2,1)S(1)}, bf16[8,2880]{1,0:T(8,128)(2,1)S(1)}, u32[]{:S(2)}, u32[]{:S(2)}) collective-permute-start(bf16[8,2880]{1,0:T(8,128)(2,1)S(1)} %get-tuple-element.24), channel_id=1, source_target_pairs={{0,4},{2,6},{4,0},{6,2},{8,12},{10,14},{12,8},{14,10},{1,5},{3,7},... | collective-permute-start | bytes 138248 | tf_op jit(solution)/shard_map/ppermute | solution.py:362
  25.8 5.4 %collective-permute-start.7 = (bf16[8,2880]{1,0:T(8,128)(2,1)S(1)}, bf16[8,2880]{1,0:T(8,128)(2,1)S(1)}, u32[]{:S(2)}, u32[]{:S(2)}) collective-permute-start(bf16[8,2880]{1,0:T(8,128)(2,1)S(1)} %get-tuple-element.25), channel_id=1, source_target_pairs={{0,8},{2,10},{4,12},{6,14},{8,0},{10,2},{12,4},{14,6},{1,9},{3,11}... | collective-permute-start | bytes 138248 | tf_op jit(solution)/shard_map/ppermute | solution.py:362
  27.8 6.0 %collective-permute-start.8 = (bf16[8,2880]{1,0:T(8,128)(2,1)S(1)}, bf16[8,2880]{1,0:T(8,128)(2,1)S(1)}, u32[]{:S(2)}, u32[]{:S(2)}) collective-permute-start(bf16[8,2880]{1,0:T(8,128)(2,1)S(1)} %get-tuple-element.26), channel_id=1, source_target_pairs={{0,12},{2,14},{4,8},{6,10},{8,4},{10,6},{12,0},{14,2},{1,13},{3,15... | collective-permute-start | bytes 138248 | tf_op jit(solution)/shard_map/ppermute | solution.py:362
  33.9 3.9 %collective-permute-start.9 = (bf16[8,1440]{1,0:T(8,128)(2,1)S(1)}, bf16[8,1440]{1,0:T(8,128)(2,1)S(1)}, u32[]{:S(2)}, u32[]{:S(2)}) collective-permute-start(bf16[8,1440]{1,0:T(8,128)(2,1)S(1)} %get-tuple-element.28), channel_id=1, source_target_pairs={{0,1},{1,0},{2,3},{3,2},{4,5},{5,4},{6,7},{7,6},{8,9},{9,8},{10,11... | collective-permute-start | bytes 69128 | tf_op jit(solution)/shard_map/ppermute | solution.py:435

commit v8 on v7

--- a/solution.py
+++ b/solution.py
@@ -47,7 +47,6 @@
 
 VMEM = pl.BlockSpec(memory_space=pltpu.VMEM)
 LAST_DIMS = (((1,), (1,)), ((), ()))
-FIRST_DIMS = (((0,), (0,)), ((), ()))
 MIB = 1 << 20
 
 
@@ -269,10 +268,28 @@
 
 
 def pack_kernel(*refs):
-    *piece_refs, packed_ref = refs
+    *piece_refs, _, packed_ref = refs
     size = piece_refs[0].shape[0]
     for number, piece_ref in enumerate(piece_refs):
         packed_ref[pl.ds(number * size, size)] = piece_ref[...]
+
+
+def turn_kernel(source_ref, target_ref):
+    for local in range(source_ref.shape[0]):
+        target_ref[local] = source_ref[local].T
+
+
+def turn(weight):
+    count, _, _ = weight.shape
+    (turned,) = call(
+        turn_kernel,
+        [(weight.shape, weight.dtype)],
+        (weight.swapaxes(1, 2),),
+        flops=count,
+        moved=count,
+        limit=6 * MIB,
+    )
+    return turned
 
 
 def expert_kernel(experts, *refs):
@@ -286,14 +303,10 @@
         expert = lax.axis_index("expert") * local_experts + local
         chosen = (column == expert) | (column == expert + experts)
         weight = jnp.sum(jnp.where(chosen, table, 0.0), axis=1, keepdims=True)
-        gate = lax.dot_general(
-            gate_ref[local], rows, LAST_DIMS, preferred_element_type=jnp.float32
-        )
-        up = lax.dot_general(up_ref[local], rows, LAST_DIMS, preferred_element_type=jnp.float32)
+        gate = mm(rows, gate_ref[local])
+        up = mm(rows, up_ref[local])
         active = (gate * jax.nn.sigmoid(GLU_SLOPE * gate) * (up + 1.0)).astype(jnp.bfloat16)
-        part = lax.dot_general(
-            active, down_ref[local], FIRST_DIMS, preferred_element_type=jnp.float32
-        )
+        part = mm(active, down_ref[local])
         part = part * weight
         total = part if total is None else total + part
     half = mine_ref.shape[0]
@@ -391,20 +404,22 @@
     near = [rows]
     for step in range(1, outer):
         near.append(to_outer(rows, step))
+    gate_weight = turn(gate_weight)
     (near,) = call(
         pack_kernel,
         [((outer * sequences, row_width), jnp.bfloat16)],
-        near,
+        (*near, down_weight),
         flops=sequences,
         moved=4 * outer * sequences * row_width,
         limit=2 * MIB,
     )
     far = to_inner(near)
+    up_weight = turn(up_weight)
     half = (outer * sequences, width)
     mine, other = call(
         functools.partial(expert_kernel, experts),
         [(half, jnp.float32), (half, jnp.bfloat16)],
-        (near, far, gate_weight.swapaxes(1, 2), up_weight.swapaxes(1, 2), down_weight),
+        (near, far, gate_weight, up_weight, down_weight),
         flops=12 * half[0] * width * hidden_units * local_experts,
         moved=6 * width * hidden_units * local_experts,
         limit=16 * MIB,

time: 38.6 us -> 39.6 us (1.026)
  Pallas kernels: 8.47 us -> 10 us
  waiting for transfers between devices: 14.8 us -> 13.5 us
  local copies, waits for them, and re-layouts: 0.12 us -> 0.95 us
    pallas_call x5 -> x7, Pallas kernels: 3.63 us -> 5.17 us  [call(): pl.pallas_call(kernel, out_shape=[jax.ShapeDtypeStruct(shape, dtype) for...]
    ppermute x2, waiting for transfers between devices: 2.71 us -> 1.42 us  [to_inner(): lax.ppermute(values, 'expert', [(rank, rank ^ 1) for rank in range(expert...]
    unnamed x16 -> x18, local copies, waits for them, and re-layouts: 0.03 us -> 0.86 us
  transfers between devices with their start and end apart: 10 -> 10, of which waited for: 9 -> 8; matrix products, arithmetic and copies ran while one was open for 1% -> 1% of each run, Pallas kernels for 0% -> 6%
where the time goes in v8:
time: 39.6 us; the launch traced here: 39.4 us
  starting transfers between devices  14 us (35%)
  waiting for transfers between devices  13.5 us (34%)
  Pallas kernels  10 us (25%)
  local copies, waits for them, and re-layouts  0.95 us (2%)
  other arithmetic  0.81 us (2%)
    ppermute x6, starting transfers between devices, to_outer(): return lax.ppermute(values, 'expert', pairs)  9.29 us
    ppermute x6, waiting for transfers between devices, to_outer(): return lax.ppermute(values, 'expert', pairs)  8 us
    pallas_call x7, Pallas kernels, call(): pl.pallas_call(kernel, out_shape=[jax.ShapeDtypeStruct(shape, dtype) for...  5.17 us
    pallas_call x1, Pallas kernels, attend_and_project(): pl.pallas_call(functools.partial(attend_kernel, pieces), out_shape=[jax.S...  4.84 us
    ppermute x1, starting transfers between devices, exchange(): received = lax.ppermute(sent, axis, pairs)  3.04 us
    ppermute x1, waiting for transfers between devices, per_device(): total = total + lax.ppermute(piece, 'tensor', pairs).astype(jnp.float32)  2.34 us
    ppermute x1, waiting for transfers between devices, exchange(): received = lax.ppermute(sent, axis, pairs)  1.72 us
    ppermute x1, starting transfers between devices, per_device(): total = total + lax.ppermute(piece, 'tensor', pairs).astype(jnp.float32)  1.55 us
  transfers between devices with their start and end apart: 10, of which 8 were waited for; matrix products, arithmetic and copies ran while one was open for 1% of the time, Pallas kernels for 6%

profile of v8, /device:TPU:0, one launch (start us, length us, event | category | flops | bytes accessed | tf_op | source)
XLA Modules:
  0.0 39.4 jit_solution(12764227192984777492)
XLA Ops:
  0.0 0.0 copy-start.4
  0.0 0.0 copy-start.5
  0.0 0.0 copy-start.6
  0.0 0.0 copy-start.3
  0.0 0.0 copy-start.2
  0.0 4.8 %shard_map.145 = (f32[8,2880]{1,0:T(8,128)S(1)}, bf16[8,2880]{1,0:T(8,128)(2,1)S(1)}) custom-call(s32[8]{0:T(128)} %lengths_hbm.1, bf16[8,16,64]{2,1,0:T(8,128)(2,1)} %queries_hbm.1, bf16[8,4,64]{2,1,0:T(4,128)(2,1)} %new_keys_hbm.1, bf16[8,4,64]{2,1,0:T(4,128)(2,1)} %new_values_hbm.1, bf16[8,256,256]{2,1,0:T(8,128)(2,1)} %bitcast.18, ...), custom_call_target="tpu_custom_call" | custom-call | flops 47185920 | bytes 7995392 | tf_op jit(solution)/shard_map/pallas_call | solution.py:212
  4.9 3.0 %collective-permute-start = (bf16[8,2880]{1,0:T(8,128)(2,1)S(1)}, bf16[8,2880]{1,0:T(8,128)(2,1)S(1)}, u32[]{:S(2)}, u32[]{:S(2)}) collective-permute-start(bf16[8,2880]{1,0:T(8,128)(2,1)S(1)} %get-tuple-element.18), channel_id=1, source_target_pairs={{0,1},{1,0},{2,3},{3,2},{4,5},{5,4},{6,7},{7,6},{8,9},{9,8},{10,11... | collective-permute-start | bytes 138248 | tf_op jit(solution)/shard_map/ppermute | solution.py:250
  7.9 0.0 copy-done.4
  7.9 0.0 copy-done.5
  7.9 0.0 copy-done.6
  8.0 0.1 select_reduce_fusion
  8.1 0.1 pad.2.clone
  8.1 0.1 maximum_maximum_fusion.table_ref
  8.2 0.0 copy-done.3
  8.2 1.7 %collective-permute-done.received_ref = bf16[8,2880]{1,0:T(8,128)(2,1)S(1)} collective-permute-done((bf16[8,2880]{1,0:T(8,128)(2,1)S(1)}, bf16[8,2880]{1,0:T(8,128)(2,1)S(1)}, u32[]{:S(2)}, u32[]{:S(2)}) %collective-permute-start) | collective-permute-done | bytes 46112 | tf_op jit(solution)/shard_map/ppermute | solution.py:250
  9.9 0.0 copy-done.2
  10.0 0.0 copy-start
  10.0 0.1 shard_map.146
  10.1 0.0 copy-start.1
  10.1 4.2 %collective-permute-start.3 = (bf16[8,2944]{1,0:T(8,128)(2,1)S(1)}, bf16[8,2944]{1,0:T(8,128)(2,1)S(1)}, u32[]{:S(2)}, u32[]{:S(2)}) collective-permute-start(bf16[8,2944]{1,0:T(8,128)(2,1)S(1)} %get-tuple-element.20.refs_0_), channel_id=1, source_target_pairs={{0,12},{2,14},{4,8},{6,10},{8,4},{10,6},{12,0},{14,2},{1,13},{3,15... | collective-permute-start | bytes 141320 | tf_op jit(solution)/shard_map/ppermute | solution.py:375
  14.3 0.0 collective-permute-start.2
  14.3 0.6 %collective-permute-start.1 = (bf16[8,2944]{1,0:T(8,128)(2,1)S(1)}, bf16[8,2944]{1,0:T(8,128)(2,1)S(1)}, u32[]{:S(2)}, u32[]{:S(2)}) collective-permute-start(bf16[8,2944]{1,0:T(8,128)(2,1)S(1)} %get-tuple-element.20.refs_0_), channel_id=1, source_target_pairs={{0,4},{2,6},{4,0},{6,2},{8,12},{10,14},{12,8},{14,10},{1,5},{3,7},... | collective-permute-start | bytes 141320 | tf_op jit(solution)/shard_map/ppermute | solution.py:375
  14.9 1.4 %collective-permute-done.3.refs_3_ = bf16[8,2944]{1,0:T(8,128)(2,1)S(1)} collective-permute-done((bf16[8,2944]{1,0:T(8,128)(2,1)S(1)}, bf16[8,2944]{1,0:T(8,128)(2,1)S(1)}, u32[]{:S(2)}, u32[]{:S(2)}) %collective-permute-start.3) | collective-permute-done | bytes 47136 | tf_op jit(solution)/shard_map/ppermute | solution.py:375
  16.3 2.9 %collective-permute-done.2.refs_2_ = bf16[8,2944]{1,0:T(8,128)(2,1)S(1)} collective-permute-done((bf16[8,2944]{1,0:T(8,128)(2,1)S(1)}, bf16[8,2944]{1,0:T(8,128)(2,1)S(1)}, u32[]{:S(2)}, u32[]{:S(2)}) %collective-permute-start.2) | collective-permute-done | bytes 47136 | tf_op jit(solution)/shard_map/ppermute | solution.py:375
  19.3 0.0 collective-permute-done.1.refs_1_
  19.3 0.0 copy-done
  19.3 0.0 slice-start
  19.3 0.1 collective-permute-start.4
  19.4 0.0 copy-done.1
  19.4 0.0 slice-start.1
  19.4 1.3 %shard_map.148.refs_2_ = bf16[1,2880,720]{2,1,0:T(8,128)(2,1)S(1)} custom-call(bf16[1,720,2880]{2,1,0:T(8,128)(2,1)S(1)} %bitcast.13), custom_call_target="tpu_custom_call" | custom-call | flops 1 | bytes 1 | tf_op jit(solution)/shard_map/pallas_call | solution.py:54
  20.7 0.8 %slice-done = s8[4194304]{0:T(1024)(128)(4,1)S(1)} async-done(((s8[4239360]{0:T(1024)(128)(4,1)}), s8[4194304]{0:T(1024)(128)(4,1)S(1)}, s32[]{:S(2)}) %slice-start) | async-done | bytes 4194328
  21.5 0.0 slice-done.1
  21.5 1.2 %shard_map.149.refs_3_ = bf16[1,2880,720]{2,1,0:T(8,128)(2,1)S(1)} custom-call(bf16[1,720,2880]{2,1,0:T(8,128)(2,1)S(1)} %bitcast.16), custom_call_target="tpu_custom_call" | custom-call | flops 1 | bytes 1 | tf_op jit(solution)/shard_map/pallas_call | solution.py:54
  22.7 0.0 collective-permute-done.4.refs_1_
  22.7 2.3 %shard_map.150 = (f32[32,2880]{1,0:T(8,128)S(1)}, bf16[32,2880]{1,0:T(8,128)(2,1)S(1)}) custom-call(bf16[32,2944]{1,0:T(8,128)(2,1)S(1)} %shard_map.147.refs_0_, bf16[32,2944]{1,0:T(8,128)(2,1)S(1)} %collective-permute-done.4.refs_1_, bf16[1,2880,720]{2,1,0:T(8,128)(2,1)S(1)} %shard_map.148.refs_2_, bf16[1,2880,720]{2,1,0:T(8,128)(2,1)S(1)} %shard_map.149.refs_3_, ...), custom_call_target="tpu_custom_call" | custom-call | flops 796262400 | bytes 12441600 | tf_op jit(solution)/shard_map/pallas_call | solution.py:54
  25.1 0.1 collective-permute-start.5
  25.2 1.4 %collective-permute-done.5.received_ref = bf16[32,2880]{1,0:T(8,128)(2,1)S(1)} collective-permute-done((bf16[32,2880]{1,0:T(8,128)(2,1)S(1)}, bf16[32,2880]{1,0:T(8,128)(2,1)S(1)}, u32[]{:S(2)}, u32[]{:S(2)}) %collective-permute-start.5) | collective-permute-done | bytes 184352 | tf_op jit(solution)/shard_map/ppermute | solution.py:378
  26.6 0.2 collective-permute-start.6
  26.8 2.0 %collective-permute-start.7 = (bf16[8,2880]{1,0:T(8,128)(2,1)S(1)}, bf16[8,2880]{1,0:T(8,128)(2,1)S(1)}, u32[]{:S(2)}, u32[]{:S(2)}) collective-permute-start(bf16[8,2880]{1,0:T(8,128)(2,1)S(1)} %get-tuple-element.25), channel_id=1, source_target_pairs={{0,8},{2,10},{4,12},{6,14},{8,0},{10,2},{12,4},{14,6},{1,9},{3,11}... | collective-permute-start | bytes 138248 | tf_op jit(solution)/shard_map/ppermute | solution.py:375
  28.8 2.3 %collective-permute-start.8 = (bf16[8,2880]{1,0:T(8,128)(2,1)S(1)}, bf16[8,2880]{1,0:T(8,128)(2,1)S(1)}, u32[]{:S(2)}, u32[]{:S(2)}) collective-permute-start(bf16[8,2880]{1,0:T(8,128)(2,1)S(1)} %get-tuple-element.26), channel_id=1, source_target_pairs={{0,12},{2,14},{4,8},{6,10},{8,4},{10,6},{12,0},{14,2},{1,13},{3,15... | collective-permute-start | bytes 138248 | tf_op jit(solution)/shard_map/ppermute | solution.py:375
  31.1 0.2 collective-permute-done.6.refs_1_
  31.3 1.0 %collective-permute-done.7.refs_2_ = bf16[8,2880]{1,0:T(8,128)(2,1)S(1)} collective-permute-done((bf16[8,2880]{1,0:T(8,128)(2,1)S(1)}, bf16[8,2880]{1,0:T(8,128)(2,1)S(1)}, u32[]{:S(2)}, u32[]{:S(2)}) %collective-permute-start.7) | collective-permute-done | bytes 46112 | tf_op jit(solution)/shard_map/ppermute | solution.py:375
  32.2 2.5 %collective-permute-done.8.refs_3_ = bf16[8,2880]{1,0:T(8,128)(2,1)S(1)} collective-permute-done((bf16[8,2880]{1,0:T(8,128)(2,1)S(1)}, bf16[8,2880]{1,0:T(8,128)(2,1)S(1)}, u32[]{:S(2)}, u32[]{:S(2)}) %collective-permute-start.8) | collective-permute-done | bytes 46112 | tf_op jit(solution)/shard_map/ppermute | solution.py:375
  34.8 0.2 shard_map.152
  34.9 1.5 %collective-permute-start.9 = (bf16[8,1440]{1,0:T(8,128)(2,1)S(1)}, bf16[8,1440]{1,0:T(8,128)(2,1)S(1)}, u32[]{:S(2)}, u32[]{:S(2)}) collective-permute-start(bf16[8,1440]{1,0:T(8,128)(2,1)S(1)} %get-tuple-element.28), channel_id=1, source_target_pairs={{0,1},{1,0},{2,3},{3,2},{4,5},{5,4},{6,7},{7,6},{8,9},{9,8},{10,11... | collective-permute-start | bytes 69128 | tf_op jit(solution)/shard_map/ppermute | solution.py:450
  36.5 2.3 %collective-permute-done.9 = bf16[8,1440]{1,0:T(8,128)(2,1)S(1)} collective-permute-done((bf16[8,1440]{1,0:T(8,128)(2,1)S(1)}, bf16[8,1440]{1,0:T(8,128)(2,1)S(1)}, u32[]{:S(2)}, u32[]{:S(2)}) %collective-permute-start.9) | collective-permute-done | bytes 23072 | tf_op jit(solution)/shard_map/ppermute | solution.py:450
  38.8 0.6 %add_convert_fusion = bf16[8,1440]{1,0:T(8,128)(2,1)} fusion(f32[8,1440]{1,0:T(8,128)S(1)} %get-tuple-element.27, bf16[8,1440]{1,0:T(8,128)(2,1)S(1)} %collective-permute-done.9), kind=kLoop, calls=%fused_computation | loop fusion | flops 34560 | bytes 92160 | tf_op jit(solution)/shard_map/convert_element_type | solution.py:451
  (9 shorter events, 0.1 us)
Async XLA Ops:
  0.0 7.9 %copy-start.4 = (f32[8,4]{0,1:T(4,128)S(1)}, f32[8,4]{0,1:T(4,128)}, u32[]{:S(2)}) copy-start(f32[8,4]{0,1:T(4,128)} %param.25) | copy-start | bytes 388
  0.0 7.9 %copy-start.5 = (s32[8,4]{0,1:T(4,128)S(1)}, s32[8,4]{0,1:T(4,128)}, u32[]{:S(2)}) copy-start(s32[8,4]{0,1:T(4,128)} %param.26) | copy-start | bytes 388
  0.0 7.9 %copy-start.6 = (s32[8,4]{0,1:T(4,128)S(1)}, s32[8,4]{0,1:T(4,128)}, u32[]{:S(2)}) copy-start(s32[8,4]{0,1:T(4,128)} %param.24) | copy-start | bytes 388
  0.0 8.2 %copy-start.3 = (f32[2880]{0:T(1024)S(1)}, f32[2880]{0:T(1024)}, u32[]{:S(2)}) copy-start(f32[2880]{0:T(1024)} %param.23) | copy-start | bytes 34564
  0.0 9.9 %copy-start.2 = (bf16[8,2880]{1,0:T(8,128)(2,1)S(1)}, bf16[8,2880]{1,0:T(8,128)(2,1)}, u32[]{:S(2)}) copy-start(bf16[8,2880]{1,0:T(8,128)(2,1)} %hidden_ref.1) | copy-start | bytes 138244
  4.9 5.1 %collective-permute-start = (bf16[8,2880]{1,0:T(8,128)(2,1)S(1)}, bf16[8,2880]{1,0:T(8,128)(2,1)S(1)}, u32[]{:S(2)}, u32[]{:S(2)}) collective-permute-start(bf16[8,2880]{1,0:T(8,128)(2,1)S(1)} %get-tuple-element.18), channel_id=1, source_target_pairs={{0,1},{1,0},{2,3},{3,2},{4,5},{5,4},{6,7},{7,6},{8,9},{9,8},{10,11... | collective-permute-start | bytes 138248 | tf_op jit(solution)/shard_map/ppermute | solution.py:250
  10.0 9.3 %copy-start = (bf16[1,720,2880]{2,1,0:T(8,128)(2,1)S(1)}, bf16[1,720,2880]{2,1,0:T(8,128)(2,1)}, u32[]{:S(2)}) copy-start(bf16[1,720,2880]{2,1,0:T(8,128)(2,1)} %refs_4_.3) | copy-start | bytes 12441604
  10.1 9.3 %copy-start.1 = (bf16[1,2880,720]{1,2,0:T(8,128)(2,1)S(1)}, bf16[1,2880,720]{1,2,0:T(8,128)(2,1)}, u32[]{:S(2)}) copy-start(bf16[1,2880,720]{1,2,0:T(8,128)(2,1)} %param.27) | copy-start | bytes 12441604
  10.1 6.2 %collective-permute-start.3 = (bf16[8,2944]{1,0:T(8,128)(2,1)S(1)}, bf16[8,2944]{1,0:T(8,128)(2,1)S(1)}, u32[]{:S(2)}, u32[]{:S(2)}) collective-permute-start(bf16[8,2944]{1,0:T(8,128)(2,1)S(1)} %get-tuple-element.20.refs_0_), channel_id=1, source_target_pairs={{0,12},{2,14},{4,8},{6,10},{8,4},{10,6},{12,0},{14,2},{1,13},{3,15... | collective-permute-start | bytes 141320 | tf_op jit(solution)/shard_map/ppermute | solution.py:375
  14.3 5.0 %collective-permute-start.2 = (bf16[8,2944]{1,0:T(8,128)(2,1)S(1)}, bf16[8,2944]{1,0:T(8,128)(2,1)S(1)}, u32[]{:S(2)}, u32[]{:S(2)}) collective-permute-start(bf16[8,2944]{1,0:T(8,128)(2,1)S(1)} %get-tuple-element.20.refs_0_), channel_id=1, source_target_pairs={{0,8},{2,10},{4,12},{6,14},{8,0},{10,2},{12,4},{14,6},{1,9},{3,11}... | collective-permute-start | bytes 141320 | tf_op jit(solution)/shard_map/ppermute | solution.py:375
  14.3 5.0 %collective-permute-start.1 = (bf16[8,2944]{1,0:T(8,128)(2,1)S(1)}, bf16[8,2944]{1,0:T(8,128)(2,1)S(1)}, u32[]{:S(2)}, u32[]{:S(2)}) collective-permute-start(bf16[8,2944]{1,0:T(8,128)(2,1)S(1)} %get-tuple-element.20.refs_0_), channel_id=1, source_target_pairs={{0,4},{2,6},{4,0},{6,2},{8,12},{10,14},{12,8},{14,10},{1,5},{3,7},... | collective-permute-start | bytes 141320 | tf_op jit(solution)/shard_map/ppermute | solution.py:375
  19.3 2.2 %slice-start = ((s8[4239360]{0:T(1024)(128)(4,1)}), s8[4194304]{0:T(1024)(128)(4,1)S(1)}, s32[]{:S(2)}) async-start(s8[4239360]{0:T(1024)(128)(4,1)} %bitcast.14), calls=%async_computation | async-start | bytes 8388608
  19.3 3.4 %collective-permute-start.4 = (bf16[32,2944]{1,0:T(8,128)(2,1)S(1)}, bf16[32,2944]{1,0:T(8,128)(2,1)S(1)}, u32[]{:S(2)}, u32[]{:S(2)}) collective-permute-start(bf16[32,2944]{1,0:T(8,128)(2,1)S(1)} %shard_map.147.refs_0_), channel_id=1, source_target_pairs={{0,2},{2,0},{4,6},{6,4},{8,10},{10,8},{12,14},{14,12},{1,3},{3,1},... | collective-permute-start | bytes 565256 | tf_op jit(solution)/shard_map/ppermute | solution.py:378
  19.4 2.1 %slice-start.1 = ((s8[4239360]{0:T(1024)(128)(4,1)}), s8[45056]{0:T(1024)(128)(4,1)S(1)}, s32[]{:S(2)}) async-start(s8[4239360]{0:T(1024)(128)(4,1)} %bitcast.14), calls=%async_computation.1 | async-start | bytes 90112
  25.1 1.5 %collective-permute-start.5 = (bf16[32,2880]{1,0:T(8,128)(2,1)S(1)}, bf16[32,2880]{1,0:T(8,128)(2,1)S(1)}, u32[]{:S(2)}, u32[]{:S(2)}) collective-permute-start(bf16[32,2880]{1,0:T(8,128)(2,1)S(1)} %get-tuple-element.22), channel_id=1, source_target_pairs={{0,2},{2,0},{4,6},{6,4},{8,10},{10,8},{12,14},{14,12},{1,3},{3,1},... | collective-permute-start | bytes 552968 | tf_op jit(solution)/shard_map/ppermute | solution.py:378
  26.6 4.6 %collective-permute-start.6 = (bf16[8,2880]{1,0:T(8,128)(2,1)S(1)}, bf16[8,2880]{1,0:T(8,128)(2,1)S(1)}, u32[]{:S(2)}, u32[]{:S(2)}) collective-permute-start(bf16[8,2880]{1,0:T(8,128)(2,1)S(1)} %get-tuple-element.24), channel_id=1, source_target_pairs={{0,4},{2,6},{4,0},{6,2},{8,12},{10,14},{12,8},{14,10},{1,5},{3,7},... | collective-permute-start | bytes 138248 | tf_op jit(solution)/shard_map/ppermute | solution.py:375
  26.8 5.4 %collective-permute-start.7 = (bf16[8,2880]{1,0:T(8,128)(2,1)S(1)}, bf16[8,2880]{1,0:T(8,128)(2,1)S(1)}, u32[]{:S(2)}, u32[]{:S(2)}) collective-permute-start(bf16[8,2880]{1,0:T(8,128)(2,1)S(1)} %get-tuple-element.25), channel_id=1, source_target_pairs={{0,8},{2,10},{4,12},{6,14},{8,0},{10,2},{12,4},{14,6},{1,9},{3,11}... | collective-permute-start | bytes 138248 | tf_op jit(solution)/shard_map/ppermute | solution.py:375
  28.8 6.0 %collective-permute-start.8 = (bf16[8,2880]{1,0:T(8,128)(2,1)S(1)}, bf16[8,2880]{1,0:T(8,128)(2,1)S(1)}, u32[]{:S(2)}, u32[]{:S(2)}) collective-permute-start(bf16[8,2880]{1,0:T(8,128)(2,1)S(1)} %get-tuple-element.26), channel_id=1, source_target_pairs={{0,12},{2,14},{4,8},{6,10},{8,4},{10,6},{12,0},{14,2},{1,13},{3,15... | collective-permute-start | bytes 138248 | tf_op jit(solution)/shard_map/ppermute | solution.py:375
  34.9 3.9 %collective-permute-start.9 = (bf16[8,1440]{1,0:T(8,128)(2,1)S(1)}, bf16[8,1440]{1,0:T(8,128)(2,1)S(1)}, u32[]{:S(2)}, u32[]{:S(2)}) collective-permute-start(bf16[8,1440]{1,0:T(8,128)(2,1)S(1)} %get-tuple-element.28), channel_id=1, source_target_pairs={{0,1},{1,0},{2,3},{3,2},{4,5},{5,4},{6,7},{7,6},{8,9},{9,8},{10,11... | collective-permute-start | bytes 69128 | tf_op jit(solution)/shard_map/ppermute | solution.py:450

commit v9 on v7

--- a/solution.py
+++ b/solution.py
@@ -47,7 +47,6 @@
 
 VMEM = pl.BlockSpec(memory_space=pltpu.VMEM)
 LAST_DIMS = (((1,), (1,)), ((), ()))
-FIRST_DIMS = (((0,), (0,)), ((), ()))
 MIB = 1 << 20
 
 
@@ -275,6 +274,23 @@
         packed_ref[pl.ds(number * size, size)] = piece_ref[...]
 
 
+def turn_kernel(*refs):
+    for source_ref, target_ref in zip(refs[: len(refs) // 2], refs[len(refs) // 2 :]):
+        for local in range(source_ref.shape[0]):
+            target_ref[local] = source_ref[local].T
+
+
+def turn(*weights):
+    return call(
+        turn_kernel,
+        [(weight.shape, weight.dtype) for weight in weights],
+        [weight.swapaxes(1, 2) for weight in weights],
+        flops=1,
+        moved=1,
+        limit=6 * MIB,
+    )
+
+
 def expert_kernel(experts, *refs):
     *row_refs, gate_ref, up_ref, down_ref, mine_ref, other_ref = refs
     local_experts, _, width = down_ref.shape
@@ -286,14 +302,10 @@
         expert = lax.axis_index("expert") * local_experts + local
         chosen = (column == expert) | (column == expert + experts)
         weight = jnp.sum(jnp.where(chosen, table, 0.0), axis=1, keepdims=True)
-        gate = lax.dot_general(
-            gate_ref[local], rows, LAST_DIMS, preferred_element_type=jnp.float32
-        )
-        up = lax.dot_general(up_ref[local], rows, LAST_DIMS, preferred_element_type=jnp.float32)
+        gate = mm(rows, gate_ref[local])
+        up = mm(rows, up_ref[local])
         active = (gate * jax.nn.sigmoid(GLU_SLOPE * gate) * (up + 1.0)).astype(jnp.bfloat16)
-        part = lax.dot_general(
-            active, down_ref[local], FIRST_DIMS, preferred_element_type=jnp.float32
-        )
+        part = mm(active, down_ref[local])
         part = part * weight
         total = part if total is None else total + part
     half = mine_ref.shape[0]
@@ -391,6 +403,7 @@
     near = [rows]
     for step in range(1, outer):
         near.append(to_outer(rows, step))
+    gate_weight, up_weight = turn(gate_weight, up_weight)
     (near,) = call(
         pack_kernel,
         [((outer * sequences, row_width), jnp.bfloat16)],
@@ -404,7 +417,7 @@
     mine, other = call(
         functools.partial(expert_kernel, experts),
         [(half, jnp.float32), (half, jnp.bfloat16)],
-        (near, far, gate_weight.swapaxes(1, 2), up_weight.swapaxes(1, 2), down_weight),
+        (near, far, gate_weight, up_weight, down_weight),
         flops=12 * half[0] * width * hidden_units * local_experts,
         moved=6 * width * hidden_units * local_experts,
         limit=16 * MIB,

time: 38.6 us -> 38.7 us (level)
  waiting for transfers between devices: 14.8 us -> 13 us
  Pallas kernels: 8.47 us -> 9.94 us
    ppermute x2, waiting for transfers between devices: 2.71 us -> 1.06 us  [to_inner(): lax.ppermute(values, 'expert', [(rank, rank ^ 1) for rank in range(expert...]
    pallas_call x5 -> x6, Pallas kernels: 3.63 us -> 5.1 us  [call(): pl.pallas_call(kernel, out_shape=[jax.ShapeDtypeStruct(shape, dtype) for...]
  transfers between devices with their start and end apart: 10 -> 10, of which waited for: 9 -> 7; matrix products, arithmetic and copies ran while one was open for 1% -> 1% of each run, Pallas kernels for 0% -> 6%
where the time goes in v9:
time: 38.7 us; the launch traced here: 38.6 us
  starting transfers between devices  14.5 us (37%)
  waiting for transfers between devices  13 us (34%)
  Pallas kernels  9.94 us (26%)
  other arithmetic  0.81 us (2%)
    ppermute x6, starting transfers between devices, to_outer(): return lax.ppermute(values, 'expert', pairs)  9.29 us
    ppermute x6, waiting for transfers between devices, to_outer(): return lax.ppermute(values, 'expert', pairs)  7.9 us
    pallas_call x6, Pallas kernels, call(): pl.pallas_call(kernel, out_shape=[jax.ShapeDtypeStruct(shape, dtype) for...  5.1 us
    pallas_call x1, Pallas kernels, attend_and_project(): pl.pallas_call(functools.partial(attend_kernel, pieces), out_shape=[jax.S...  4.84 us
    ppermute x1, starting transfers between devices, exchange(): received = lax.ppermute(sent, axis, pairs)  3.04 us
    ppermute x1, waiting for transfers between devices, per_device(): total = total + lax.ppermute(piece, 'tensor', pairs).astype(jnp.float32)  2.33 us
    ppermute x1, waiting for transfers between devices, exchange(): received = lax.ppermute(sent, axis, pairs)  1.72 us
    ppermute x1, starting transfers between devices, per_device(): total = total + lax.ppermute(piece, 'tensor', pairs).astype(jnp.float32)  1.56 us
  transfers between devices with their start and end apart: 10, of which 7 were waited for; matrix products, arithmetic and copies ran while one was open for 1% of the time, Pallas kernels for 6%

profile of v9, /device:TPU:0, one launch (start us, length us, event | category | flops | bytes accessed | tf_op | source)
XLA Modules:
  0.0 38.6 jit_solution(5325141232299008993)
XLA Ops:
  0.0 0.0 copy-start.4
  0.0 0.0 copy-start.5
  0.0 0.0 copy-start.6
  0.0 0.0 copy-start.3
  0.0 0.0 copy-start.2
  0.0 4.8 %shard_map.145 = (f32[8,2880]{1,0:T(8,128)S(1)}, bf16[8,2880]{1,0:T(8,128)(2,1)S(1)}) custom-call(s32[8]{0:T(128)} %lengths_hbm.1, bf16[8,16,64]{2,1,0:T(8,128)(2,1)} %queries_hbm.1, bf16[8,4,64]{2,1,0:T(4,128)(2,1)} %new_keys_hbm.1, bf16[8,4,64]{2,1,0:T(4,128)(2,1)} %new_values_hbm.1, bf16[8,256,256]{2,1,0:T(8,128)(2,1)} %bitcast.18, ...), custom_call_target="tpu_custom_call" | custom-call | flops 47185920 | bytes 7995392 | tf_op jit(solution)/shard_map/pallas_call | solution.py:212
  4.9 3.0 %collective-permute-start = (bf16[8,2880]{1,0:T(8,128)(2,1)S(1)}, bf16[8,2880]{1,0:T(8,128)(2,1)S(1)}, u32[]{:S(2)}, u32[]{:S(2)}) collective-permute-start(bf16[8,2880]{1,0:T(8,128)(2,1)S(1)} %get-tuple-element.20), channel_id=1, source_target_pairs={{0,1},{1,0},{2,3},{3,2},{4,5},{5,4},{6,7},{7,6},{8,9},{9,8},{10,11... | collective-permute-start | bytes 138248 | tf_op jit(solution)/shard_map/ppermute | solution.py:250
  7.9 0.0 copy-done.4
  7.9 0.0 copy-done.5
  7.9 0.0 copy-done.6
  8.0 0.1 select_reduce_fusion
  8.1 0.1 pad.2.clone
  8.1 0.1 maximum_maximum_fusion.table_ref
  8.2 0.0 copy-done.3
  8.2 1.7 %collective-permute-done.received_ref = bf16[8,2880]{1,0:T(8,128)(2,1)S(1)} collective-permute-done((bf16[8,2880]{1,0:T(8,128)(2,1)S(1)}, bf16[8,2880]{1,0:T(8,128)(2,1)S(1)}, u32[]{:S(2)}, u32[]{:S(2)}) %collective-permute-start) | collective-permute-done | bytes 46112 | tf_op jit(solution)/shard_map/ppermute | solution.py:250
  9.9 0.0 copy-done.2
  10.0 0.0 copy-start
  10.0 0.0 copy-start.1
  10.0 0.1 shard_map.146
  10.1 0.0 slice-start
  10.1 4.2 %collective-permute-start.3 = (bf16[8,2944]{1,0:T(8,128)(2,1)S(1)}, bf16[8,2944]{1,0:T(8,128)(2,1)S(1)}, u32[]{:S(2)}, u32[]{:S(2)}) collective-permute-start(bf16[8,2944]{1,0:T(8,128)(2,1)S(1)} %get-tuple-element.22.refs_0_), channel_id=1, source_target_pairs={{0,12},{2,14},{4,8},{6,10},{8,4},{10,6},{12,0},{14,2},{1,13},{3,15... | collective-permute-start | bytes 141320 | tf_op jit(solution)/shard_map/ppermute | solution.py:374
  14.3 0.0 collective-permute-start.2
  14.3 0.6 %collective-permute-start.1 = (bf16[8,2944]{1,0:T(8,128)(2,1)S(1)}, bf16[8,2944]{1,0:T(8,128)(2,1)S(1)}, u32[]{:S(2)}, u32[]{:S(2)}) collective-permute-start(bf16[8,2944]{1,0:T(8,128)(2,1)S(1)} %get-tuple-element.22.refs_0_), channel_id=1, source_target_pairs={{0,4},{2,6},{4,0},{6,2},{8,12},{10,14},{12,8},{14,10},{1,5},{3,7},... | collective-permute-start | bytes 141320 | tf_op jit(solution)/shard_map/ppermute | solution.py:374
  14.9 1.4 %collective-permute-done.3.refs_3_ = bf16[8,2944]{1,0:T(8,128)(2,1)S(1)} collective-permute-done((bf16[8,2944]{1,0:T(8,128)(2,1)S(1)}, bf16[8,2944]{1,0:T(8,128)(2,1)S(1)}, u32[]{:S(2)}, u32[]{:S(2)}) %collective-permute-start.3) | collective-permute-done | bytes 47136 | tf_op jit(solution)/shard_map/ppermute | solution.py:374
  16.3 2.9 %collective-permute-done.2.refs_2_ = bf16[8,2944]{1,0:T(8,128)(2,1)S(1)} collective-permute-done((bf16[8,2944]{1,0:T(8,128)(2,1)S(1)}, bf16[8,2944]{1,0:T(8,128)(2,1)S(1)}, u32[]{:S(2)}, u32[]{:S(2)}) %collective-permute-start.2) | collective-permute-done | bytes 47136 | tf_op jit(solution)/shard_map/ppermute | solution.py:374
  19.3 0.0 collective-permute-done.1.refs_1_
  19.3 0.1 collective-permute-start.4
  19.4 0.0 copy-done
  19.4 0.0 copy-done.1
  19.4 0.0 slice-start.1
  19.4 2.4 %shard_map.148 = (bf16[1,2880,720]{2,1,0:T(8,128)(2,1)S(1)}, bf16[1,2880,720]{2,1,0:T(8,128)(2,1)S(1)}) custom-call(bf16[1,720,2880]{2,1,0:T(8,128)(2,1)S(1)} %bitcast.13, bf16[1,720,2880]{2,1,0:T(8,128)(2,1)S(1)} %bitcast.14), custom_call_target="tpu_custom_call" | custom-call | flops 1 | bytes 1 | tf_op jit(solution)/shard_map/pallas_call | solution.py:54
  21.8 0.0 collective-permute-done.4.refs_1_
  21.8 0.0 slice-done
  21.8 0.0 slice-done.1
  21.9 2.3 %shard_map.149 = (f32[32,2880]{1,0:T(8,128)S(1)}, bf16[32,2880]{1,0:T(8,128)(2,1)S(1)}) custom-call(bf16[32,2944]{1,0:T(8,128)(2,1)S(1)} %shard_map.147.refs_0_, bf16[32,2944]{1,0:T(8,128)(2,1)S(1)} %collective-permute-done.4.refs_1_, bf16[1,2880,720]{2,1,0:T(8,128)(2,1)S(1)} %get-tuple-element.23.refs_2_, ...), custom_call_target="tpu_custom_call" | custom-call | flops 796262400 | bytes 12441600 | tf_op jit(solution)/shard_map/pallas_call | solution.py:54
  24.2 0.5 %collective-permute-start.5 = (bf16[32,2880]{1,0:T(8,128)(2,1)S(1)}, bf16[32,2880]{1,0:T(8,128)(2,1)S(1)}, u32[]{:S(2)}, u32[]{:S(2)}) collective-permute-start(bf16[32,2880]{1,0:T(8,128)(2,1)S(1)} %get-tuple-element.26), channel_id=1, source_target_pairs={{0,2},{2,0},{4,6},{6,4},{8,10},{10,8},{12,14},{14,12},{1,3},{3,1},... | collective-permute-start | bytes 552968 | tf_op jit(solution)/shard_map/ppermute | solution.py:377
  24.7 1.1 %collective-permute-done.5.received_ref = bf16[32,2880]{1,0:T(8,128)(2,1)S(1)} collective-permute-done((bf16[32,2880]{1,0:T(8,128)(2,1)S(1)}, bf16[32,2880]{1,0:T(8,128)(2,1)S(1)}, u32[]{:S(2)}, u32[]{:S(2)}) %collective-permute-start.5) | collective-permute-done | bytes 184352 | tf_op jit(solution)/shard_map/ppermute | solution.py:377
  25.8 0.2 collective-permute-start.6
  26.0 2.0 %collective-permute-start.7 = (bf16[8,2880]{1,0:T(8,128)(2,1)S(1)}, bf16[8,2880]{1,0:T(8,128)(2,1)S(1)}, u32[]{:S(2)}, u32[]{:S(2)}) collective-permute-start(bf16[8,2880]{1,0:T(8,128)(2,1)S(1)} %get-tuple-element.29), channel_id=1, source_target_pairs={{0,8},{2,10},{4,12},{6,14},{8,0},{10,2},{12,4},{14,6},{1,9},{3,11}... | collective-permute-start | bytes 138248 | tf_op jit(solution)/shard_map/ppermute | solution.py:374
  28.0 2.3 %collective-permute-start.8 = (bf16[8,2880]{1,0:T(8,128)(2,1)S(1)}, bf16[8,2880]{1,0:T(8,128)(2,1)S(1)}, u32[]{:S(2)}, u32[]{:S(2)}) collective-permute-start(bf16[8,2880]{1,0:T(8,128)(2,1)S(1)} %get-tuple-element.30), channel_id=1, source_target_pairs={{0,12},{2,14},{4,8},{6,10},{8,4},{10,6},{12,0},{14,2},{1,13},{3,15... | collective-permute-start | bytes 138248 | tf_op jit(solution)/shard_map/ppermute | solution.py:374
  30.3 0.7 %collective-permute-done.6.refs_1_ = bf16[8,2880]{1,0:T(8,128)(2,1)S(1)} collective-permute-done((bf16[8,2880]{1,0:T(8,128)(2,1)S(1)}, bf16[8,2880]{1,0:T(8,128)(2,1)S(1)}, u32[]{:S(2)}, u32[]{:S(2)}) %collective-permute-start.6) | collective-permute-done | bytes 46112 | tf_op jit(solution)/shard_map/ppermute | solution.py:374
  31.0 0.0 collective-permute-done.7.refs_2_
  31.0 2.9 %collective-permute-done.8.refs_3_ = bf16[8,2880]{1,0:T(8,128)(2,1)S(1)} collective-permute-done((bf16[8,2880]{1,0:T(8,128)(2,1)S(1)}, bf16[8,2880]{1,0:T(8,128)(2,1)S(1)}, u32[]{:S(2)}, u32[]{:S(2)}) %collective-permute-start.8) | collective-permute-done | bytes 46112 | tf_op jit(solution)/shard_map/ppermute | solution.py:374
  33.9 0.2 shard_map.151
  34.0 1.6 %collective-permute-start.9 = (bf16[8,1440]{1,0:T(8,128)(2,1)S(1)}, bf16[8,1440]{1,0:T(8,128)(2,1)S(1)}, u32[]{:S(2)}, u32[]{:S(2)}) collective-permute-start(bf16[8,1440]{1,0:T(8,128)(2,1)S(1)} %get-tuple-element.32), channel_id=1, source_target_pairs={{0,1},{1,0},{2,3},{3,2},{4,5},{5,4},{6,7},{7,6},{8,9},{9,8},{10,11... | collective-permute-start | bytes 69128 | tf_op jit(solution)/shard_map/ppermute | solution.py:448
  35.6 2.3 %collective-permute-done.9 = bf16[8,1440]{1,0:T(8,128)(2,1)S(1)} collective-permute-done((bf16[8,1440]{1,0:T(8,128)(2,1)S(1)}, bf16[8,1440]{1,0:T(8,128)(2,1)S(1)}, u32[]{:S(2)}, u32[]{:S(2)}) %collective-permute-start.9) | collective-permute-done | bytes 23072 | tf_op jit(solution)/shard_map/ppermute | solution.py:448
  37.9 0.6 %add_convert_fusion = bf16[8,1440]{1,0:T(8,128)(2,1)} fusion(f32[8,1440]{1,0:T(8,128)S(1)} %get-tuple-element.31, bf16[8,1440]{1,0:T(8,128)(2,1)S(1)} %collective-permute-done.9), kind=kLoop, calls=%fused_computation | loop fusion | flops 34560 | bytes 92160 | tf_op jit(solution)/shard_map/convert_element_type | solution.py:449
  (9 shorter events, 0.1 us)
Async XLA Ops:
  0.0 7.9 %copy-start.4 = (f32[8,4]{0,1:T(4,128)S(1)}, f32[8,4]{0,1:T(4,128)}, u32[]{:S(2)}) copy-start(f32[8,4]{0,1:T(4,128)} %param.25) | copy-start | bytes 388
  0.0 7.9 %copy-start.5 = (s32[8,4]{0,1:T(4,128)S(1)}, s32[8,4]{0,1:T(4,128)}, u32[]{:S(2)}) copy-start(s32[8,4]{0,1:T(4,128)} %param.26) | copy-start | bytes 388
  0.0 7.9 %copy-start.6 = (s32[8,4]{0,1:T(4,128)S(1)}, s32[8,4]{0,1:T(4,128)}, u32[]{:S(2)}) copy-start(s32[8,4]{0,1:T(4,128)} %param.24) | copy-start | bytes 388
  0.0 8.2 %copy-start.3 = (f32[2880]{0:T(1024)S(1)}, f32[2880]{0:T(1024)}, u32[]{:S(2)}) copy-start(f32[2880]{0:T(1024)} %param.23) | copy-start | bytes 34564
  0.0 9.9 %copy-start.2 = (bf16[8,2880]{1,0:T(8,128)(2,1)S(1)}, bf16[8,2880]{1,0:T(8,128)(2,1)}, u32[]{:S(2)}) copy-start(bf16[8,2880]{1,0:T(8,128)(2,1)} %hidden_ref.1) | copy-start | bytes 138244
  4.9 5.1 %collective-permute-start = (bf16[8,2880]{1,0:T(8,128)(2,1)S(1)}, bf16[8,2880]{1,0:T(8,128)(2,1)S(1)}, u32[]{:S(2)}, u32[]{:S(2)}) collective-permute-start(bf16[8,2880]{1,0:T(8,128)(2,1)S(1)} %get-tuple-element.20), channel_id=1, source_target_pairs={{0,1},{1,0},{2,3},{3,2},{4,5},{5,4},{6,7},{7,6},{8,9},{9,8},{10,11... | collective-permute-start | bytes 138248 | tf_op jit(solution)/shard_map/ppermute | solution.py:250
  10.0 9.4 %copy-start = (bf16[1,2880,720]{1,2,0:T(8,128)(2,1)S(1)}, bf16[1,2880,720]{1,2,0:T(8,128)(2,1)}, u32[]{:S(2)}) copy-start(bf16[1,2880,720]{1,2,0:T(8,128)(2,1)} %param.27) | copy-start | bytes 12441604
  10.0 9.4 %copy-start.1 = (bf16[1,2880,720]{1,2,0:T(8,128)(2,1)S(1)}, bf16[1,2880,720]{1,2,0:T(8,128)(2,1)}, u32[]{:S(2)}) copy-start(bf16[1,2880,720]{1,2,0:T(8,128)(2,1)} %param.28) | copy-start | bytes 12441604
  10.1 11.7 %slice-start = ((s8[4239360]{0:T(1024)(128)(4,1)}), s8[4194304]{0:T(1024)(128)(4,1)S(1)}, s32[]{:S(2)}) async-start(s8[4239360]{0:T(1024)(128)(4,1)} %bitcast.15), calls=%async_computation | async-start | bytes 8388608
  10.1 6.2 %collective-permute-start.3 = (bf16[8,2944]{1,0:T(8,128)(2,1)S(1)}, bf16[8,2944]{1,0:T(8,128)(2,1)S(1)}, u32[]{:S(2)}, u32[]{:S(2)}) collective-permute-start(bf16[8,2944]{1,0:T(8,128)(2,1)S(1)} %get-tuple-element.22.refs_0_), channel_id=1, source_target_pairs={{0,12},{2,14},{4,8},{6,10},{8,4},{10,6},{12,0},{14,2},{1,13},{3,15... | collective-permute-start | bytes 141320 | tf_op jit(solution)/shard_map/ppermute | solution.py:374
  14.3 5.0 %collective-permute-start.2 = (bf16[8,2944]{1,0:T(8,128)(2,1)S(1)}, bf16[8,2944]{1,0:T(8,128)(2,1)S(1)}, u32[]{:S(2)}, u32[]{:S(2)}) collective-permute-start(bf16[8,2944]{1,0:T(8,128)(2,1)S(1)} %get-tuple-element.22.refs_0_), channel_id=1, source_target_pairs={{0,8},{2,10},{4,12},{6,14},{8,0},{10,2},{12,4},{14,6},{1,9},{3,11}... | collective-permute-start | bytes 141320 | tf_op jit(solution)/shard_map/ppermute | solution.py:374
  14.3 5.0 %collective-permute-start.1 = (bf16[8,2944]{1,0:T(8,128)(2,1)S(1)}, bf16[8,2944]{1,0:T(8,128)(2,1)S(1)}, u32[]{:S(2)}, u32[]{:S(2)}) collective-permute-start(bf16[8,2944]{1,0:T(8,128)(2,1)S(1)} %get-tuple-element.22.refs_0_), channel_id=1, source_target_pairs={{0,4},{2,6},{4,0},{6,2},{8,12},{10,14},{12,8},{14,10},{1,5},{3,7},... | collective-permute-start | bytes 141320 | tf_op jit(solution)/shard_map/ppermute | solution.py:374
  19.3 2.5 %collective-permute-start.4 = (bf16[32,2944]{1,0:T(8,128)(2,1)S(1)}, bf16[32,2944]{1,0:T(8,128)(2,1)S(1)}, u32[]{:S(2)}, u32[]{:S(2)}) collective-permute-start(bf16[32,2944]{1,0:T(8,128)(2,1)S(1)} %shard_map.147.refs_0_), channel_id=1, source_target_pairs={{0,2},{2,0},{4,6},{6,4},{8,10},{10,8},{12,14},{14,12},{1,3},{3,1},... | collective-permute-start | bytes 565256 | tf_op jit(solution)/shard_map/ppermute | solution.py:377
  19.4 2.5 %slice-start.1 = ((s8[4239360]{0:T(1024)(128)(4,1)}), s8[45056]{0:T(1024)(128)(4,1)S(1)}, s32[]{:S(2)}) async-start(s8[4239360]{0:T(1024)(128)(4,1)} %bitcast.15), calls=%async_computation.1 | async-start | bytes 90112
  24.2 1.6 %collective-permute-start.5 = (bf16[32,2880]{1,0:T(8,128)(2,1)S(1)}, bf16[32,2880]{1,0:T(8,128)(2,1)S(1)}, u32[]{:S(2)}, u32[]{:S(2)}) collective-permute-start(bf16[32,2880]{1,0:T(8,128)(2,1)S(1)} %get-tuple-element.26), channel_id=1, source_target_pairs={{0,2},{2,0},{4,6},{6,4},{8,10},{10,8},{12,14},{14,12},{1,3},{3,1},... | collective-permute-start | bytes 552968 | tf_op jit(solution)/shard_map/ppermute | solution.py:377
  25.8 5.1 %collective-permute-start.6 = (bf16[8,2880]{1,0:T(8,128)(2,1)S(1)}, bf16[8,2880]{1,0:T(8,128)(2,1)S(1)}, u32[]{:S(2)}, u32[]{:S(2)}) collective-permute-start(bf16[8,2880]{1,0:T(8,128)(2,1)S(1)} %get-tuple-element.28), channel_id=1, source_target_pairs={{0,4},{2,6},{4,0},{6,2},{8,12},{10,14},{12,8},{14,10},{1,5},{3,7},... | collective-permute-start | bytes 138248 | tf_op jit(solution)/shard_map/ppermute | solution.py:374
  26.0 5.0 %collective-permute-start.7 = (bf16[8,2880]{1,0:T(8,128)(2,1)S(1)}, bf16[8,2880]{1,0:T(8,128)(2,1)S(1)}, u32[]{:S(2)}, u32[]{:S(2)}) collective-permute-start(bf16[8,2880]{1,0:T(8,128)(2,1)S(1)} %get-tuple-element.29), channel_id=1, source_target_pairs={{0,8},{2,10},{4,12},{6,14},{8,0},{10,2},{12,4},{14,6},{1,9},{3,11}... | collective-permute-start | bytes 138248 | tf_op jit(solution)/shard_map/ppermute | solution.py:374
  28.0 5.9 %collective-permute-start.8 = (bf16[8,2880]{1,0:T(8,128)(2,1)S(1)}, bf16[8,2880]{1,0:T(8,128)(2,1)S(1)}, u32[]{:S(2)}, u32[]{:S(2)}) collective-permute-start(bf16[8,2880]{1,0:T(8,128)(2,1)S(1)} %get-tuple-element.30), channel_id=1, source_target_pairs={{0,12},{2,14},{4,8},{6,10},{8,4},{10,6},{12,0},{14,2},{1,13},{3,15... | collective-permute-start | bytes 138248 | tf_op jit(solution)/shard_map/ppermute | solution.py:374
  34.0 3.9 %collective-permute-start.9 = (bf16[8,1440]{1,0:T(8,128)(2,1)S(1)}, bf16[8,1440]{1,0:T(8,128)(2,1)S(1)}, u32[]{:S(2)}, u32[]{:S(2)}) collective-permute-start(bf16[8,1440]{1,0:T(8,128)(2,1)S(1)} %get-tuple-element.32), channel_id=1, source_target_pairs={{0,1},{1,0},{2,3},{3,2},{4,5},{5,4},{6,7},{7,6},{8,9},{9,8},{10,11... | collective-permute-start | bytes 69128 | tf_op jit(solution)/shard_map/ppermute | solution.py:448
